TPU v7x, 256 devices: a whole 4x4x8 slice. The times are simulated.
256 devices in a mesh: ang: 32 (over y, z_lo, core), sl: 8 (over z_hi, x).
Axes of the slice: x: 4, y: 4, z: 8 (z_hi: 2, z_lo: 4; z = z_hi * 4 + z_lo), core: 2. Of those that a mesh axis runs over, the one named last changes fastest.
Arguments:
- sinogram: bfloat16 [64, 64, 1024], P('sl', 'ang'), may hold values from -72 to 72
- detector_coord: int32 [64, 64, 512], P('ang', 'sl'), may hold values from 0 to 1072693247
Outputs:
- image_rows: float32 [64, 64, 512], P('ang', 'sl')
All inputs are finite; a program needn't handle non-finite values.
Results may differ from a plain program's by a relative error of at most 0.0052.
Values may be sent and summed in bfloat16 or wider, within the bound.
No kernel may reach another device: no remote copies, remote signals or barrier semaphores. Data moves between devices by JAX's collectives and lax.ppermute only.
A program may use at most 64 MiB of HBM per device.

v0:
```python
import math

import jax
import jax.numpy as jnp
from jax import lax
from jax.sharding import PartitionSpec as P


def sent_to_all(array, axis):
    devices = lax.axis_size(axis)
    return lax.all_to_all(
        jnp.broadcast_to(array[None], (devices, *array.shape)), axis, 0, 0, tiled=True
    )


def in_order(tiles, dim):
    tiles = jnp.moveaxis(tiles, 0, dim)
    shape = tiles.shape
    return tiles.reshape(*shape[:dim], shape[dim] * shape[dim + 1], *shape[dim + 2 :])


def gathered_copies(array, axis, dim):
    tiles = sent_to_all(array, axis)
    return in_order(tiles, dim)


def ramp_table(bin_count):
    first = lax.broadcasted_iota(jnp.int32, (bin_count, bin_count), 0)
    second = lax.broadcasted_iota(jnp.int32, (bin_count, bin_count), 1)
    offset = second - first
    offset_sq = jnp.maximum((offset * offset).astype(jnp.float32), jnp.float32(1.0))
    odd_mask = offset % 2 != 0
    values = jnp.where(
        offset == 0,
        jnp.float32(0.25),
        jnp.where(odd_mask, jnp.float32(-1.0 / math.pi**2) / offset_sq, jnp.float32(0.0)),
    )
    return values.astype(jnp.bfloat16)


def dense_weights(row_coords, bin_count):
    bin_left = row_coords // 1048576
    fraction = (row_coords % 1048576).astype(jnp.float32) / jnp.float32(1048576.0)
    positions = lax.broadcasted_iota(jnp.int32, row_coords.shape + (bin_count,), row_coords.ndim)
    left_part = jnp.where(
        positions == bin_left[..., None], 1.0 - fraction[..., None], jnp.float32(0.0)
    )
    right_part = jnp.where(
        positions == bin_left[..., None] + 1, fraction[..., None], jnp.float32(0.0)
    )
    return (left_part + right_part).astype(jnp.bfloat16)


def project_block(coords_block, projections):
    weights = dense_weights(coords_block, projections.shape[2])
    return jnp.einsum("arxb,sab->rsx", weights, projections, preferred_element_type=jnp.float32)


def shards(sinogram, detector_coord):
    slices, angles, bin_count = sinogram.shape
    width_pixels = detector_coord.shape[2]
    table = ramp_table(bin_count)
    filtered = jnp.dot(
        sinogram.reshape(slices * angles, bin_count), table, preferred_element_type=jnp.float32
    )
    filtered = filtered.astype(jnp.bfloat16).reshape(slices, angles, bin_count)
    fbp_scale = jnp.float32(math.pi / (angles * lax.axis_size("ang")))
    coord_table = gathered_copies(detector_coord, "sl", 1)
    row_share = coord_table.shape[1] // lax.axis_size("ang")
    own_rows = lax.all_to_all(coord_table, "ang", split_axis=1, concat_axis=0, tiled=True)
    start_value = jnp.zeros((row_share, slices, width_pixels), jnp.float32)
    shard_piece = gathered_copies(filtered, "ang", 1)
    group_count = shard_piece.shape[1] // angles

    def one_group(group_step, inner):
        coords_block = lax.dynamic_slice_in_dim(own_rows, group_step * angles, angles, 0)
        projections = lax.dynamic_slice_in_dim(shard_piece, group_step * angles, angles, 1)
        return inner + project_block(coords_block, projections)

    summed = lax.fori_loop(0, group_count, one_group, start_value)
    image_rows = summed * fbp_scale
    return image_rows


def solution(mesh):
    in_specs = (P("sl", "ang", None), P("ang", "sl", None))
    out_specs = P("ang", "sl", None)
    return jax.shard_map(shards, mesh=mesh, in_specs=in_specs, out_specs=out_specs, check_vma=False)
```

profile of v0, /device:TPU:2, one launch (start us, length us, event | category | flops | bytes accessed | tf_op | source)
XLA Modules:
  0.0 151.0 jit_solution(7158897896248793487)
XLA Ops:
  1.5 11.5 %all-to-all-start.1 = ((s32[8,2,8,512]{3,2,1,0:T(8,128)}), s32[8,2,8,512]{3,2,1,0:T(8,128)S(1)}, u32[]{:S(2)}, u32[]{:S(2)}) async-start(s32[8,2,8,512]{3,2,1,0:T(8,128)} %broadcast_in_dim.84), calls=%async_computation.1 | async-start | bytes 524288 | tf_op jit(solution)/shard_map/all_to_all | solution.py:11
  13.7 8.6 %all-to-all-done.1 = s32[8,2,8,512]{3,2,1,0:T(8,128)S(1)} async-done(((s32[8,2,8,512]{3,2,1,0:T(8,128)}), s32[8,2,8,512]{3,2,1,0:T(8,128)S(1)}, u32[]{:S(2)}, u32[]{:S(2)}) %all-to-all-start.1) | async-done | bytes 262176 | tf_op jit(solution)/shard_map/all_to_all | solution.py:11
  23.3 8.5 %all-to-all-start.2 = ((s32[2,64,512]{2,0,1:T(2,128)}), s32[2,64,512]{2,0,1:T(2,128)S(1)}, u32[]{:S(2)}, u32[]{:S(2)}) async-start(s32[2,64,512]{2,0,1:T(2,128)} %copy.12), calls=%async_computation.2 | async-start | bytes 524288 | tf_op jit(solution)/shard_map/all_to_all | solution.py:70
  31.8 3.2 %fusion.17 = bf16[16,1024]{1,0:T(8,128)(2,1)S(1)} fusion(bf16[16,1024]{1,0:T(8,128)(2,1)S(1)} %reshape.17), kind=kOutput, calls=%fused_computation.35 | convolution fusion | flops 55590912 | bytes 65536 | tf_op jit(solution)/shard_map/dot_general | solution.py:63
  35.0 7.4 %all-to-all-done.2 = s32[2,64,512]{2,0,1:T(2,128)S(1)} async-done(((s32[2,64,512]{2,0,1:T(2,128)}), s32[2,64,512]{2,0,1:T(2,128)S(1)}, u32[]{:S(2)}, u32[]{:S(2)}) %all-to-all-start.2) | async-done | bytes 262176 | tf_op jit(solution)/shard_map/all_to_all | solution.py:70
  43.5 4.2 %all-to-all-start = ((bf16[32,8,2,1024]{3,1,2,0:T(8,128)(2,1)}), bf16[32,8,2,1024]{3,1,2,0:T(8,128)(2,1)S(1)}, u32[]{:S(2)}, u32[]{:S(2)}) async-start(bf16[32,8,2,1024]{3,1,2,0:T(8,128)(2,1)} %broadcast_in_dim.83), calls=%async_computation | async-start | bytes 2097152 | tf_op jit(solution)/shard_map/all_to_all | solution.py:11
  47.8 27.7 %all-to-all-done = bf16[32,8,2,1024]{3,1,2,0:T(8,128)(2,1)S(1)} async-done(((bf16[32,8,2,1024]{3,1,2,0:T(8,128)(2,1)}), bf16[32,8,2,1024]{3,1,2,0:T(8,128)(2,1)S(1)}, u32[]{:S(2)}, u32[]{:S(2)}) %all-to-all-start) | async-done | bytes 1048608 | tf_op jit(solution)/shard_map/all_to_all | solution.py:11
  75.5 74.9 %while.16 = (s32[]{:T(128)}, f32[2,8,512]{2,1,0:T(8,128)S(1)}, bf16[8,64,1024]{2,0,1:T(8,128)(2,1)S(1)}, s32[64,2,512]{2,1,0:T(2,128)S(1)}, s32[]{:T(128)}, /*index=5*/s32[]{:T(128)}, s32[]{:T(128)}, s32[]{:T(128)}) while((s32[]{:T(128)}, f32[2,8,512]{2,1,0:T(8,128)S(1)}, bf16[8,64,1024]{2,0,1:T(8,128)(2,1)S(1)}, ...), condition=%wide.region_1.2_spmd.clone, body=%wide.region_0.1_spmd.clone.sunk | while | flops 46215176 | bytes 196757 | solution.py:80
  75.6 2.3 %fusion.30 = f32[2,8,512]{2,1,0:T(8,128)S(1)} fusion(f32[2,2,512]{2,0,1:T(2,128)S(1)} %get-tuple-element.183, s32[2,2,512]{2,0,1:T(2,128)S(1)} %get-tuple-element.184, f32[2,2,512]{2,0,1:T(2,128)S(1)} %get-tuple-element.185, s32[2,2,512]{2,0,1:T(2,128)S(1)} %get-tuple-element.186, f32[2,8,512]{2,1,0:T(8,128)S(1)} %get-tuple-element.196, ...), kind=kOutput, calls=%fused_computation.5.clone.1 | convolution fusion | flops 46153728 | bytes 131077 | tf_op jit(solution)/shard_map/while/body/eval_jaxpr/arxb,sab->rsx/dot_general | solution.py:56
  77.9 2.3 %fusion.30 = f32[2,8,512]{2,1,0:T(8,128)S(1)} fusion(f32[2,2,512]{2,0,1:T(2,128)S(1)} %get-tuple-element.183, s32[2,2,512]{2,0,1:T(2,128)S(1)} %get-tuple-element.184, f32[2,2,512]{2,0,1:T(2,128)S(1)} %get-tuple-element.185, s32[2,2,512]{2,0,1:T(2,128)S(1)} %get-tuple-element.186, f32[2,8,512]{2,1,0:T(8,128)S(1)} %get-tuple-element.196, ...), kind=kOutput, calls=%fused_computation.5.clone.1 | convolution fusion | flops 46153728 | bytes 131077 | tf_op jit(solution)/shard_map/while/body/eval_jaxpr/arxb,sab->rsx/dot_general | solution.py:56
  80.3 2.3 %fusion.30 = f32[2,8,512]{2,1,0:T(8,128)S(1)} fusion(f32[2,2,512]{2,0,1:T(2,128)S(1)} %get-tuple-element.183, s32[2,2,512]{2,0,1:T(2,128)S(1)} %get-tuple-element.184, f32[2,2,512]{2,0,1:T(2,128)S(1)} %get-tuple-element.185, s32[2,2,512]{2,0,1:T(2,128)S(1)} %get-tuple-element.186, f32[2,8,512]{2,1,0:T(8,128)S(1)} %get-tuple-element.196, ...), kind=kOutput, calls=%fused_computation.5.clone.1 | convolution fusion | flops 46153728 | bytes 131077 | tf_op jit(solution)/shard_map/while/body/eval_jaxpr/arxb,sab->rsx/dot_general | solution.py:56
  82.6 2.3 %fusion.30 = f32[2,8,512]{2,1,0:T(8,128)S(1)} fusion(f32[2,2,512]{2,0,1:T(2,128)S(1)} %get-tuple-element.183, s32[2,2,512]{2,0,1:T(2,128)S(1)} %get-tuple-element.184, f32[2,2,512]{2,0,1:T(2,128)S(1)} %get-tuple-element.185, s32[2,2,512]{2,0,1:T(2,128)S(1)} %get-tuple-element.186, f32[2,8,512]{2,1,0:T(8,128)S(1)} %get-tuple-element.196, ...), kind=kOutput, calls=%fused_computation.5.clone.1 | convolution fusion | flops 46153728 | bytes 131077 | tf_op jit(solution)/shard_map/while/body/eval_jaxpr/arxb,sab->rsx/dot_general | solution.py:56
  85.0 2.3 %fusion.30 = f32[2,8,512]{2,1,0:T(8,128)S(1)} fusion(f32[2,2,512]{2,0,1:T(2,128)S(1)} %get-tuple-element.183, s32[2,2,512]{2,0,1:T(2,128)S(1)} %get-tuple-element.184, f32[2,2,512]{2,0,1:T(2,128)S(1)} %get-tuple-element.185, s32[2,2,512]{2,0,1:T(2,128)S(1)} %get-tuple-element.186, f32[2,8,512]{2,1,0:T(8,128)S(1)} %get-tuple-element.196, ...), kind=kOutput, calls=%fused_computation.5.clone.1 | convolution fusion | flops 46153728 | bytes 131077 | tf_op jit(solution)/shard_map/while/body/eval_jaxpr/arxb,sab->rsx/dot_general | solution.py:56
  87.3 2.3 %fusion.30 = f32[2,8,512]{2,1,0:T(8,128)S(1)} fusion(f32[2,2,512]{2,0,1:T(2,128)S(1)} %get-tuple-element.183, s32[2,2,512]{2,0,1:T(2,128)S(1)} %get-tuple-element.184, f32[2,2,512]{2,0,1:T(2,128)S(1)} %get-tuple-element.185, s32[2,2,512]{2,0,1:T(2,128)S(1)} %get-tuple-element.186, f32[2,8,512]{2,1,0:T(8,128)S(1)} %get-tuple-element.196, ...), kind=kOutput, calls=%fused_computation.5.clone.1 | convolution fusion | flops 46153728 | bytes 131077 | tf_op jit(solution)/shard_map/while/body/eval_jaxpr/arxb,sab->rsx/dot_general | solution.py:56
  89.6 2.3 %fusion.30 = f32[2,8,512]{2,1,0:T(8,128)S(1)} fusion(f32[2,2,512]{2,0,1:T(2,128)S(1)} %get-tuple-element.183, s32[2,2,512]{2,0,1:T(2,128)S(1)} %get-tuple-element.184, f32[2,2,512]{2,0,1:T(2,128)S(1)} %get-tuple-element.185, s32[2,2,512]{2,0,1:T(2,128)S(1)} %get-tuple-element.186, f32[2,8,512]{2,1,0:T(8,128)S(1)} %get-tuple-element.196, ...), kind=kOutput, calls=%fused_computation.5.clone.1 | convolution fusion | flops 46153728 | bytes 131077 | tf_op jit(solution)/shard_map/while/body/eval_jaxpr/arxb,sab->rsx/dot_general | solution.py:56
  92.0 2.3 %fusion.30 = f32[2,8,512]{2,1,0:T(8,128)S(1)} fusion(f32[2,2,512]{2,0,1:T(2,128)S(1)} %get-tuple-element.183, s32[2,2,512]{2,0,1:T(2,128)S(1)} %get-tuple-element.184, f32[2,2,512]{2,0,1:T(2,128)S(1)} %get-tuple-element.185, s32[2,2,512]{2,0,1:T(2,128)S(1)} %get-tuple-element.186, f32[2,8,512]{2,1,0:T(8,128)S(1)} %get-tuple-element.196, ...), kind=kOutput, calls=%fused_computation.5.clone.1 | convolution fusion | flops 46153728 | bytes 131077 | tf_op jit(solution)/shard_map/while/body/eval_jaxpr/arxb,sab->rsx/dot_general | solution.py:56
  94.3 2.3 %fusion.30 = f32[2,8,512]{2,1,0:T(8,128)S(1)} fusion(f32[2,2,512]{2,0,1:T(2,128)S(1)} %get-tuple-element.183, s32[2,2,512]{2,0,1:T(2,128)S(1)} %get-tuple-element.184, f32[2,2,512]{2,0,1:T(2,128)S(1)} %get-tuple-element.185, s32[2,2,512]{2,0,1:T(2,128)S(1)} %get-tuple-element.186, f32[2,8,512]{2,1,0:T(8,128)S(1)} %get-tuple-element.196, ...), kind=kOutput, calls=%fused_computation.5.clone.1 | convolution fusion | flops 46153728 | bytes 131077 | tf_op jit(solution)/shard_map/while/body/eval_jaxpr/arxb,sab->rsx/dot_general | solution.py:56
  96.7 2.3 %fusion.30 = f32[2,8,512]{2,1,0:T(8,128)S(1)} fusion(f32[2,2,512]{2,0,1:T(2,128)S(1)} %get-tuple-element.183, s32[2,2,512]{2,0,1:T(2,128)S(1)} %get-tuple-element.184, f32[2,2,512]{2,0,1:T(2,128)S(1)} %get-tuple-element.185, s32[2,2,512]{2,0,1:T(2,128)S(1)} %get-tuple-element.186, f32[2,8,512]{2,1,0:T(8,128)S(1)} %get-tuple-element.196, ...), kind=kOutput, calls=%fused_computation.5.clone.1 | convolution fusion | flops 46153728 | bytes 131077 | tf_op jit(solution)/shard_map/while/body/eval_jaxpr/arxb,sab->rsx/dot_general | solution.py:56
  99.0 2.3 %fusion.30 = f32[2,8,512]{2,1,0:T(8,128)S(1)} fusion(f32[2,2,512]{2,0,1:T(2,128)S(1)} %get-tuple-element.183, s32[2,2,512]{2,0,1:T(2,128)S(1)} %get-tuple-element.184, f32[2,2,512]{2,0,1:T(2,128)S(1)} %get-tuple-element.185, s32[2,2,512]{2,0,1:T(2,128)S(1)} %get-tuple-element.186, f32[2,8,512]{2,1,0:T(8,128)S(1)} %get-tuple-element.196, ...), kind=kOutput, calls=%fused_computation.5.clone.1 | convolution fusion | flops 46153728 | bytes 131077 | tf_op jit(solution)/shard_map/while/body/eval_jaxpr/arxb,sab->rsx/dot_general | solution.py:56
  101.3 2.3 %fusion.30 = f32[2,8,512]{2,1,0:T(8,128)S(1)} fusion(f32[2,2,512]{2,0,1:T(2,128)S(1)} %get-tuple-element.183, s32[2,2,512]{2,0,1:T(2,128)S(1)} %get-tuple-element.184, f32[2,2,512]{2,0,1:T(2,128)S(1)} %get-tuple-element.185, s32[2,2,512]{2,0,1:T(2,128)S(1)} %get-tuple-element.186, f32[2,8,512]{2,1,0:T(8,128)S(1)} %get-tuple-element.196, ...), kind=kOutput, calls=%fused_computation.5.clone.1 | convolution fusion | flops 46153728 | bytes 131077 | tf_op jit(solution)/shard_map/while/body/eval_jaxpr/arxb,sab->rsx/dot_general | solution.py:56
  103.7 2.3 %fusion.30 = f32[2,8,512]{2,1,0:T(8,128)S(1)} fusion(f32[2,2,512]{2,0,1:T(2,128)S(1)} %get-tuple-element.183, s32[2,2,512]{2,0,1:T(2,128)S(1)} %get-tuple-element.184, f32[2,2,512]{2,0,1:T(2,128)S(1)} %get-tuple-element.185, s32[2,2,512]{2,0,1:T(2,128)S(1)} %get-tuple-element.186, f32[2,8,512]{2,1,0:T(8,128)S(1)} %get-tuple-element.196, ...), kind=kOutput, calls=%fused_computation.5.clone.1 | convolution fusion | flops 46153728 | bytes 131077 | tf_op jit(solution)/shard_map/while/body/eval_jaxpr/arxb,sab->rsx/dot_general | solution.py:56
  106.0 2.3 %fusion.30 = f32[2,8,512]{2,1,0:T(8,128)S(1)} fusion(f32[2,2,512]{2,0,1:T(2,128)S(1)} %get-tuple-element.183, s32[2,2,512]{2,0,1:T(2,128)S(1)} %get-tuple-element.184, f32[2,2,512]{2,0,1:T(2,128)S(1)} %get-tuple-element.185, s32[2,2,512]{2,0,1:T(2,128)S(1)} %get-tuple-element.186, f32[2,8,512]{2,1,0:T(8,128)S(1)} %get-tuple-element.196, ...), kind=kOutput, calls=%fused_computation.5.clone.1 | convolution fusion | flops 46153728 | bytes 131077 | tf_op jit(solution)/shard_map/while/body/eval_jaxpr/arxb,sab->rsx/dot_general | solution.py:56
  108.4 2.3 %fusion.30 = f32[2,8,512]{2,1,0:T(8,128)S(1)} fusion(f32[2,2,512]{2,0,1:T(2,128)S(1)} %get-tuple-element.183, s32[2,2,512]{2,0,1:T(2,128)S(1)} %get-tuple-element.184, f32[2,2,512]{2,0,1:T(2,128)S(1)} %get-tuple-element.185, s32[2,2,512]{2,0,1:T(2,128)S(1)} %get-tuple-element.186, f32[2,8,512]{2,1,0:T(8,128)S(1)} %get-tuple-element.196, ...), kind=kOutput, calls=%fused_computation.5.clone.1 | convolution fusion | flops 46153728 | bytes 131077 | tf_op jit(solution)/shard_map/while/body/eval_jaxpr/arxb,sab->rsx/dot_general | solution.py:56
  110.7 2.3 %fusion.30 = f32[2,8,512]{2,1,0:T(8,128)S(1)} fusion(f32[2,2,512]{2,0,1:T(2,128)S(1)} %get-tuple-element.183, s32[2,2,512]{2,0,1:T(2,128)S(1)} %get-tuple-element.184, f32[2,2,512]{2,0,1:T(2,128)S(1)} %get-tuple-element.185, s32[2,2,512]{2,0,1:T(2,128)S(1)} %get-tuple-element.186, f32[2,8,512]{2,1,0:T(8,128)S(1)} %get-tuple-element.196, ...), kind=kOutput, calls=%fused_computation.5.clone.1 | convolution fusion | flops 46153728 | bytes 131077 | tf_op jit(solution)/shard_map/while/body/eval_jaxpr/arxb,sab->rsx/dot_general | solution.py:56
  (122 shorter events, 43.1 us)
Async XLA Ops:
  1.5 20.9 %all-to-all-start.1 = ((s32[8,2,8,512]{3,2,1,0:T(8,128)}), s32[8,2,8,512]{3,2,1,0:T(8,128)S(1)}, u32[]{:S(2)}, u32[]{:S(2)}) async-start(s32[8,2,8,512]{3,2,1,0:T(8,128)} %broadcast_in_dim.84), calls=%async_computation.1 | async-start | bytes 524288 | tf_op jit(solution)/shard_map/all_to_all | solution.py:11
  23.3 19.1 %all-to-all-start.2 = ((s32[2,64,512]{2,0,1:T(2,128)}), s32[2,64,512]{2,0,1:T(2,128)S(1)}, u32[]{:S(2)}, u32[]{:S(2)}) async-start(s32[2,64,512]{2,0,1:T(2,128)} %copy.12), calls=%async_computation.2 | async-start | bytes 524288 | tf_op jit(solution)/shard_map/all_to_all | solution.py:70
  43.5 32.1 %all-to-all-start = ((bf16[32,8,2,1024]{3,1,2,0:T(8,128)(2,1)}), bf16[32,8,2,1024]{3,1,2,0:T(8,128)(2,1)S(1)}, u32[]{:S(2)}, u32[]{:S(2)}) async-start(bf16[32,8,2,1024]{3,1,2,0:T(8,128)(2,1)} %broadcast_in_dim.83), calls=%async_computation | async-start | bytes 2097152 | tf_op jit(solution)/shard_map/all_to_all | solution.py:11
where the time goes:
time: 154 us; the launch traced here: 151 us
  matrix products  75.6 us (49%)
  waiting for transfers between devices  43.7 us (28%)
  starting transfers between devices  24.1 us (16%)
  local copies, waits for them, and re-layouts  4.48 us (3%)
  other arithmetic  2.41 us (2%)
    dot_general x32, matrix products, project_block(): jnp.einsum('arxb,sab->rsx', weights, projections, preferred_element_type=...  72.4 us
    all_to_all x2, waiting for transfers between devices, sent_to_all(): lax.all_to_all(jnp.broadcast_to(array[None], (devices, *array.shape)), ax...  36.3 us
    all_to_all x2, starting transfers between devices, sent_to_all(): lax.all_to_all(jnp.broadcast_to(array[None], (devices, *array.shape)), ax...  15.7 us
    all_to_all x1, starting transfers between devices, shards(): lax.all_to_all(coord_table, 'ang', split_axis=1, concat_axis=0, tiled=True)  8.48 us
    all_to_all x1, waiting for transfers between devices, shards(): lax.all_to_all(coord_table, 'ang', split_axis=1, concat_axis=0, tiled=True)  7.39 us
    dot_general x1, matrix products, shards(): jnp.dot(sinogram.reshape(slices * angles, bin_count), table, preferred_el...  3.19 us
  transfers between devices with their start and end apart: 3, of which 3 were waited for; matrix products, arithmetic and copies ran while one was open for 3% of the time, Pallas kernels for 0%

commit v1 on v0

v1 whole, which is shorter than its diff:
```python
import math

import jax
import jax.numpy as jnp
from jax import lax
from jax.experimental import pallas as pl
from jax.experimental.pallas import tpu as pltpu
from jax.sharding import Mesh
from jax.sharding import PartitionSpec as P

SLICE_ORDER = (0, 2, 4, 6, 1, 3, 5, 7)
LANES = 128
LANE_DIMS = lax.GatherDimensionNumbers(
    offset_dims=(),
    collapsed_slice_dims=(1,),
    start_index_map=(1,),
    operand_batching_dims=(0,),
    start_indices_batching_dims=(0,),
)


def ramp_table(bin_count):
    first = lax.broadcasted_iota(jnp.int32, (bin_count, bin_count), 0)
    second = lax.broadcasted_iota(jnp.int32, (bin_count, bin_count), 1)
    offset = second - first
    offset_sq = jnp.maximum((offset * offset).astype(jnp.float32), jnp.float32(1.0))
    odd_mask = offset % 2 != 0
    values = jnp.where(
        offset == 0,
        jnp.float32(0.25),
        jnp.where(odd_mask, jnp.float32(-1.0 / math.pi**2) / offset_sq, jnp.float32(0.0)),
    )
    return values.astype(jnp.bfloat16)


def lane_gather(table, lanes):
    return lax.gather(
        table, lanes[..., None], LANE_DIMS, (1, 1), mode=lax.GatherScatterMode.PROMISE_IN_BOUNDS
    )


def project_kernel(place, tab, *refs):
    coords, (out, tab_s, left_s, w1_s, w2_s) = refs[:8], refs[8:]
    tab_s[...] = tab[...]
    even = lax.broadcasted_iota(jnp.int32, (8, LANES), 0) % 2 == 0
    for n in range(8):
        for core in range(2):
            c = coords[n][core]
            fraction = (c & 1048575).astype(jnp.float32) * jnp.float32(1.0 / 1048576.0)
            left_s[n, core] = c >> 20
            w1_s[n, core] = (1.0 - fraction).astype(jnp.bfloat16).astype(jnp.float32)
            w2_s[n, core] = fraction.astype(jnp.bfloat16).astype(jnp.float32)

    def one_tile(step, carry):
        n = step // 4
        lanes_at = pl.ds(pl.multiple_of((step % 4) * LANES, LANES), LANES)
        owner = place[n]
        for pair in range(2):
            for row in range(2):
                acc_even = acc_odd = None
                for core in range(2):
                    for angle in range(2):
                        i = angle * 4 + pair * 2 + row
                        left = jnp.broadcast_to(left_s[n, core, i : i + 1, lanes_at], (16, LANES))
                        left = left.astype(jnp.int16)
                        low = left & jnp.int16(LANES - 1)
                        taps = [
                            lane_gather(tab_s[core * 2 + angle, :, k * LANES : (k + 1) * LANES], low)
                            for k in range(8)
                        ]
                        for bit in (128, 256, 512):
                            high = (left & jnp.int16(bit)) != 0
                            taps = [
                                jnp.where(high, taps[k + 1], taps[k]) for k in range(0, len(taps), 2)
                            ]
                        both = taps[0].astype(jnp.float32)
                        weight = jnp.where(
                            even,
                            jnp.broadcast_to(w1_s[n, core, i : i + 1, lanes_at], (8, LANES)),
                            jnp.broadcast_to(w2_s[n, core, i : i + 1, lanes_at], (8, LANES)),
                        )
                        part_even, part_odd = both[:8] * weight, both[8:] * weight
                        acc_even = part_even if acc_even is None else acc_even + part_even
                        acc_odd = part_odd if acc_odd is None else acc_odd + part_odd
                total = jnp.where(
                    even, acc_even + pltpu.roll(acc_even, 7, 0), acc_odd + pltpu.roll(acc_odd, 1, 0)
                )
                out[2 * owner + pair, row * 8 : (row + 1) * 8, lanes_at] = total.astype(out.dtype)
        return carry

    lax.fori_loop(0, 32, one_tile, 0)


def project(place, tab, coords):
    vmem = pl.BlockSpec(memory_space=pltpu.VMEM)
    return pl.pallas_call(
        project_kernel,
        out_shape=jax.ShapeDtypeStruct((16, 16, 512), jnp.bfloat16),
        in_specs=[pl.BlockSpec(memory_space=pltpu.SMEM), vmem] + [vmem] * 8,
        out_specs=vmem,
        scratch_shapes=[
            pltpu.VMEM((4, 16, 1024), jnp.bfloat16),
            pltpu.VMEM((8, 2, 8, 512), jnp.int32),
            pltpu.VMEM((8, 2, 8, 512), jnp.float32),
            pltpu.VMEM((8, 2, 8, 512), jnp.float32),
        ],
        name="project",
    )(place, tab, *coords)


def shards(sinogram, detector_coord):
    slices, angles, bins = sinogram.shape
    width = detector_coord.shape[2]
    core, z_high, x = lax.axis_index("core"), lax.axis_index("z_hi"), lax.axis_index("x")
    swap = [(0, 1), (1, 0)]

    by_core = detector_coord.reshape(angles, 2, 2, 2, width)
    keep = lax.dynamic_index_in_dim(by_core, core, 2, keepdims=False).reshape(8, width)
    give = lax.dynamic_index_in_dim(by_core, 1 - core, 2, keepdims=False).reshape(8, width)
    own = jnp.stack([keep, lax.ppermute(give, "core", swap)])
    other = lax.ppermute(own, "z_hi", swap)

    def from_x(array, step):
        return lax.ppermute(array, "x", [((i + step) % 4, i) for i in range(4)])

    coords = [own] + [from_x(own, s) for s in (1, 2, 3)]
    coords += [other] + [from_x(other, s) for s in (1, 2, 3)]
    places = [4 * z + (x + s) % 4 for z in (z_high, 1 - z_high) for s in range(4)]
    place = jnp.stack(places).astype(jnp.int32)

    other_sino = lax.ppermute(sinogram, "core", swap)
    rows = jnp.stack([sinogram, other_sino]).transpose(0, 2, 1, 3)[:, :, SLICE_ORDER, :]
    filtered = jnp.dot(
        rows.reshape(4 * slices, bins), ramp_table(bins), preferred_element_type=jnp.float32
    ).astype(jnp.bfloat16)
    ahead = jnp.concatenate([filtered[:, 1:], filtered[:, :1]], axis=1)
    tab = jnp.stack([filtered, ahead], axis=1).reshape(4, 16, bins)

    partial = project(place, tab, coords)
    parts = lax.all_to_all(partial, ("y", "z_lo"), 0, 0, tiled=True)
    scale = jnp.float32(math.pi / (angles * lax.axis_size(("y", "z_lo", "core"))))
    image_rows = jnp.sum(parts.astype(jnp.float32), axis=0) * scale
    return image_rows.reshape(2, slices, width)


def solution(mesh):
    names = ("y", "z_lo", "core", "z_hi", "x")
    fine = Mesh(mesh.devices.reshape(4, 4, 2, 2, 4), names)
    ang, sl = ("y", "z_lo", "core"), ("z_hi", "x")
    in_specs = (P(sl, ang, None), P(ang, sl, None))
    return jax.shard_map(
        shards, mesh=fine, in_specs=in_specs, out_specs=P(ang, sl, None), check_vma=False
    )
```

time: 154 us -> 53.7 us (0.35); the launches traced: 151 us -> 53.3 us
  matrix products: 75.6 us -> 3.22 us
  waiting for transfers between devices: 43.7 us -> 2.57 us
  blocking collectives: 0 us -> 15.1 us
  Pallas kernels: 0 us -> 10.4 us
  starting transfers between devices: 24.1 us -> 16.2 us
    dot_general x33 -> x1, matrix products: 75.6 us -> 3.22 us  [shards(): jnp.dot(rows.reshape(4 * slices, bins), ramp_table(bins), preferred_eleme...]
    all_to_all x3 -> x0, waiting for transfers between devices: 43.7 us -> none  [the longest x2 36.3 us: sent_to_all(): lax.all_to_all(jnp.broadcast_to(array[None], (devices, *array.shape)), ax...]
    all_to_all x3 -> x0, starting transfers between devices: 24.1 us -> none  [the longest x2 15.7 us: sent_to_all(): lax.all_to_all(jnp.broadcast_to(array[None], (devices, *array.shape)), ax...]
    ppermute x0 -> x9, starting transfers between devices: none -> 16.2 us  [the longest x6 8.33 us: from_x(): return lax.ppermute(array, 'x', [((i + step) % 4, i) for i in range(4)])]
    all_to_all x0 -> x1, blocking collectives: none -> 15.1 us  [shards(): parts = lax.all_to_all(partial, ('y', 'z_lo'), 0, 0, tiled=True)]
    pallas_call x0 -> x1, Pallas kernels: none -> 10.4 us  [project(): pl.pallas_call(project_kernel, out_shape=jax.ShapeDtypeStruct((16, 16, 51...]
    broadcast_in_dim x4 -> x0, local copies, waits for them, and re-layouts: 2.6 us -> none  [sent_to_all(): jnp.broadcast_to(array[None], (devices, *array.shape))]
    ppermute x0 -> x9, waiting for transfers between devices: none -> 2.57 us  [the longest x6 2.56 us: from_x(): return lax.ppermute(array, 'x', [((i + step) % 4, i) for i in range(4)])]
  transfers between devices with their start and end apart: 3 -> 9, of which waited for: 3 -> 2; matrix products, arithmetic and copies ran while one was open for 3% -> 12% of each run, Pallas kernels for 0% -> 0%
where the time goes in v1:
time: 53.7 us; the launch traced here: 53.3 us
  starting transfers between devices  16.2 us (30%)
  blocking collectives  15.1 us (28%)
  Pallas kernels  10.4 us (19%)
  local copies, waits for them, and re-layouts  4.21 us (8%)
  matrix products  3.22 us (6%)
  waiting for transfers between devices  2.57 us (5%)
  other arithmetic  1.51 us (3%)
    all_to_all x1, blocking collectives, shards(): parts = lax.all_to_all(partial, ('y', 'z_lo'), 0, 0, tiled=True)  15.1 us
    pallas_call x1, Pallas kernels, project(): pl.pallas_call(project_kernel, out_shape=jax.ShapeDtypeStruct((16, 16, 51...  10.4 us
    ppermute x6, starting transfers between devices, from_x(): return lax.ppermute(array, 'x', [((i + step) % 4, i) for i in range(4)])  8.33 us
    ppermute x1, starting transfers between devices, shards(): other = lax.ppermute(own, 'z_hi', swap)  7.28 us
    dot_general x1, matrix products, shards(): jnp.dot(rows.reshape(4 * slices, bins), ramp_table(bins), preferred_eleme...  3.22 us
    ppermute x6, waiting for transfers between devices, from_x(): return lax.ppermute(array, 'x', [((i + step) % 4, i) for i in range(4)])  2.56 us
    unnamed x19, local copies, waits for them, and re-layouts  1.07 us
  transfers between devices with their start and end apart: 9, of which 2 were waited for; matrix products, arithmetic and copies ran while one was open for 12% of the time, Pallas kernels for 0%

profile of v1, /device:TPU:2, one launch (start us, length us, event | category | flops | bytes accessed | tf_op | source)
XLA Modules:
  0.0 53.3 jit_solution(750267258546519236)
XLA Ops:
  0.0 0.8 %reshape.20 = s32[2,2,2,2,512]{4,3,2,1,0:T(2,128)S(1)} reshape(s32[2,8,512]{2,1,0:T(8,128)} %param.4) | data formatting | bytes 65536 | tf_op jit(solution)/shard_map/reshape | solution.py:117
  0.8 0.1 collective-permute-start.1
  0.9 0.5 collective-permute-start
  1.4 0.7 %pad_clamp_fusion = s32[1024]{0:T(1024)S(1)} fusion(s32[8]{0:T(128)} %constant.91), kind=kLoop, calls=%fused_computation.22 | loop fusion | flops 1024 | bytes 4128 | tf_op jit(solution)/shard_map/gather | solution.py:132
  2.1 0.7 %stack.59.place = s32[8]{0:T(128)} concatenate(s32[1]{0:T(128)} %bitcast, s32[1]{0:T(128)} %bitcast.1, s32[1]{0:T(128)} %bitcast.2, s32[1]{0:T(128)} %bitcast.3, s32[1]{0:T(128)} %bitcast.4, s32[1]{0:T(128)} %bitcast.5, s32[1]{0:T(128)} %bitcast.6, s32[1]{0:T(128)} %bitcast.7), dimensions={0} | concatenate | bytes 64 | tf_op jit(solution)/shard_map/stack | solution.py:129
  2.8 7.3 %collective-permute-start.5 = (s32[2,8,512]{2,1,0:T(8,128)S(1)}, s32[2,8,512]{2,1,0:T(8,128)S(1)}, u32[]{:S(2)}, u32[]{:S(2)}) collective-permute-start(s32[2,8,512]{2,1,0:T(8,128)S(1)} %pad_add_fusion.refs_0_), channel_id=1, source_target_pairs={{0,4},{4,0},{1,5},{5,1},{2,6},{6,2},{3,7},{7,3},{8,12},{12,8},{9,1... | collective-permute-start | bytes 98312 | tf_op jit(solution)/shard_map/ppermute | solution.py:121
  10.1 1.5 %collective-permute-start.4 = (s32[2,8,512]{2,1,0:T(8,128)S(1)}, s32[2,8,512]{2,1,0:T(8,128)S(1)}, u32[]{:S(2)}, u32[]{:S(2)}) collective-permute-start(s32[2,8,512]{2,1,0:T(8,128)S(1)} %pad_add_fusion.refs_0_), channel_id=1, source_target_pairs={{3,0},{0,1},{1,2},{2,3},{7,4},{4,5},{5,6},{6,7},{11,8},{8,9},{9,10... | collective-permute-start | bytes 98312 | tf_op jit(solution)/shard_map/ppermute | solution.py:124
  11.6 1.1 %collective-permute-start.3 = (s32[2,8,512]{2,1,0:T(8,128)S(1)}, s32[2,8,512]{2,1,0:T(8,128)S(1)}, u32[]{:S(2)}, u32[]{:S(2)}) collective-permute-start(s32[2,8,512]{2,1,0:T(8,128)S(1)} %pad_add_fusion.refs_0_), channel_id=1, source_target_pairs={{2,0},{3,1},{0,2},{1,3},{6,4},{7,5},{4,6},{5,7},{10,8},{11,9},{8,1... | collective-permute-start | bytes 98312 | tf_op jit(solution)/shard_map/ppermute | solution.py:124
  12.7 2.2 %collective-permute-start.2 = (s32[2,8,512]{2,1,0:T(8,128)S(1)}, s32[2,8,512]{2,1,0:T(8,128)S(1)}, u32[]{:S(2)}, u32[]{:S(2)}) collective-permute-start(s32[2,8,512]{2,1,0:T(8,128)S(1)} %pad_add_fusion.refs_0_), channel_id=1, source_target_pairs={{1,0},{2,1},{3,2},{0,3},{5,4},{6,5},{7,6},{4,7},{9,8},{10,9},{11,1... | collective-permute-start | bytes 98312 | tf_op jit(solution)/shard_map/ppermute | solution.py:124
  14.8 0.1 maximum_bitcast_fusion
  14.9 0.7 %gather_fusion = bf16[8,2,2,1024]{3,2,1,0:T(2,128)(2,1)S(1)} fusion(bf16[2,2,8,1024]{3,1,2,0:T(2,128)(2,1)S(1)} %maximum_bitcast_fusion, s32[1024]{0:T(1024)S(1)} %pad_clamp_fusion), kind=kCustom, calls=%fused_computation | custom fusion | bytes 131104 | tf_op jit(solution)/shard_map/gather | solution.py:132
  15.6 3.2 %fusion.7 = bf16[32,1024]{1,0:T(8,128)(2,1)S(1)} fusion(bf16[32,1024]{1,0:T(8,128)(2,1)S(1)} %bitcast.31), kind=kOutput, calls=%fused_computation.13 | convolution fusion | flops 89161728 | bytes 131072 | tf_op jit(solution)/shard_map/dot_general | solution.py:133
  18.9 0.1 slice.10
  19.0 0.1 maximum_bitcast_fusion.1
  19.2 3.5 %collective-permute-start.7 = (s32[2,8,512]{2,1,0:T(8,128)S(1)}, s32[2,8,512]{2,1,0:T(8,128)S(1)}, u32[]{:S(2)}, u32[]{:S(2)}) collective-permute-start(s32[2,8,512]{2,1,0:T(8,128)S(1)} %collective-permute-done.5.refs_4_), channel_id=1, source_target_pairs={{2,0},{3,1},{0,2},{1,3},{6,4},{7,5},{4,6},{5,7},{10,8},{11,9},{8,1... | collective-permute-start | bytes 98312 | tf_op jit(solution)/shard_map/ppermute | solution.py:124
  22.7 0.1 copy.11
  22.8 0.4 copy-done.2
  23.3 0.7 %reshape.19.tab = bf16[4,16,1024]{2,1,0:T(8,128)(2,1)} reshape(bf16[32,2,1024]{2,1,0:T(2,128)(2,1)S(1)} %copy.11) | data formatting | bytes 262144 | tf_op jit(solution)/shard_map/reshape | solution.py:137
  24.0 0.7 %collective-permute-done.7.refs_6_ = s32[2,8,512]{2,1,0:T(8,128)S(1)} collective-permute-done((s32[2,8,512]{2,1,0:T(8,128)S(1)}, s32[2,8,512]{2,1,0:T(8,128)S(1)}, u32[]{:S(2)}, u32[]{:S(2)}) %collective-permute-start.7) | collective-permute-done | bytes 32800 | tf_op jit(solution)/shard_map/ppermute | solution.py:124
  24.7 1.9 %collective-permute-done.6.refs_5_ = s32[2,8,512]{2,1,0:T(8,128)S(1)} collective-permute-done((s32[2,8,512]{2,1,0:T(8,128)S(1)}, s32[2,8,512]{2,1,0:T(8,128)S(1)}, u32[]{:S(2)}, u32[]{:S(2)}) %collective-permute-start.6) | collective-permute-done | bytes 32800 | tf_op jit(solution)/shard_map/ppermute | solution.py:124
  26.6 0.6 %copy-done.7 = s32[2,8,512]{2,1,0:T(8,128)} copy-done((s32[2,8,512]{2,1,0:T(8,128)}, s32[2,8,512]{2,1,0:T(8,128)S(1)}, u32[]{:S(2)}) %copy-start.7) | copy-done | bytes 32792
  27.2 10.4 %project.1 = bf16[16,16,512]{2,1,0:T(8,128)(2,1)} custom-call(s32[8]{0:T(128)} %stack.59.place, bf16[4,16,1024]{2,1,0:T(8,128)(2,1)} %reshape.19.tab, s32[2,8,512]{2,1,0:T(8,128)} %copy-done, s32[2,8,512]{2,1,0:T(8,128)} %copy-done.4, s32[2,8,512]{2,1,0:T(8,128)} %copy-done.3, s32[2,8,512]{2,1,0:T(8,128)} %copy-done.2, s32[2,8,512]{2,1,0:T(8,128)} %copy-done.1, ...), custom_call_target="tpu_custom_call" | custom-call | tf_op jit(solution)/shard_map/project/pallas_call | solution.py:96
  37.6 15.1 %all_to_all.5 = bf16[16,16,512]{2,1,0:T(8,128)(2,1)S(1)} all-to-all(bf16[16,16,512]{2,1,0:T(8,128)(2,1)} %project.1), channel_id=1, replica_groups=mesh['y'=4,'z_lo'=4,'core'=2,'z_hi'=2,'x'=4] {'y','z_lo'}, dimensions={0} | all-to-all | bytes 524288 | tf_op jit(solution)/shard_map/all_to_all | solution.py:140
  52.7 0.6 %multiply_bitcast_fusion = f32[2,8,512]{2,1,0:T(8,128)} fusion(f32[16,512]{1,0:T(8,128)S(1)} %convert_reduce_fusion), kind=kLoop, calls=%fused_computation.19 | loop fusion | flops 8192 | bytes 65536 | tf_op jit(solution)/shard_map/mul | solution.py:142
  (33 shorter events, 0.3 us)
Async XLA Ops:
  0.0 14.8 %copy-start.8 = (bf16[8,2,1024]{2,1,0:T(2,128)(2,1)S(1)}, bf16[8,2,1024]{2,1,0:T(2,128)(2,1)}, u32[]{:S(2)}) copy-start(bf16[8,2,1024]{2,1,0:T(2,128)(2,1)} %param.3) | copy-start | bytes 98308
  0.8 1.9 %collective-permute-start.1 = (s32[8,512]{1,0:T(8,128)S(1)}, s32[8,512]{1,0:T(8,128)S(1)}, u32[]{:S(2)}, u32[]{:S(2)}) collective-permute-start(s32[8,512]{1,0:T(8,128)S(1)} %reshape.21), channel_id=1, source_target_pairs={{0,8},{8,0},{1,9},{9,1},{2,10},{10,2},{3,11},{11,3},{4,12},{12,4},... | collective-permute-start | bytes 49160 | tf_op jit(solution)/shard_map/ppermute | solution.py:120
  0.9 13.9 %collective-permute-start = (bf16[8,2,1024]{2,1,0:T(2,128)(2,1)}, bf16[8,2,1024]{2,1,0:T(2,128)(2,1)S(1)}, u32[]{:S(2)}, u32[]{:S(2)}) collective-permute-start(bf16[8,2,1024]{2,1,0:T(2,128)(2,1)} %param.3), channel_id=1, source_target_pairs={{0,8},{8,0},{1,9},{9,1},{2,10},{10,2},{3,11},{11,3},{4,12},{12,4},... | collective-permute-start | bytes 98312 | tf_op jit(solution)/shard_map/ppermute | solution.py:131
  2.8 16.1 %copy-start = (s32[2,8,512]{2,1,0:T(8,128)}, s32[2,8,512]{2,1,0:T(8,128)S(1)}, u32[]{:S(2)}) copy-start(s32[2,8,512]{2,1,0:T(8,128)S(1)} %pad_add_fusion.refs_0_) | copy-start | bytes 98308
  2.8 16.3 %collective-permute-start.5 = (s32[2,8,512]{2,1,0:T(8,128)S(1)}, s32[2,8,512]{2,1,0:T(8,128)S(1)}, u32[]{:S(2)}, u32[]{:S(2)}) collective-permute-start(s32[2,8,512]{2,1,0:T(8,128)S(1)} %pad_add_fusion.refs_0_), channel_id=1, source_target_pairs={{0,4},{4,0},{1,5},{5,1},{2,6},{6,2},{3,7},{7,3},{8,12},{12,8},{9,1... | collective-permute-start | bytes 98312 | tf_op jit(solution)/shard_map/ppermute | solution.py:121
  10.1 12.6 %collective-permute-start.4 = (s32[2,8,512]{2,1,0:T(8,128)S(1)}, s32[2,8,512]{2,1,0:T(8,128)S(1)}, u32[]{:S(2)}, u32[]{:S(2)}) collective-permute-start(s32[2,8,512]{2,1,0:T(8,128)S(1)} %pad_add_fusion.refs_0_), channel_id=1, source_target_pairs={{3,0},{0,1},{1,2},{2,3},{7,4},{4,5},{5,6},{6,7},{11,8},{8,9},{9,10... | collective-permute-start | bytes 98312 | tf_op jit(solution)/shard_map/ppermute | solution.py:124
  11.6 12.4 %collective-permute-start.3 = (s32[2,8,512]{2,1,0:T(8,128)S(1)}, s32[2,8,512]{2,1,0:T(8,128)S(1)}, u32[]{:S(2)}, u32[]{:S(2)}) collective-permute-start(s32[2,8,512]{2,1,0:T(8,128)S(1)} %pad_add_fusion.refs_0_), channel_id=1, source_target_pairs={{2,0},{3,1},{0,2},{1,3},{6,4},{7,5},{4,6},{5,7},{10,8},{11,9},{8,1... | collective-permute-start | bytes 98312 | tf_op jit(solution)/shard_map/ppermute | solution.py:124
  12.7 11.3 %collective-permute-start.2 = (s32[2,8,512]{2,1,0:T(8,128)S(1)}, s32[2,8,512]{2,1,0:T(8,128)S(1)}, u32[]{:S(2)}, u32[]{:S(2)}) collective-permute-start(s32[2,8,512]{2,1,0:T(8,128)S(1)} %pad_add_fusion.refs_0_), channel_id=1, source_target_pairs={{1,0},{2,1},{3,2},{0,3},{5,4},{6,5},{7,6},{4,7},{9,8},{10,9},{11,1... | collective-permute-start | bytes 98312 | tf_op jit(solution)/shard_map/ppermute | solution.py:124
  19.1 3.8 %copy-start.1 = (s32[2,8,512]{2,1,0:T(8,128)}, s32[2,8,512]{2,1,0:T(8,128)S(1)}, u32[]{:S(2)}) copy-start(s32[2,8,512]{2,1,0:T(8,128)S(1)} %collective-permute-done.5.refs_4_) | copy-start | bytes 98308
  19.1 4.9 %collective-permute-start.8 = (s32[2,8,512]{2,1,0:T(8,128)S(1)}, s32[2,8,512]{2,1,0:T(8,128)S(1)}, u32[]{:S(2)}, u32[]{:S(2)}) collective-permute-start(s32[2,8,512]{2,1,0:T(8,128)S(1)} %collective-permute-done.5.refs_4_), channel_id=1, source_target_pairs={{3,0},{0,1},{1,2},{2,3},{7,4},{4,5},{5,6},{6,7},{11,8},{8,9},{9,10... | collective-permute-start | bytes 98312 | tf_op jit(solution)/shard_map/ppermute | solution.py:124
  19.2 5.5 %collective-permute-start.7 = (s32[2,8,512]{2,1,0:T(8,128)S(1)}, s32[2,8,512]{2,1,0:T(8,128)S(1)}, u32[]{:S(2)}, u32[]{:S(2)}) collective-permute-start(s32[2,8,512]{2,1,0:T(8,128)S(1)} %collective-permute-done.5.refs_4_), channel_id=1, source_target_pairs={{2,0},{3,1},{0,2},{1,3},{6,4},{7,5},{4,6},{5,7},{10,8},{11,9},{8,1... | collective-permute-start | bytes 98312 | tf_op jit(solution)/shard_map/ppermute | solution.py:124
  22.7 0.6 %copy-start.2 = (s32[2,8,512]{2,1,0:T(8,128)}, s32[2,8,512]{2,1,0:T(8,128)S(1)}, u32[]{:S(2)}) copy-start(s32[2,8,512]{2,1,0:T(8,128)S(1)} %collective-permute-done.4.refs_3_) | copy-start | bytes 98308
  22.7 3.9 %collective-permute-start.6 = (s32[2,8,512]{2,1,0:T(8,128)S(1)}, s32[2,8,512]{2,1,0:T(8,128)S(1)}, u32[]{:S(2)}, u32[]{:S(2)}) collective-permute-start(s32[2,8,512]{2,1,0:T(8,128)S(1)} %collective-permute-done.5.refs_4_), channel_id=1, source_target_pairs={{1,0},{2,1},{3,2},{0,3},{5,4},{6,5},{7,6},{4,7},{9,8},{10,9},{11,1... | collective-permute-start | bytes 98312 | tf_op jit(solution)/shard_map/ppermute | solution.py:124
  24.0 2.6 %copy-start.3 = (s32[2,8,512]{2,1,0:T(8,128)}, s32[2,8,512]{2,1,0:T(8,128)S(1)}, u32[]{:S(2)}) copy-start(s32[2,8,512]{2,1,0:T(8,128)S(1)} %collective-permute-done.3.refs_2_) | copy-start | bytes 98308
  24.0 2.6 %copy-start.4 = (s32[2,8,512]{2,1,0:T(8,128)}, s32[2,8,512]{2,1,0:T(8,128)S(1)}, u32[]{:S(2)}) copy-start(s32[2,8,512]{2,1,0:T(8,128)S(1)} %collective-permute-done.2.refs_1_) | copy-start | bytes 98308
  24.0 2.6 %copy-start.5 = (s32[2,8,512]{2,1,0:T(8,128)}, s32[2,8,512]{2,1,0:T(8,128)S(1)}, u32[]{:S(2)}) copy-start(s32[2,8,512]{2,1,0:T(8,128)S(1)} %collective-permute-done.8.refs_7_) | copy-start | bytes 98308
  24.7 1.9 %copy-start.6 = (s32[2,8,512]{2,1,0:T(8,128)}, s32[2,8,512]{2,1,0:T(8,128)S(1)}, u32[]{:S(2)}) copy-start(s32[2,8,512]{2,1,0:T(8,128)S(1)} %collective-permute-done.7.refs_6_) | copy-start | bytes 98308
  26.6 0.6 %copy-start.7 = (s32[2,8,512]{2,1,0:T(8,128)}, s32[2,8,512]{2,1,0:T(8,128)S(1)}, u32[]{:S(2)}) copy-start(s32[2,8,512]{2,1,0:T(8,128)S(1)} %collective-permute-done.6.refs_5_) | copy-start | bytes 98308

commit v2 on v1

v2 whole, which is shorter than its diff:
```python
import math

import jax
import jax.numpy as jnp
from jax import lax
from jax.experimental import pallas as pl
from jax.experimental.pallas import tpu as pltpu
from jax.sharding import Mesh
from jax.sharding import PartitionSpec as P

LANES = 128
LANE_DIMS = lax.GatherDimensionNumbers(
    offset_dims=(),
    collapsed_slice_dims=(1,),
    start_index_map=(1,),
    operand_batching_dims=(0,),
    start_indices_batching_dims=(0,),
)
VMEM = pl.BlockSpec(memory_space=pltpu.VMEM)


def lane_gather(table, lanes):
    return lax.gather(
        table, lanes[..., None], LANE_DIMS, (1, 1), mode=lax.GatherScatterMode.PROMISE_IN_BOUNDS
    )


def filter_kernel(own, other, out, strip):
    bins = own.shape[1]
    blocks = bins // LANES
    for j in range(2 * blocks - 1):
        first = lax.broadcasted_iota(jnp.int32, (LANES, LANES), 0)
        second = lax.broadcasted_iota(jnp.int32, (LANES, LANES), 1)
        offset = second - first + (j - blocks + 1) * LANES
        offset_sq = jnp.maximum((offset * offset).astype(jnp.float32), jnp.float32(1.0))
        values = jnp.where(
            (offset & 1) != 0, jnp.float32(-1.0 / math.pi**2) / offset_sq, jnp.float32(0.0)
        )
        if j == blocks - 1:
            values = jnp.where(offset == 0, jnp.float32(0.25), values)
        strip[:, j * LANES : (j + 1) * LANES] = values.astype(jnp.bfloat16)
    rows = jnp.concatenate([own[...], other[...]], axis=0)
    total = None
    for k in range(blocks):
        start = (blocks - 1 - k) * LANES
        part = jnp.dot(
            rows[:, k * LANES : (k + 1) * LANES],
            strip[:, start : start + bins],
            preferred_element_type=jnp.float32,
        )
        total = part if total is None else total + part
    out[...] = total.astype(jnp.bfloat16).astype(jnp.float32)


def filter_rows(own, other):
    rows, bins = own.shape
    return pl.pallas_call(
        filter_kernel,
        out_shape=jax.ShapeDtypeStruct((2 * rows, bins), jnp.float32),
        in_specs=[VMEM, VMEM],
        out_specs=VMEM,
        scratch_shapes=[pltpu.VMEM((LANES, 2 * bins - LANES), jnp.bfloat16)],
        compiler_params=pltpu.CompilerParams(vmem_limit_bytes=8 * 2**20),
        name="filter_rows",
    )(own, other)


def transposed(tiles):
    sublane = lax.broadcasted_iota(jnp.int32, (8, LANES), 0)
    for step in (4, 2, 1):
        low = (sublane & step) == 0
        done = list(tiles)
        for i in range(8):
            if not i & step:
                a, b = tiles[i], tiles[i + step]
                done[i] = jnp.where(low, a, pltpu.roll(b, step, 0))
                done[i + step] = jnp.where(low, pltpu.roll(a, 8 - step, 0), b)
        tiles = done
    return tiles


def project_half(tab, coords, out, base):
    x = lax.axis_index("x")
    sublane = lax.broadcasted_iota(jnp.int32, (8, LANES), 0)

    def one_tile(step):
        two, at = step // 4, pl.ds(pl.multiple_of((step % 4) * LANES, LANES), LANES)
        sums = [None] * 8
        for core in range(2):
            first, second = coords[2 * two, core, :, at], coords[2 * two + 1, core, :, at]
            for angle in range(2):
                if angle == 0:
                    c = jnp.where(sublane < 4, first, pltpu.roll(second, 4, 0))
                else:
                    c = jnp.where(sublane < 4, pltpu.roll(first, 4, 0), second)
                left = c >> 20
                fraction = (c & 1048575).astype(jnp.float32) * jnp.float32(1.0 / 1048576.0)
                w_left = (1.0 - fraction).astype(jnp.bfloat16).astype(jnp.float32)
                w_right = fraction.astype(jnp.bfloat16).astype(jnp.float32)
                bins = jnp.concatenate([left, left + 1], axis=0).astype(jnp.int16)
                lanes = bins & jnp.int16(LANES - 1)
                high = [(bins & jnp.int16(bit)) != 0 for bit in (128, 256, 512)]
                for s in range(8):
                    row = core * 16 + s * 2 + angle
                    taps = []
                    for k in range(8):
                        source = jnp.broadcast_to(
                            tab[row : row + 1, k * LANES : (k + 1) * LANES], (16, LANES)
                        )
                        taps.append(lane_gather(source.astype(jnp.bfloat16), lanes))
                    for mask in high:
                        taps = [
                            jnp.where(mask, taps[k + 1], taps[k]) for k in range(0, len(taps), 2)
                        ]
                    both = taps[0].astype(jnp.float32)
                    part = both[:8] * w_left + both[8:] * w_right
                    sums[s] = part if sums[s] is None else sums[s] + part
        rows = transposed(sums)
        for i in range(2):
            owner = base + 2 * ((x + 2 * two + i) & 3)
            for pair in range(2):
                for r in range(2):
                    value = rows[i * 4 + pair * 2 + r].astype(out.dtype)
                    out[owner + pair, r * 8 : (r + 1) * 8, at] = value

    def two_tiles(step, carry):
        one_tile(2 * step)
        one_tile(2 * step + 1)
        return carry

    lax.fori_loop(0, 4, two_tiles, 0)


def near_kernel(tab, c0, c1, c2, c3, out, coords):
    for i, c in enumerate((c0, c1, c2, c3)):
        coords[i] = c[...]
    project_half(tab, coords, out, 0)


def far_kernel(tab, c0, c1, c2, c3, near, out, coords):
    for i, c in enumerate((c0, c1, c2, c3)):
        coords[i] = c[...]
    z_high = lax.axis_index("z_hi")
    out[pl.ds(8 * z_high, 8)] = near[...]
    project_half(tab, coords, out, 8 * (1 - z_high))


def project(kernel, owners, operands, name):
    return pl.pallas_call(
        kernel,
        out_shape=jax.ShapeDtypeStruct((owners, 16, 512), jnp.bfloat16),
        in_specs=[VMEM] * len(operands),
        out_specs=VMEM,
        scratch_shapes=[pltpu.VMEM((4, 2, 8, 512), jnp.int32)],
        compiler_params=pltpu.CompilerParams(vmem_limit_bytes=8 * 2**20),
        name=name,
    )(*operands)


def shards(sinogram, detector_coord):
    slices, angles, bins = sinogram.shape
    width = detector_coord.shape[2]
    core = lax.axis_index("core")
    swap = [(0, 1), (1, 0)]

    by_core = detector_coord.reshape(angles, 2, 2, 2, width)
    keep = lax.dynamic_index_in_dim(by_core, core, 2, keepdims=False).reshape(8, width)
    give = lax.dynamic_index_in_dim(by_core, 1 - core, 2, keepdims=False).reshape(8, width)
    own = jnp.stack([keep, lax.ppermute(give, "core", swap)])
    other = lax.ppermute(own, "z_hi", swap)

    def from_x(array, step):
        return lax.ppermute(array, "x", [((i + step) % 4, i) for i in range(4)])

    near = [own] + [from_x(own, s) for s in (1, 2, 3)]
    far = [other] + [from_x(other, s) for s in (1, 2, 3)]

    other_sino = lax.ppermute(sinogram, "core", swap)
    tab = filter_rows(
        sinogram.reshape(slices * angles, bins), other_sino.reshape(slices * angles, bins)
    )
    half = project(near_kernel, 8, [tab, *near], "near")
    partial = project(far_kernel, 16, [tab, *far, half], "far")
    parts = lax.all_to_all(partial, ("y", "z_lo"), 0, 0, tiled=True)
    scale = jnp.float32(math.pi / (angles * lax.axis_size(("y", "z_lo", "core"))))
    image_rows = jnp.sum(parts.astype(jnp.float32), axis=0) * scale
    return image_rows.reshape(2, slices, width)


def solution(mesh):
    names = ("y", "z_lo", "core", "z_hi", "x")
    fine = Mesh(mesh.devices.reshape(4, 4, 2, 2, 4), names)
    ang, sl = ("y", "z_lo", "core"), ("z_hi", "x")
    in_specs = (P(sl, ang, None), P(ang, sl, None))
    return jax.shard_map(
        shards, mesh=fine, in_specs=in_specs, out_specs=P(ang, sl, None), check_vma=False
    )
```

time: 53.7 us -> 40.6 us (0.76)
  Pallas kernels: 10.4 us -> 5.88 us
  local copies, waits for them, and re-layouts: 4.21 us -> 0.86 us
  matrix products: 3.22 us -> 0 us
  other arithmetic: 1.51 us -> 0.66 us
  waiting for transfers between devices: 2.57 us -> 1.74 us
  starting transfers between devices: 16.2 us -> 15.5 us
    pallas_call x1 -> x3, Pallas kernels: 10.4 us -> 5.88 us  [the longest x2 5.26 us: project(): pl.pallas_call(kernel, out_shape=jax.ShapeDtypeStruct((owners, 16, 512),...]
    dot_general x1 -> x0, matrix products: 3.22 us -> none  [shards(): jnp.dot(rows.reshape(4 * slices, bins), ramp_table(bins), preferred_eleme...]
    ppermute x6, waiting for transfers between devices: 2.56 us -> 0.58 us  [from_x(): return lax.ppermute(array, 'x', [((i + step) % 4, i) for i in range(4)])]
    ppermute x1, waiting for transfers between devices: 0.01 us -> 1.15 us  [shards(): own = jnp.stack([keep, lax.ppermute(give, 'core', swap)])]
    unnamed x19 -> x3, local copies, waits for them, and re-layouts: 1.07 us -> 0.02 us
    another operation x2 -> x0, local copies, waits for them, and re-layouts: 0.81 us -> none  [the longest x1 0.67 us: shards(): place = jnp.stack(places).astype(jnp.int32)]
    gather x2 -> x0, local copies, waits for them, and re-layouts: 0.71 us -> none  [shards(): jnp.stack([sinogram, other_sino]).transpose(0, 2, 1, 3)]
    reshape x1 -> x2, local copies, waits for them, and re-layouts: 0.7 us -> 0.04 us  [the longest x1 0.02 us: shards(): other_sino.reshape(slices * angles, bins)]
  transfers between devices with their start and end apart: 9 -> 9, of which waited for: 2 -> 2; matrix products, arithmetic and copies ran while one was open for 12% -> 0% of each run, Pallas kernels for 0% -> 8%
where the time goes in v2:
time: 40.6 us; the launch traced here: 40 us
  starting transfers between devices  15.5 us (38%)
  blocking collectives  15.2 us (37%)
  Pallas kernels  5.88 us (14%)
  waiting for transfers between devices  1.74 us (4%)
  local copies, waits for them, and re-layouts  0.86 us (2%)
  other arithmetic  0.66 us (2%)
    all_to_all x1, blocking collectives, shards(): parts = lax.all_to_all(partial, ('y', 'z_lo'), 0, 0, tiled=True)  15.2 us
    ppermute x6, starting transfers between devices, from_x(): return lax.ppermute(array, 'x', [((i + step) % 4, i) for i in range(4)])  8.26 us
    ppermute x1, starting transfers between devices, shards(): other = lax.ppermute(own, 'z_hi', swap)  7.19 us
    pallas_call x2, Pallas kernels, project(): pl.pallas_call(kernel, out_shape=jax.ShapeDtypeStruct((owners, 16, 512),...  5.26 us
    ppermute x1, waiting for transfers between devices, shards(): own = jnp.stack([keep, lax.ppermute(give, 'core', swap)])  1.15 us
  transfers between devices with their start and end apart: 9, of which 2 were waited for; matrix products, arithmetic and copies ran while one was open for 0% of the time, Pallas kernels for 8%

profile of v2, /device:TPU:2, one launch (start us, length us, event | category | flops | bytes accessed | tf_op | source)
XLA Modules:
  0.0 40.0 jit_solution(5815338523095626390)
XLA Ops:
  0.0 0.8 %reshape.20 = s32[2,2,2,2,512]{4,3,2,1,0:T(2,128)S(1)} reshape(s32[2,8,512]{2,1,0:T(8,128)} %param.3) | data formatting | bytes 65536 | tf_op jit(solution)/shard_map/reshape | solution.py:166
  0.8 0.1 collective-permute-start.1
  0.9 1.1 %collective-permute-done.1 = s32[8,512]{1,0:T(8,128)S(1)} collective-permute-done((s32[8,512]{1,0:T(8,128)S(1)}, s32[8,512]{1,0:T(8,128)S(1)}, u32[]{:S(2)}, u32[]{:S(2)}) %collective-permute-start.1) | collective-permute-done | bytes 16416 | tf_op jit(solution)/shard_map/ppermute | solution.py:169
  2.1 7.2 %collective-permute-start.2 = (s32[2,8,512]{2,1,0:T(8,128)S(1)}, s32[2,8,512]{2,1,0:T(8,128)S(1)}, u32[]{:S(2)}, u32[]{:S(2)}) collective-permute-start(s32[2,8,512]{2,1,0:T(8,128)S(1)} %pad_add_fusion.c0), channel_id=1, source_target_pairs={{0,4},{4,0},{1,5},{5,1},{2,6},{6,2},{3,7},{7,3},{8,12},{12,8},{9,1... | collective-permute-start | bytes 98312 | tf_op jit(solution)/shard_map/ppermute | solution.py:170
  9.3 0.0 collective-permute-start
  9.3 1.5 %collective-permute-start.8 = (s32[2,8,512]{2,1,0:T(8,128)S(1)}, s32[2,8,512]{2,1,0:T(8,128)S(1)}, u32[]{:S(2)}, u32[]{:S(2)}) collective-permute-start(s32[2,8,512]{2,1,0:T(8,128)S(1)} %pad_add_fusion.c0), channel_id=1, source_target_pairs={{3,0},{0,1},{1,2},{2,3},{7,4},{4,5},{5,6},{6,7},{11,8},{8,9},{9,10... | collective-permute-start | bytes 98312 | tf_op jit(solution)/shard_map/ppermute | solution.py:173
  10.8 1.1 %collective-permute-start.7 = (s32[2,8,512]{2,1,0:T(8,128)S(1)}, s32[2,8,512]{2,1,0:T(8,128)S(1)}, u32[]{:S(2)}, u32[]{:S(2)}) collective-permute-start(s32[2,8,512]{2,1,0:T(8,128)S(1)} %pad_add_fusion.c0), channel_id=1, source_target_pairs={{2,0},{3,1},{0,2},{1,3},{6,4},{7,5},{4,6},{5,7},{10,8},{11,9},{8,1... | collective-permute-start | bytes 98312 | tf_op jit(solution)/shard_map/ppermute | solution.py:173
  11.9 2.2 %collective-permute-start.6 = (s32[2,8,512]{2,1,0:T(8,128)S(1)}, s32[2,8,512]{2,1,0:T(8,128)S(1)}, u32[]{:S(2)}, u32[]{:S(2)}) collective-permute-start(s32[2,8,512]{2,1,0:T(8,128)S(1)} %pad_add_fusion.c0), channel_id=1, source_target_pairs={{1,0},{2,1},{3,2},{0,3},{5,4},{6,5},{7,6},{4,7},{9,8},{10,9},{11,1... | collective-permute-start | bytes 98312 | tf_op jit(solution)/shard_map/ppermute | solution.py:173
  14.1 0.0 collective-permute-done.2.c0
  14.1 0.0 collective-permute-start.5
  14.1 0.0 collective-permute-done
  14.1 3.5 %collective-permute-start.4 = (s32[2,8,512]{2,1,0:T(8,128)S(1)}, s32[2,8,512]{2,1,0:T(8,128)S(1)}, u32[]{:S(2)}, u32[]{:S(2)}) collective-permute-start(s32[2,8,512]{2,1,0:T(8,128)S(1)} %collective-permute-done.2.c0), channel_id=1, source_target_pairs={{2,0},{3,1},{0,2},{1,3},{6,4},{7,5},{4,6},{5,7},{10,8},{11,9},{8,1... | collective-permute-start | bytes 98312 | tf_op jit(solution)/shard_map/ppermute | solution.py:173
  17.6 0.0 collective-permute-done.8.c3
  17.6 0.0 collective-permute-start.3
  17.6 0.6 %filter_rows.1.tab = f32[32,1024]{1,0:T(8,128)S(1)} custom-call(bf16[16,1024]{1,0:T(8,128)(2,1)S(1)} %reshape.18.own, bf16[16,1024]{1,0:T(8,128)(2,1)S(1)} %reshape.19.other), custom_call_target="tpu_custom_call" | custom-call | tf_op jit(solution)/shard_map/filter_rows/pallas_call | solution.py:57
  18.2 0.0 collective-permute-done.7.c2
  18.2 0.0 collective-permute-done.6.c1
  18.3 2.6 %near.1 = bf16[8,16,512]{2,1,0:T(8,128)(2,1)S(1)} custom-call(f32[32,1024]{1,0:T(8,128)S(1)} %filter_rows.1.tab, s32[2,8,512]{2,1,0:T(8,128)S(1)} %pad_add_fusion.c0, s32[2,8,512]{2,1,0:T(8,128)S(1)} %collective-permute-done.6.c1, s32[2,8,512]{2,1,0:T(8,128)S(1)} %collective-permute-done.7.c2, s32[2,8,512]{2,1,0:T(8,128)S(1)} %collective-permute-done.8.c3), custom_call_target="tpu_custom_call" | custom-call | tf_op jit(solution)/shard_map/near/pallas_call | solution.py:149
  20.9 0.0 collective-permute-done.5.c3
  20.9 0.0 collective-permute-done.4.c2
  20.9 0.6 %collective-permute-done.3.c1 = s32[2,8,512]{2,1,0:T(8,128)S(1)} collective-permute-done((s32[2,8,512]{2,1,0:T(8,128)S(1)}, s32[2,8,512]{2,1,0:T(8,128)S(1)}, u32[]{:S(2)}, u32[]{:S(2)}) %collective-permute-start.3) | collective-permute-done | bytes 32800 | tf_op jit(solution)/shard_map/ppermute | solution.py:173
  21.5 2.6 %far.1 = bf16[16,16,512]{2,1,0:T(8,128)(2,1)S(1)} custom-call(f32[32,1024]{1,0:T(8,128)S(1)} %filter_rows.1.tab, s32[2,8,512]{2,1,0:T(8,128)S(1)} %collective-permute-done.2.c0, s32[2,8,512]{2,1,0:T(8,128)S(1)} %collective-permute-done.3.c1, s32[2,8,512]{2,1,0:T(8,128)S(1)} %collective-permute-done.4.c2, s32[2,8,512]{2,1,0:T(8,128)S(1)} %collective-permute-done.5.c3, ...), custom_call_target="tpu_custom_call" | custom-call | tf_op jit(solution)/shard_map/far/pallas_call | solution.py:149
  24.1 15.2 %all_to_all.5 = bf16[16,16,512]{2,1,0:T(8,128)(2,1)S(1)} all-to-all(bf16[16,16,512]{2,1,0:T(8,128)(2,1)S(1)} %far.1), channel_id=1, replica_groups=mesh['y'=4,'z_lo'=4,'core'=2,'z_hi'=2,'x'=4] {'y','z_lo'}, dimensions={0} | all-to-all | bytes 524288 | tf_op jit(solution)/shard_map/all_to_all | solution.py:184
  39.4 0.6 %multiply_bitcast_fusion = f32[2,8,512]{2,1,0:T(8,128)} fusion(f32[16,512]{1,0:T(8,128)S(1)} %convert_reduce_fusion), kind=kLoop, calls=%fused_computation.2 | loop fusion | flops 8192 | bytes 65536 | tf_op jit(solution)/shard_map/mul | solution.py:186
  (9 shorter events, 0.1 us)
Async XLA Ops:
  0.8 1.3 %collective-permute-start.1 = (s32[8,512]{1,0:T(8,128)S(1)}, s32[8,512]{1,0:T(8,128)S(1)}, u32[]{:S(2)}, u32[]{:S(2)}) collective-permute-start(s32[8,512]{1,0:T(8,128)S(1)} %reshape.21), channel_id=1, source_target_pairs={{0,8},{8,0},{1,9},{9,1},{2,10},{10,2},{3,11},{11,3},{4,12},{12,4},... | collective-permute-start | bytes 49160 | tf_op jit(solution)/shard_map/ppermute | solution.py:169
  2.1 7.2 %copy-start = (bf16[8,2,1024]{2,1,0:T(2,128)(2,1)S(1)}, bf16[8,2,1024]{2,1,0:T(2,128)(2,1)}, u32[]{:S(2)}) copy-start(bf16[8,2,1024]{2,1,0:T(2,128)(2,1)} %param.2) | copy-start | bytes 98308
  2.1 12.0 %collective-permute-start.2 = (s32[2,8,512]{2,1,0:T(8,128)S(1)}, s32[2,8,512]{2,1,0:T(8,128)S(1)}, u32[]{:S(2)}, u32[]{:S(2)}) collective-permute-start(s32[2,8,512]{2,1,0:T(8,128)S(1)} %pad_add_fusion.c0), channel_id=1, source_target_pairs={{0,4},{4,0},{1,5},{5,1},{2,6},{6,2},{3,7},{7,3},{8,12},{12,8},{9,1... | collective-permute-start | bytes 98312 | tf_op jit(solution)/shard_map/ppermute | solution.py:170
  9.3 4.8 %collective-permute-start = (bf16[8,2,1024]{2,1,0:T(2,128)(2,1)S(1)}, bf16[8,2,1024]{2,1,0:T(2,128)(2,1)S(1)}, u32[]{:S(2)}, u32[]{:S(2)}) collective-permute-start(bf16[8,2,1024]{2,1,0:T(2,128)(2,1)S(1)} %copy-done), channel_id=1, source_target_pairs={{0,8},{8,0},{1,9},{9,1},{2,10},{10,2},{3,11},{11,3},{4,12},{12,4},... | collective-permute-start | bytes 98312 | tf_op jit(solution)/shard_map/ppermute | solution.py:178
  9.3 8.3 %collective-permute-start.8 = (s32[2,8,512]{2,1,0:T(8,128)S(1)}, s32[2,8,512]{2,1,0:T(8,128)S(1)}, u32[]{:S(2)}, u32[]{:S(2)}) collective-permute-start(s32[2,8,512]{2,1,0:T(8,128)S(1)} %pad_add_fusion.c0), channel_id=1, source_target_pairs={{3,0},{0,1},{1,2},{2,3},{7,4},{4,5},{5,6},{6,7},{11,8},{8,9},{9,10... | collective-permute-start | bytes 98312 | tf_op jit(solution)/shard_map/ppermute | solution.py:173
  10.8 7.4 %collective-permute-start.7 = (s32[2,8,512]{2,1,0:T(8,128)S(1)}, s32[2,8,512]{2,1,0:T(8,128)S(1)}, u32[]{:S(2)}, u32[]{:S(2)}) collective-permute-start(s32[2,8,512]{2,1,0:T(8,128)S(1)} %pad_add_fusion.c0), channel_id=1, source_target_pairs={{2,0},{3,1},{0,2},{1,3},{6,4},{7,5},{4,6},{5,7},{10,8},{11,9},{8,1... | collective-permute-start | bytes 98312 | tf_op jit(solution)/shard_map/ppermute | solution.py:173
  11.9 6.3 %collective-permute-start.6 = (s32[2,8,512]{2,1,0:T(8,128)S(1)}, s32[2,8,512]{2,1,0:T(8,128)S(1)}, u32[]{:S(2)}, u32[]{:S(2)}) collective-permute-start(s32[2,8,512]{2,1,0:T(8,128)S(1)} %pad_add_fusion.c0), channel_id=1, source_target_pairs={{1,0},{2,1},{3,2},{0,3},{5,4},{6,5},{7,6},{4,7},{9,8},{10,9},{11,1... | collective-permute-start | bytes 98312 | tf_op jit(solution)/shard_map/ppermute | solution.py:173
  14.1 6.8 %collective-permute-start.5 = (s32[2,8,512]{2,1,0:T(8,128)S(1)}, s32[2,8,512]{2,1,0:T(8,128)S(1)}, u32[]{:S(2)}, u32[]{:S(2)}) collective-permute-start(s32[2,8,512]{2,1,0:T(8,128)S(1)} %collective-permute-done.2.c0), channel_id=1, source_target_pairs={{3,0},{0,1},{1,2},{2,3},{7,4},{4,5},{5,6},{6,7},{11,8},{8,9},{9,10... | collective-permute-start | bytes 98312 | tf_op jit(solution)/shard_map/ppermute | solution.py:173
  14.1 6.8 %collective-permute-start.4 = (s32[2,8,512]{2,1,0:T(8,128)S(1)}, s32[2,8,512]{2,1,0:T(8,128)S(1)}, u32[]{:S(2)}, u32[]{:S(2)}) collective-permute-start(s32[2,8,512]{2,1,0:T(8,128)S(1)} %collective-permute-done.2.c0), channel_id=1, source_target_pairs={{2,0},{3,1},{0,2},{1,3},{6,4},{7,5},{4,6},{5,7},{10,8},{11,9},{8,1... | collective-permute-start | bytes 98312 | tf_op jit(solution)/shard_map/ppermute | solution.py:173
  17.6 3.9 %collective-permute-start.3 = (s32[2,8,512]{2,1,0:T(8,128)S(1)}, s32[2,8,512]{2,1,0:T(8,128)S(1)}, u32[]{:S(2)}, u32[]{:S(2)}) collective-permute-start(s32[2,8,512]{2,1,0:T(8,128)S(1)} %collective-permute-done.2.c0), channel_id=1, source_target_pairs={{1,0},{2,1},{3,2},{0,3},{5,4},{6,5},{7,6},{4,7},{9,8},{10,9},{11,1... | collective-permute-start | bytes 98312 | tf_op jit(solution)/shard_map/ppermute | solution.py:173

commit v3 on v2

--- a/solution.py
+++ b/solution.py
@@ -79,15 +79,14 @@
     return tiles
 
 
-def project_half(tab, coords, out, base):
-    x = lax.axis_index("x")
+def project_rows(tab, first_x, second_x, out, places):
     sublane = lax.broadcasted_iota(jnp.int32, (8, LANES), 0)
 
     def one_tile(step):
-        two, at = step // 4, pl.ds(pl.multiple_of((step % 4) * LANES, LANES), LANES)
+        at = pl.ds(pl.multiple_of(step * LANES, LANES), LANES)
         sums = [None] * 8
         for core in range(2):
-            first, second = coords[2 * two, core, :, at], coords[2 * two + 1, core, :, at]
+            first, second = first_x[core, :, at], second_x[core, :, at]
             for angle in range(2):
                 if angle == 0:
                     c = jnp.where(sublane < 4, first, pltpu.roll(second, 4, 0))
@@ -117,32 +116,33 @@
                     sums[s] = part if sums[s] is None else sums[s] + part
         rows = transposed(sums)
         for i in range(2):
-            owner = base + 2 * ((x + 2 * two + i) & 3)
             for pair in range(2):
                 for r in range(2):
                     value = rows[i * 4 + pair * 2 + r].astype(out.dtype)
-                    out[owner + pair, r * 8 : (r + 1) * 8, at] = value
+                    out[places[i] + pair, r * 8 : (r + 1) * 8, at] = value
 
     def two_tiles(step, carry):
         one_tile(2 * step)
         one_tile(2 * step + 1)
         return carry
 
-    lax.fori_loop(0, 4, two_tiles, 0)
+    lax.fori_loop(0, 2, two_tiles, 0)
 
 
-def near_kernel(tab, c0, c1, c2, c3, out, coords):
-    for i, c in enumerate((c0, c1, c2, c3)):
-        coords[i] = c[...]
-    project_half(tab, coords, out, 0)
+def quarter_kernel(tab, first_x, second_x, out):
+    project_rows(tab, first_x, second_x, out, (0, 2))
 
 
-def far_kernel(tab, c0, c1, c2, c3, near, out, coords):
-    for i, c in enumerate((c0, c1, c2, c3)):
-        coords[i] = c[...]
-    z_high = lax.axis_index("z_hi")
-    out[pl.ds(8 * z_high, 8)] = near[...]
-    project_half(tab, coords, out, 8 * (1 - z_high))
+def last_kernel(tab, first_x, second_x, near_1, near_2, far_1, out):
+    x, z_high = lax.axis_index("x"), lax.axis_index("z_hi")
+    near_at, far_at = 8 * z_high, 8 * (1 - z_high)
+    places = [2 * ((x + step) & 3) for step in range(4)]
+    for step, part in ((0, near_1), (2, near_2)):
+        for i in range(2):
+            out[pl.ds(near_at + places[step + i], 2)] = part[2 * i : 2 * i + 2]
+    for i in range(2):
+        out[pl.ds(far_at + places[i], 2)] = far_1[2 * i : 2 * i + 2]
+    project_rows(tab, first_x, second_x, out, (far_at + places[2], far_at + places[3]))
 
 
 def project(kernel, owners, operands, name):
@@ -151,7 +151,6 @@
         out_shape=jax.ShapeDtypeStruct((owners, 16, 512), jnp.bfloat16),
         in_specs=[VMEM] * len(operands),
         out_specs=VMEM,
-        scratch_shapes=[pltpu.VMEM((4, 2, 8, 512), jnp.int32)],
         compiler_params=pltpu.CompilerParams(vmem_limit_bytes=8 * 2**20),
         name=name,
     )(*operands)
@@ -172,15 +171,17 @@
     def from_x(array, step):
         return lax.ppermute(array, "x", [((i + step) % 4, i) for i in range(4)])
 
-    near = [own] + [from_x(own, s) for s in (1, 2, 3)]
-    far = [other] + [from_x(other, s) for s in (1, 2, 3)]
-
     other_sino = lax.ppermute(sinogram, "core", swap)
     tab = filter_rows(
         sinogram.reshape(slices * angles, bins), other_sino.reshape(slices * angles, bins)
     )
-    half = project(near_kernel, 8, [tab, *near], "near")
-    partial = project(far_kernel, 16, [tab, *far, half], "far")
+    near = [own] + [from_x(own, s) for s in (1, 2, 3)]
+    near_1 = project(quarter_kernel, 4, [tab, *near[:2]], "near_1")
+    other, near_1 = lax.optimization_barrier((other, near_1))
+    far = [other] + [from_x(other, s) for s in (1, 2, 3)]
+    near_2 = project(quarter_kernel, 4, [tab, *near[2:]], "near_2")
+    far_1 = project(quarter_kernel, 4, [tab, *far[:2]], "far_1")
+    partial = project(last_kernel, 16, [tab, *far[2:], near_1, near_2, far_1], "far_2")
     parts = lax.all_to_all(partial, ("y", "z_lo"), 0, 0, tiled=True)
     scale = jnp.float32(math.pi / (angles * lax.axis_size(("y", "z_lo", "core"))))
     image_rows = jnp.sum(parts.astype(jnp.float32), axis=0) * scale

time: 40.6 us -> 41.4 us (1.020)
  starting transfers between devices: 15.5 us -> 16.2 us
  local copies, waits for them, and re-layouts: 0.86 us -> 1.49 us
    ppermute x6, starting transfers between devices: 8.26 us -> 10.7 us  [from_x(): return lax.ppermute(array, 'x', [((i + step) % 4, i) for i in range(4)])]
    ppermute x1, starting transfers between devices: 7.19 us -> 5.48 us  [shards(): other = lax.ppermute(own, 'z_hi', swap)]
    ppermute x6, waiting for transfers between devices: 0.58 us -> 1.38 us  [from_x(): return lax.ppermute(array, 'x', [((i + step) % 4, i) for i in range(4)])]
    unnamed x3, local copies, waits for them, and re-layouts: 0.02 us -> 0.64 us
    ppermute x1, waiting for transfers between devices: 1.15 us -> 0.52 us  [shards(): own = jnp.stack([keep, lax.ppermute(give, 'core', swap)])]
    pallas_call x2 -> x4, Pallas kernels: 5.26 us -> 5.22 us  [project(): pl.pallas_call(kernel, out_shape=jax.ShapeDtypeStruct((owners, 16, 512),...]
  transfers between devices with their start and end apart: 9 -> 9, of which waited for: 2 -> 2; matrix products, arithmetic and copies ran while one was open for 0% -> 0% of each run, Pallas kernels for 8% -> 11%
where the time goes in v3:
time: 41.4 us; the launch traced here: 41.1 us
  starting transfers between devices  16.2 us (39%)
  blocking collectives  14.9 us (36%)
  Pallas kernels  5.83 us (14%)
  waiting for transfers between devices  1.91 us (5%)
  local copies, waits for them, and re-layouts  1.49 us (4%)
  other arithmetic  0.66 us (2%)
    all_to_all x1, blocking collectives, shards(): parts = lax.all_to_all(partial, ('y', 'z_lo'), 0, 0, tiled=True)  14.9 us
    ppermute x6, starting transfers between devices, from_x(): return lax.ppermute(array, 'x', [((i + step) % 4, i) for i in range(4)])  10.7 us
    ppermute x1, starting transfers between devices, shards(): other = lax.ppermute(own, 'z_hi', swap)  5.48 us
    pallas_call x4, Pallas kernels, project(): pl.pallas_call(kernel, out_shape=jax.ShapeDtypeStruct((owners, 16, 512),...  5.22 us
    ppermute x6, waiting for transfers between devices, from_x(): return lax.ppermute(array, 'x', [((i + step) % 4, i) for i in range(4)])  1.38 us
  transfers between devices with their start and end apart: 9, of which 2 were waited for; matrix products, arithmetic and copies ran while one was open for 0% of the time, Pallas kernels for 11%

profile of v3, /device:TPU:2, one launch (start us, length us, event | category | flops | bytes accessed | tf_op | source)
XLA Modules:
  0.0 41.1 jit_solution(4682898857578505879)
XLA Ops:
  0.0 0.8 %reshape.20 = s32[2,2,2,2,512]{4,3,2,1,0:T(2,128)S(1)} reshape(s32[2,8,512]{2,1,0:T(8,128)} %param.3) | data formatting | bytes 65536 | tf_op jit(solution)/shard_map/reshape | solution.py:165
  0.8 0.0 copy-start
  0.8 0.1 collective-permute-start.1
  0.9 0.6 %copy-done = bf16[8,2,1024]{2,1,0:T(2,128)(2,1)S(1)} copy-done((bf16[8,2,1024]{2,1,0:T(2,128)(2,1)S(1)}, bf16[8,2,1024]{2,1,0:T(2,128)(2,1)}, u32[]{:S(2)}) %copy-start) | copy-done | bytes 32792
  1.6 0.5 %collective-permute-done.1 = s32[8,512]{1,0:T(8,128)S(1)} collective-permute-done((s32[8,512]{1,0:T(8,128)S(1)}, s32[8,512]{1,0:T(8,128)S(1)}, u32[]{:S(2)}, u32[]{:S(2)}) %collective-permute-start.1) | collective-permute-done | bytes 16416 | tf_op jit(solution)/shard_map/ppermute | solution.py:168
  2.1 2.2 %collective-permute-start.3 = (s32[2,8,512]{2,1,0:T(8,128)S(1)}, s32[2,8,512]{2,1,0:T(8,128)S(1)}, u32[]{:S(2)}, u32[]{:S(2)}) collective-permute-start(s32[2,8,512]{2,1,0:T(8,128)S(1)} %pad_add_fusion.first_x), channel_id=1, source_target_pairs={{1,0},{2,1},{3,2},{0,3},{5,4},{6,5},{7,6},{4,7},{9,8},{10,9},{11,1... | collective-permute-start | bytes 98312 | tf_op jit(solution)/shard_map/ppermute | solution.py:172
  4.4 5.5 %collective-permute-start.2 = (s32[2,8,512]{2,1,0:T(8,128)S(1)}, s32[2,8,512]{2,1,0:T(8,128)S(1)}, u32[]{:S(2)}, u32[]{:S(2)}) collective-permute-start(s32[2,8,512]{2,1,0:T(8,128)S(1)} %pad_add_fusion.first_x), channel_id=1, source_target_pairs={{0,4},{4,0},{1,5},{5,1},{2,6},{6,2},{3,7},{7,3},{8,12},{12,8},{9,1... | collective-permute-start | bytes 98312 | tf_op jit(solution)/shard_map/ppermute | solution.py:169
  9.9 1.6 %collective-permute-start.7 = (s32[2,8,512]{2,1,0:T(8,128)S(1)}, s32[2,8,512]{2,1,0:T(8,128)S(1)}, u32[]{:S(2)}, u32[]{:S(2)}) collective-permute-start(s32[2,8,512]{2,1,0:T(8,128)S(1)} %pad_add_fusion.first_x), channel_id=1, source_target_pairs={{3,0},{0,1},{1,2},{2,3},{7,4},{4,5},{5,6},{6,7},{11,8},{8,9},{9,10... | collective-permute-start | bytes 98312 | tf_op jit(solution)/shard_map/ppermute | solution.py:172
  11.4 3.3 %collective-permute-start.6 = (s32[2,8,512]{2,1,0:T(8,128)S(1)}, s32[2,8,512]{2,1,0:T(8,128)S(1)}, u32[]{:S(2)}, u32[]{:S(2)}) collective-permute-start(s32[2,8,512]{2,1,0:T(8,128)S(1)} %pad_add_fusion.first_x), channel_id=1, source_target_pairs={{2,0},{3,1},{0,2},{1,3},{6,4},{7,5},{4,6},{5,7},{10,8},{11,9},{8,1... | collective-permute-start | bytes 98312 | tf_op jit(solution)/shard_map/ppermute | solution.py:172
  14.8 0.6 %filter_rows.1.tab = f32[32,1024]{1,0:T(8,128)S(1)} custom-call(bf16[16,1024]{1,0:T(8,128)(2,1)S(1)} %reshape.18.own, bf16[16,1024]{1,0:T(8,128)(2,1)S(1)} %reshape.19.other), custom_call_target="tpu_custom_call" | custom-call | tf_op jit(solution)/shard_map/filter_rows/pallas_call | solution.py:57
  15.4 0.0 collective-permute-done.3.second_x
  15.4 1.3 %near_1.1 = bf16[4,16,512]{2,1,0:T(8,128)(2,1)S(1)} custom-call(f32[32,1024]{1,0:T(8,128)S(1)} %filter_rows.1.tab, s32[2,8,512]{2,1,0:T(8,128)S(1)} %pad_add_fusion.first_x, s32[2,8,512]{2,1,0:T(8,128)S(1)} %collective-permute-done.3.second_x), custom_call_target="tpu_custom_call" | custom-call | tf_op jit(solution)/shard_map/near_1/pallas_call | solution.py:149
  16.7 0.0 collective-permute-done.2.first_x
  16.7 0.3 collective-permute-start.8
  17.0 1.8 %collective-permute-start.5 = (s32[2,8,512]{2,1,0:T(8,128)S(1)}, s32[2,8,512]{2,1,0:T(8,128)S(1)}, u32[]{:S(2)}, u32[]{:S(2)}) collective-permute-start(s32[2,8,512]{2,1,0:T(8,128)S(1)} %collective-permute-done.2.first_x), channel_id=1, source_target_pairs={{3,0},{0,1},{1,2},{2,3},{7,4},{4,5},{5,6},{6,7},{11,8},{8,9},{9,10... | collective-permute-start | bytes 98312 | tf_op jit(solution)/shard_map/ppermute | solution.py:172
  18.8 1.4 %collective-permute-start.4 = (s32[2,8,512]{2,1,0:T(8,128)S(1)}, s32[2,8,512]{2,1,0:T(8,128)S(1)}, u32[]{:S(2)}, u32[]{:S(2)}) collective-permute-start(s32[2,8,512]{2,1,0:T(8,128)S(1)} %collective-permute-done.2.first_x), channel_id=1, source_target_pairs={{2,0},{3,1},{0,2},{1,3},{6,4},{7,5},{4,6},{5,7},{10,8},{11,9},{8,1... | collective-permute-start | bytes 98312 | tf_op jit(solution)/shard_map/ppermute | solution.py:172
  20.2 0.0 collective-permute-done.7.second_x
  20.2 1.3 %near_2.1 = bf16[4,16,512]{2,1,0:T(8,128)(2,1)S(1)} custom-call(f32[32,1024]{1,0:T(8,128)S(1)} %filter_rows.1.tab, s32[2,8,512]{2,1,0:T(8,128)S(1)} %collective-permute-done.6.first_x, s32[2,8,512]{2,1,0:T(8,128)S(1)} %collective-permute-done.7.second_x), custom_call_target="tpu_custom_call" | custom-call | tf_op jit(solution)/shard_map/near_2/pallas_call | solution.py:149
  21.6 0.0 collective-permute-done.8.second_x
  21.6 1.3 %far_1.1 = bf16[4,16,512]{2,1,0:T(8,128)(2,1)S(1)} custom-call(f32[32,1024]{1,0:T(8,128)S(1)} %filter_rows.1.tab, s32[2,8,512]{2,1,0:T(8,128)S(1)} %collective-permute-done.2.first_x, s32[2,8,512]{2,1,0:T(8,128)S(1)} %collective-permute-done.8.second_x), custom_call_target="tpu_custom_call" | custom-call | tf_op jit(solution)/shard_map/far_1/pallas_call | solution.py:149
  22.9 1.4 %collective-permute-done.4.first_x = s32[2,8,512]{2,1,0:T(8,128)S(1)} collective-permute-done((s32[2,8,512]{2,1,0:T(8,128)S(1)}, s32[2,8,512]{2,1,0:T(8,128)S(1)}, u32[]{:S(2)}, u32[]{:S(2)}) %collective-permute-start.4) | collective-permute-done | bytes 32800 | tf_op jit(solution)/shard_map/ppermute | solution.py:172
  24.3 1.3 %far_2.1 = bf16[16,16,512]{2,1,0:T(8,128)(2,1)S(1)} custom-call(f32[32,1024]{1,0:T(8,128)S(1)} %filter_rows.1.tab, s32[2,8,512]{2,1,0:T(8,128)S(1)} %collective-permute-done.4.first_x, s32[2,8,512]{2,1,0:T(8,128)S(1)} %collective-permute-done.5.second_x, bf16[4,16,512]{2,1,0:T(8,128)(2,1)S(1)} %near_1.1, bf16[4,16,512]{2,1,0:T(8,128)(2,1)S(1)} %near_2.1, ...), custom_call_target="tpu_custom_call" | custom-call | tf_op jit(solution)/shard_map/far_2/pallas_call | solution.py:149
  25.6 14.9 %all_to_all.5 = bf16[16,16,512]{2,1,0:T(8,128)(2,1)S(1)} all-to-all(bf16[16,16,512]{2,1,0:T(8,128)(2,1)S(1)} %far_2.1), channel_id=1, replica_groups=mesh['y'=4,'z_lo'=4,'core'=2,'z_hi'=2,'x'=4] {'y','z_lo'}, dimensions={0} | all-to-all | bytes 524288 | tf_op jit(solution)/shard_map/all_to_all | solution.py:185
  40.5 0.6 %multiply_bitcast_fusion = f32[2,8,512]{2,1,0:T(8,128)} fusion(f32[16,512]{1,0:T(8,128)S(1)} %convert_reduce_fusion), kind=kLoop, calls=%fused_computation.2 | loop fusion | flops 8192 | bytes 65536 | tf_op jit(solution)/shard_map/mul | solution.py:187
  (11 shorter events, 0.1 us)
Async XLA Ops:
  0.8 0.8 %copy-start = (bf16[8,2,1024]{2,1,0:T(2,128)(2,1)S(1)}, bf16[8,2,1024]{2,1,0:T(2,128)(2,1)}, u32[]{:S(2)}) copy-start(bf16[8,2,1024]{2,1,0:T(2,128)(2,1)} %param.2) | copy-start | bytes 98308
  0.8 1.3 %collective-permute-start.1 = (s32[8,512]{1,0:T(8,128)S(1)}, s32[8,512]{1,0:T(8,128)S(1)}, u32[]{:S(2)}, u32[]{:S(2)}) collective-permute-start(s32[8,512]{1,0:T(8,128)S(1)} %reshape.21), channel_id=1, source_target_pairs={{0,8},{8,0},{1,9},{9,1},{2,10},{10,2},{3,11},{11,3},{4,12},{12,4},... | collective-permute-start | bytes 49160 | tf_op jit(solution)/shard_map/ppermute | solution.py:168
  1.6 13.2 %collective-permute-start = (bf16[8,2,1024]{2,1,0:T(2,128)(2,1)S(1)}, bf16[8,2,1024]{2,1,0:T(2,128)(2,1)S(1)}, u32[]{:S(2)}, u32[]{:S(2)}) collective-permute-start(bf16[8,2,1024]{2,1,0:T(2,128)(2,1)S(1)} %copy-done), channel_id=1, source_target_pairs={{0,8},{8,0},{1,9},{9,1},{2,10},{10,2},{3,11},{11,3},{4,12},{12,4},... | collective-permute-start | bytes 98312 | tf_op jit(solution)/shard_map/ppermute | solution.py:174
  2.1 13.3 %collective-permute-start.3 = (s32[2,8,512]{2,1,0:T(8,128)S(1)}, s32[2,8,512]{2,1,0:T(8,128)S(1)}, u32[]{:S(2)}, u32[]{:S(2)}) collective-permute-start(s32[2,8,512]{2,1,0:T(8,128)S(1)} %pad_add_fusion.first_x), channel_id=1, source_target_pairs={{1,0},{2,1},{3,2},{0,3},{5,4},{6,5},{7,6},{4,7},{9,8},{10,9},{11,1... | collective-permute-start | bytes 98312 | tf_op jit(solution)/shard_map/ppermute | solution.py:172
  4.4 12.4 %collective-permute-start.2 = (s32[2,8,512]{2,1,0:T(8,128)S(1)}, s32[2,8,512]{2,1,0:T(8,128)S(1)}, u32[]{:S(2)}, u32[]{:S(2)}) collective-permute-start(s32[2,8,512]{2,1,0:T(8,128)S(1)} %pad_add_fusion.first_x), channel_id=1, source_target_pairs={{0,4},{4,0},{1,5},{5,1},{2,6},{6,2},{3,7},{7,3},{8,12},{12,8},{9,1... | collective-permute-start | bytes 98312 | tf_op jit(solution)/shard_map/ppermute | solution.py:169
  9.9 10.4 %collective-permute-start.7 = (s32[2,8,512]{2,1,0:T(8,128)S(1)}, s32[2,8,512]{2,1,0:T(8,128)S(1)}, u32[]{:S(2)}, u32[]{:S(2)}) collective-permute-start(s32[2,8,512]{2,1,0:T(8,128)S(1)} %pad_add_fusion.first_x), channel_id=1, source_target_pairs={{3,0},{0,1},{1,2},{2,3},{7,4},{4,5},{5,6},{6,7},{11,8},{8,9},{9,10... | collective-permute-start | bytes 98312 | tf_op jit(solution)/shard_map/ppermute | solution.py:172
  11.4 8.8 %collective-permute-start.6 = (s32[2,8,512]{2,1,0:T(8,128)S(1)}, s32[2,8,512]{2,1,0:T(8,128)S(1)}, u32[]{:S(2)}, u32[]{:S(2)}) collective-permute-start(s32[2,8,512]{2,1,0:T(8,128)S(1)} %pad_add_fusion.first_x), channel_id=1, source_target_pairs={{2,0},{3,1},{0,2},{1,3},{6,4},{7,5},{4,6},{5,7},{10,8},{11,9},{8,1... | collective-permute-start | bytes 98312 | tf_op jit(solution)/shard_map/ppermute | solution.py:172
  16.7 4.8 %collective-permute-start.8 = (s32[2,8,512]{2,1,0:T(8,128)S(1)}, s32[2,8,512]{2,1,0:T(8,128)S(1)}, u32[]{:S(2)}, u32[]{:S(2)}) collective-permute-start(s32[2,8,512]{2,1,0:T(8,128)S(1)} %collective-permute-done.2.first_x), channel_id=1, source_target_pairs={{1,0},{2,1},{3,2},{0,3},{5,4},{6,5},{7,6},{4,7},{9,8},{10,9},{11,1... | collective-permute-start | bytes 98312 | tf_op jit(solution)/shard_map/ppermute | solution.py:172
  17.0 5.8 %collective-permute-start.5 = (s32[2,8,512]{2,1,0:T(8,128)S(1)}, s32[2,8,512]{2,1,0:T(8,128)S(1)}, u32[]{:S(2)}, u32[]{:S(2)}) collective-permute-start(s32[2,8,512]{2,1,0:T(8,128)S(1)} %collective-permute-done.2.first_x), channel_id=1, source_target_pairs={{3,0},{0,1},{1,2},{2,3},{7,4},{4,5},{5,6},{6,7},{11,8},{8,9},{9,10... | collective-permute-start | bytes 98312 | tf_op jit(solution)/shard_map/ppermute | solution.py:172
  18.8 5.4 %collective-permute-start.4 = (s32[2,8,512]{2,1,0:T(8,128)S(1)}, s32[2,8,512]{2,1,0:T(8,128)S(1)}, u32[]{:S(2)}, u32[]{:S(2)}) collective-permute-start(s32[2,8,512]{2,1,0:T(8,128)S(1)} %collective-permute-done.2.first_x), channel_id=1, source_target_pairs={{2,0},{3,1},{0,2},{1,3},{6,4},{7,5},{4,6},{5,7},{10,8},{11,9},{8,1... | collective-permute-start | bytes 98312 | tf_op jit(solution)/shard_map/ppermute | solution.py:172

commit v4 on v3

--- a/solution.py
+++ b/solution.py
@@ -145,43 +145,42 @@
     project_rows(tab, first_x, second_x, out, (far_at + places[2], far_at + places[3]))
 
 
-def project(kernel, owners, operands, name):
+def project(kernel, owners, operands):
     return pl.pallas_call(
         kernel,
         out_shape=jax.ShapeDtypeStruct((owners, 16, 512), jnp.bfloat16),
         in_specs=[VMEM] * len(operands),
         out_specs=VMEM,
         compiler_params=pltpu.CompilerParams(vmem_limit_bytes=8 * 2**20),
-        name=name,
     )(*operands)
 
 
-def shards(sinogram, detector_coord):
+def permuted(array, axis, step, size):
+    return lax.ppermute(array, axis, [((i + step) % size, i) for i in range(size)])
+
+
+def image(sinogram, detector_coord):
     slices, angles, bins = sinogram.shape
     width = detector_coord.shape[2]
     core = lax.axis_index("core")
-    swap = [(0, 1), (1, 0)]
 
     by_core = detector_coord.reshape(angles, 2, 2, 2, width)
     keep = lax.dynamic_index_in_dim(by_core, core, 2, keepdims=False).reshape(8, width)
     give = lax.dynamic_index_in_dim(by_core, 1 - core, 2, keepdims=False).reshape(8, width)
-    own = jnp.stack([keep, lax.ppermute(give, "core", swap)])
-    other = lax.ppermute(own, "z_hi", swap)
+    own = jnp.stack([keep, permuted(give, "core", 1, 2)])
+    other = permuted(own, "z_hi", 1, 2)
 
-    def from_x(array, step):
-        return lax.ppermute(array, "x", [((i + step) % 4, i) for i in range(4)])
-
-    other_sino = lax.ppermute(sinogram, "core", swap)
+    other_sino = permuted(sinogram, "core", 1, 2)
     tab = filter_rows(
         sinogram.reshape(slices * angles, bins), other_sino.reshape(slices * angles, bins)
     )
-    near = [own] + [from_x(own, s) for s in (1, 2, 3)]
-    near_1 = project(quarter_kernel, 4, [tab, *near[:2]], "near_1")
+    near = [own] + [permuted(own, "x", s, 4) for s in (1, 2, 3)]
+    near_1 = project(quarter_kernel, 4, [tab, *near[:2]])
     other, near_1 = lax.optimization_barrier((other, near_1))
-    far = [other] + [from_x(other, s) for s in (1, 2, 3)]
-    near_2 = project(quarter_kernel, 4, [tab, *near[2:]], "near_2")
-    far_1 = project(quarter_kernel, 4, [tab, *far[:2]], "far_1")
-    partial = project(last_kernel, 16, [tab, *far[2:], near_1, near_2, far_1], "far_2")
+    far = [other] + [permuted(other, "x", s, 4) for s in (1, 2, 3)]
+    near_2 = project(quarter_kernel, 4, [tab, *near[2:]])
+    far_1 = project(quarter_kernel, 4, [tab, *far[:2]])
+    partial = project(last_kernel, 16, [tab, *far[2:], near_1, near_2, far_1])
     parts = lax.all_to_all(partial, ("y", "z_lo"), 0, 0, tiled=True)
     scale = jnp.float32(math.pi / (angles * lax.axis_size(("y", "z_lo", "core"))))
     image_rows = jnp.sum(parts.astype(jnp.float32), axis=0) * scale
@@ -194,5 +193,5 @@
     ang, sl = ("y", "z_lo", "core"), ("z_hi", "x")
     in_specs = (P(sl, ang, None), P(ang, sl, None))
     return jax.shard_map(
-        shards, mesh=fine, in_specs=in_specs, out_specs=P(ang, sl, None), check_vma=False
+        image, mesh=fine, in_specs=in_specs, out_specs=P(ang, sl, None), check_vma=False
     )

time: 41.4 us -> 41.4 us (level)
  no operation moved by 1% of the time
where the time goes in v4:
time: 41.4 us; the launch traced here: 41.1 us
  starting transfers between devices  16.2 us (39%)
  blocking collectives  14.9 us (36%)
  Pallas kernels  5.83 us (14%)
  waiting for transfers between devices  1.91 us (5%)
  local copies, waits for them, and re-layouts  1.49 us (4%)
  other arithmetic  0.66 us (2%)
    ppermute x9, starting transfers between devices, permuted(): lax.ppermute(array, axis, [((i + step) % size, i) for i in range(size)])  16.2 us
    all_to_all x1, blocking collectives, image(): parts = lax.all_to_all(partial, ('y', 'z_lo'), 0, 0, tiled=True)  14.9 us
    pallas_call x4, Pallas kernels, project(): pl.pallas_call(kernel, out_shape=jax.ShapeDtypeStruct((owners, 16, 512),...  5.22 us
    ppermute x9, waiting for transfers between devices, permuted(): lax.ppermute(array, axis, [((i + step) % size, i) for i in range(size)])  1.91 us
  transfers between devices with their start and end apart: 9, of which 2 were waited for; matrix products, arithmetic and copies ran while one was open for 0% of the time, Pallas kernels for 11%

profile of v4, /device:TPU:2, one launch (start us, length us, event | category | flops | bytes accessed | tf_op | source)
XLA Modules:
  0.0 41.1 jit_solution(4682898857578505879)
XLA Ops:
  0.0 0.8 %reshape.20 = s32[2,2,2,2,512]{4,3,2,1,0:T(2,128)S(1)} reshape(s32[2,8,512]{2,1,0:T(8,128)} %param.3) | data formatting | bytes 65536 | tf_op jit(solution)/shard_map/reshape | solution.py:167
  0.8 0.0 copy-start
  0.8 0.1 collective-permute-start.1
  0.9 0.6 %copy-done = bf16[8,2,1024]{2,1,0:T(2,128)(2,1)S(1)} copy-done((bf16[8,2,1024]{2,1,0:T(2,128)(2,1)S(1)}, bf16[8,2,1024]{2,1,0:T(2,128)(2,1)}, u32[]{:S(2)}) %copy-start) | copy-done | bytes 32792
  1.6 0.0 collective-permute-start
  1.6 0.5 %collective-permute-done.1 = s32[8,512]{1,0:T(8,128)S(1)} collective-permute-done((s32[8,512]{1,0:T(8,128)S(1)}, s32[8,512]{1,0:T(8,128)S(1)}, u32[]{:S(2)}, u32[]{:S(2)}) %collective-permute-start.1) | collective-permute-done | bytes 16416 | tf_op jit(solution)/shard_map/ppermute | solution.py:159
  2.1 2.2 %collective-permute-start.3 = (s32[2,8,512]{2,1,0:T(8,128)S(1)}, s32[2,8,512]{2,1,0:T(8,128)S(1)}, u32[]{:S(2)}, u32[]{:S(2)}) collective-permute-start(s32[2,8,512]{2,1,0:T(8,128)S(1)} %pad_add_fusion.first_x), channel_id=1, source_target_pairs={{1,0},{2,1},{3,2},{0,3},{5,4},{6,5},{7,6},{4,7},{9,8},{10,9},{11,1... | collective-permute-start | bytes 98312 | tf_op jit(solution)/shard_map/ppermute | solution.py:159
  4.4 5.5 %collective-permute-start.2 = (s32[2,8,512]{2,1,0:T(8,128)S(1)}, s32[2,8,512]{2,1,0:T(8,128)S(1)}, u32[]{:S(2)}, u32[]{:S(2)}) collective-permute-start(s32[2,8,512]{2,1,0:T(8,128)S(1)} %pad_add_fusion.first_x), channel_id=1, source_target_pairs={{4,0},{0,4},{5,1},{1,5},{6,2},{2,6},{7,3},{3,7},{12,8},{8,12},{13,... | collective-permute-start | bytes 98312 | tf_op jit(solution)/shard_map/ppermute | solution.py:159
  9.9 1.6 %collective-permute-start.7 = (s32[2,8,512]{2,1,0:T(8,128)S(1)}, s32[2,8,512]{2,1,0:T(8,128)S(1)}, u32[]{:S(2)}, u32[]{:S(2)}) collective-permute-start(s32[2,8,512]{2,1,0:T(8,128)S(1)} %pad_add_fusion.first_x), channel_id=1, source_target_pairs={{3,0},{0,1},{1,2},{2,3},{7,4},{4,5},{5,6},{6,7},{11,8},{8,9},{9,10... | collective-permute-start | bytes 98312 | tf_op jit(solution)/shard_map/ppermute | solution.py:159
  11.4 3.3 %collective-permute-start.6 = (s32[2,8,512]{2,1,0:T(8,128)S(1)}, s32[2,8,512]{2,1,0:T(8,128)S(1)}, u32[]{:S(2)}, u32[]{:S(2)}) collective-permute-start(s32[2,8,512]{2,1,0:T(8,128)S(1)} %pad_add_fusion.first_x), channel_id=1, source_target_pairs={{2,0},{3,1},{0,2},{1,3},{6,4},{7,5},{4,6},{5,7},{10,8},{11,9},{8,1... | collective-permute-start | bytes 98312 | tf_op jit(solution)/shard_map/ppermute | solution.py:159
  14.8 0.6 %filter_rows.1.tab = f32[32,1024]{1,0:T(8,128)S(1)} custom-call(bf16[16,1024]{1,0:T(8,128)(2,1)S(1)} %reshape.18.own, bf16[16,1024]{1,0:T(8,128)(2,1)S(1)} %reshape.19.other), custom_call_target="tpu_custom_call" | custom-call | tf_op jit(solution)/shard_map/filter_rows/pallas_call | solution.py:57
  15.4 0.0 collective-permute-done.3.second_x
  15.4 1.3 %shard_map.28.near_1 = bf16[4,16,512]{2,1,0:T(8,128)(2,1)S(1)} custom-call(f32[32,1024]{1,0:T(8,128)S(1)} %filter_rows.1.tab, s32[2,8,512]{2,1,0:T(8,128)S(1)} %pad_add_fusion.first_x, s32[2,8,512]{2,1,0:T(8,128)S(1)} %collective-permute-done.3.second_x), custom_call_target="tpu_custom_call" | custom-call | tf_op jit(solution)/shard_map/pallas_call | solution.py:149
  16.7 0.3 collective-permute-start.8
  17.0 1.8 %collective-permute-start.5 = (s32[2,8,512]{2,1,0:T(8,128)S(1)}, s32[2,8,512]{2,1,0:T(8,128)S(1)}, u32[]{:S(2)}, u32[]{:S(2)}) collective-permute-start(s32[2,8,512]{2,1,0:T(8,128)S(1)} %collective-permute-done.2.first_x), channel_id=1, source_target_pairs={{3,0},{0,1},{1,2},{2,3},{7,4},{4,5},{5,6},{6,7},{11,8},{8,9},{9,10... | collective-permute-start | bytes 98312 | tf_op jit(solution)/shard_map/ppermute | solution.py:159
  18.8 1.4 %collective-permute-start.4 = (s32[2,8,512]{2,1,0:T(8,128)S(1)}, s32[2,8,512]{2,1,0:T(8,128)S(1)}, u32[]{:S(2)}, u32[]{:S(2)}) collective-permute-start(s32[2,8,512]{2,1,0:T(8,128)S(1)} %collective-permute-done.2.first_x), channel_id=1, source_target_pairs={{2,0},{3,1},{0,2},{1,3},{6,4},{7,5},{4,6},{5,7},{10,8},{11,9},{8,1... | collective-permute-start | bytes 98312 | tf_op jit(solution)/shard_map/ppermute | solution.py:159
  20.2 1.3 %shard_map.29.near_2 = bf16[4,16,512]{2,1,0:T(8,128)(2,1)S(1)} custom-call(f32[32,1024]{1,0:T(8,128)S(1)} %filter_rows.1.tab, s32[2,8,512]{2,1,0:T(8,128)S(1)} %collective-permute-done.6.first_x, s32[2,8,512]{2,1,0:T(8,128)S(1)} %collective-permute-done.7.second_x), custom_call_target="tpu_custom_call" | custom-call | tf_op jit(solution)/shard_map/pallas_call | solution.py:149
  21.6 0.0 collective-permute-done.8.second_x
  21.6 1.3 %shard_map.30.far_1 = bf16[4,16,512]{2,1,0:T(8,128)(2,1)S(1)} custom-call(f32[32,1024]{1,0:T(8,128)S(1)} %filter_rows.1.tab, s32[2,8,512]{2,1,0:T(8,128)S(1)} %collective-permute-done.2.first_x, s32[2,8,512]{2,1,0:T(8,128)S(1)} %collective-permute-done.8.second_x), custom_call_target="tpu_custom_call" | custom-call | tf_op jit(solution)/shard_map/pallas_call | solution.py:149
  22.9 0.0 collective-permute-done.5.second_x
  22.9 1.4 %collective-permute-done.4.first_x = s32[2,8,512]{2,1,0:T(8,128)S(1)} collective-permute-done((s32[2,8,512]{2,1,0:T(8,128)S(1)}, s32[2,8,512]{2,1,0:T(8,128)S(1)}, u32[]{:S(2)}, u32[]{:S(2)}) %collective-permute-start.4) | collective-permute-done | bytes 32800 | tf_op jit(solution)/shard_map/ppermute | solution.py:159
  24.3 1.3 %shard_map.31 = bf16[16,16,512]{2,1,0:T(8,128)(2,1)S(1)} custom-call(f32[32,1024]{1,0:T(8,128)S(1)} %filter_rows.1.tab, s32[2,8,512]{2,1,0:T(8,128)S(1)} %collective-permute-done.4.first_x, s32[2,8,512]{2,1,0:T(8,128)S(1)} %collective-permute-done.5.second_x, bf16[4,16,512]{2,1,0:T(8,128)(2,1)S(1)} %shard_map.28.near_1, ...), custom_call_target="tpu_custom_call" | custom-call | tf_op jit(solution)/shard_map/pallas_call | solution.py:149
  25.6 14.9 %all_to_all.5 = bf16[16,16,512]{2,1,0:T(8,128)(2,1)S(1)} all-to-all(bf16[16,16,512]{2,1,0:T(8,128)(2,1)S(1)} %shard_map.31), channel_id=1, replica_groups=mesh['y'=4,'z_lo'=4,'core'=2,'z_hi'=2,'x'=4] {'y','z_lo'}, dimensions={0} | all-to-all | bytes 524288 | tf_op jit(solution)/shard_map/all_to_all | solution.py:184
  40.5 0.6 %multiply_bitcast_fusion = f32[2,8,512]{2,1,0:T(8,128)} fusion(f32[16,512]{1,0:T(8,128)S(1)} %convert_reduce_fusion), kind=kLoop, calls=%fused_computation.2 | loop fusion | flops 8192 | bytes 65536 | tf_op jit(solution)/shard_map/mul | solution.py:186
  (11 shorter events, 0.1 us)
Async XLA Ops:
  0.8 0.8 %copy-start = (bf16[8,2,1024]{2,1,0:T(2,128)(2,1)S(1)}, bf16[8,2,1024]{2,1,0:T(2,128)(2,1)}, u32[]{:S(2)}) copy-start(bf16[8,2,1024]{2,1,0:T(2,128)(2,1)} %param.2) | copy-start | bytes 98308
  0.8 1.3 %collective-permute-start.1 = (s32[8,512]{1,0:T(8,128)S(1)}, s32[8,512]{1,0:T(8,128)S(1)}, u32[]{:S(2)}, u32[]{:S(2)}) collective-permute-start(s32[8,512]{1,0:T(8,128)S(1)} %reshape.21), channel_id=1, source_target_pairs={{8,0},{0,8},{9,1},{1,9},{10,2},{2,10},{11,3},{3,11},{12,4},{4,12},... | collective-permute-start | bytes 49160 | tf_op jit(solution)/shard_map/ppermute | solution.py:159
  1.6 13.2 %collective-permute-start = (bf16[8,2,1024]{2,1,0:T(2,128)(2,1)S(1)}, bf16[8,2,1024]{2,1,0:T(2,128)(2,1)S(1)}, u32[]{:S(2)}, u32[]{:S(2)}) collective-permute-start(bf16[8,2,1024]{2,1,0:T(2,128)(2,1)S(1)} %copy-done), channel_id=1, source_target_pairs={{8,0},{0,8},{9,1},{1,9},{10,2},{2,10},{11,3},{3,11},{12,4},{4,12},... | collective-permute-start | bytes 98312 | tf_op jit(solution)/shard_map/ppermute | solution.py:159
  2.1 13.3 %collective-permute-start.3 = (s32[2,8,512]{2,1,0:T(8,128)S(1)}, s32[2,8,512]{2,1,0:T(8,128)S(1)}, u32[]{:S(2)}, u32[]{:S(2)}) collective-permute-start(s32[2,8,512]{2,1,0:T(8,128)S(1)} %pad_add_fusion.first_x), channel_id=1, source_target_pairs={{1,0},{2,1},{3,2},{0,3},{5,4},{6,5},{7,6},{4,7},{9,8},{10,9},{11,1... | collective-permute-start | bytes 98312 | tf_op jit(solution)/shard_map/ppermute | solution.py:159
  4.4 12.4 %collective-permute-start.2 = (s32[2,8,512]{2,1,0:T(8,128)S(1)}, s32[2,8,512]{2,1,0:T(8,128)S(1)}, u32[]{:S(2)}, u32[]{:S(2)}) collective-permute-start(s32[2,8,512]{2,1,0:T(8,128)S(1)} %pad_add_fusion.first_x), channel_id=1, source_target_pairs={{4,0},{0,4},{5,1},{1,5},{6,2},{2,6},{7,3},{3,7},{12,8},{8,12},{13,... | collective-permute-start | bytes 98312 | tf_op jit(solution)/shard_map/ppermute | solution.py:159
  9.9 10.4 %collective-permute-start.7 = (s32[2,8,512]{2,1,0:T(8,128)S(1)}, s32[2,8,512]{2,1,0:T(8,128)S(1)}, u32[]{:S(2)}, u32[]{:S(2)}) collective-permute-start(s32[2,8,512]{2,1,0:T(8,128)S(1)} %pad_add_fusion.first_x), channel_id=1, source_target_pairs={{3,0},{0,1},{1,2},{2,3},{7,4},{4,5},{5,6},{6,7},{11,8},{8,9},{9,10... | collective-permute-start | bytes 98312 | tf_op jit(solution)/shard_map/ppermute | solution.py:159
  11.4 8.8 %collective-permute-start.6 = (s32[2,8,512]{2,1,0:T(8,128)S(1)}, s32[2,8,512]{2,1,0:T(8,128)S(1)}, u32[]{:S(2)}, u32[]{:S(2)}) collective-permute-start(s32[2,8,512]{2,1,0:T(8,128)S(1)} %pad_add_fusion.first_x), channel_id=1, source_target_pairs={{2,0},{3,1},{0,2},{1,3},{6,4},{7,5},{4,6},{5,7},{10,8},{11,9},{8,1... | collective-permute-start | bytes 98312 | tf_op jit(solution)/shard_map/ppermute | solution.py:159
  16.7 4.8 %collective-permute-start.8 = (s32[2,8,512]{2,1,0:T(8,128)S(1)}, s32[2,8,512]{2,1,0:T(8,128)S(1)}, u32[]{:S(2)}, u32[]{:S(2)}) collective-permute-start(s32[2,8,512]{2,1,0:T(8,128)S(1)} %collective-permute-done.2.first_x), channel_id=1, source_target_pairs={{1,0},{2,1},{3,2},{0,3},{5,4},{6,5},{7,6},{4,7},{9,8},{10,9},{11,1... | collective-permute-start | bytes 98312 | tf_op jit(solution)/shard_map/ppermute | solution.py:159
  17.0 5.8 %collective-permute-start.5 = (s32[2,8,512]{2,1,0:T(8,128)S(1)}, s32[2,8,512]{2,1,0:T(8,128)S(1)}, u32[]{:S(2)}, u32[]{:S(2)}) collective-permute-start(s32[2,8,512]{2,1,0:T(8,128)S(1)} %collective-permute-done.2.first_x), channel_id=1, source_target_pairs={{3,0},{0,1},{1,2},{2,3},{7,4},{4,5},{5,6},{6,7},{11,8},{8,9},{9,10... | collective-permute-start | bytes 98312 | tf_op jit(solution)/shard_map/ppermute | solution.py:159
  18.8 5.4 %collective-permute-start.4 = (s32[2,8,512]{2,1,0:T(8,128)S(1)}, s32[2,8,512]{2,1,0:T(8,128)S(1)}, u32[]{:S(2)}, u32[]{:S(2)}) collective-permute-start(s32[2,8,512]{2,1,0:T(8,128)S(1)} %collective-permute-done.2.first_x), channel_id=1, source_target_pairs={{2,0},{3,1},{0,2},{1,3},{6,4},{7,5},{4,6},{5,7},{10,8},{11,9},{8,1... | collective-permute-start | bytes 98312 | tf_op jit(solution)/shard_map/ppermute | solution.py:159

commit v5 on v4

--- a/solution.py
+++ b/solution.py
@@ -79,21 +79,34 @@
     return tiles
 
 
-def project_rows(tab, first_x, second_x, out, places):
+def packed(coords):
+    tiles = [coords[..., p * LANES : (p + 1) * LANES] >> 6 for p in range(4)]
+    words = [tiles[p] | ((tiles[3] >> (8 * p)) << 24) for p in range(3)]
+    return jnp.concatenate(words, axis=-1)
+
+
+def unpacked(words):
+    tiles = [words[:, p * LANES : (p + 1) * LANES] for p in range(3)]
+    top = [lax.shift_right_logical(tile, 24) for tile in tiles]
+    return [tile & 16777215 for tile in tiles] + [top[0] | (top[1] << 8) | (top[2] << 16)]
+
+
+def project_rows(tab, first_x, second_x, out, coords, places):
     sublane = lax.broadcasted_iota(jnp.int32, (8, LANES), 0)
+    for core in range(2):
+        tiles = zip(unpacked(first_x[core]), unpacked(second_x[core]))
+        for p, (first, second) in enumerate(tiles):
+            coords[p, 2 * core] = jnp.where(sublane < 4, first, pltpu.roll(second, 4, 0))
+            coords[p, 2 * core + 1] = jnp.where(sublane < 4, pltpu.roll(first, 4, 0), second)
 
     def one_tile(step):
         at = pl.ds(pl.multiple_of(step * LANES, LANES), LANES)
         sums = [None] * 8
         for core in range(2):
-            first, second = first_x[core, :, at], second_x[core, :, at]
             for angle in range(2):
-                if angle == 0:
-                    c = jnp.where(sublane < 4, first, pltpu.roll(second, 4, 0))
-                else:
-                    c = jnp.where(sublane < 4, pltpu.roll(first, 4, 0), second)
-                left = c >> 20
-                fraction = (c & 1048575).astype(jnp.float32) * jnp.float32(1.0 / 1048576.0)
+                c = coords[step, 2 * core + angle]
+                left = c >> 14
+                fraction = (c & 16383).astype(jnp.float32) * jnp.float32(1.0 / 16384.0)
                 w_left = (1.0 - fraction).astype(jnp.bfloat16).astype(jnp.float32)
                 w_right = fraction.astype(jnp.bfloat16).astype(jnp.float32)
                 bins = jnp.concatenate([left, left + 1], axis=0).astype(jnp.int16)
@@ -129,20 +142,18 @@
     lax.fori_loop(0, 2, two_tiles, 0)
 
 
-def quarter_kernel(tab, first_x, second_x, out):
-    project_rows(tab, first_x, second_x, out, (0, 2))
-
-
-def last_kernel(tab, first_x, second_x, near_1, near_2, far_1, out):
+def quarter_kernel(tab, first_x, second_x, out, coords):
+    project_rows(tab, first_x, second_x, out, coords, (0, 2))
+
+
+def last_kernel(tab, first_x, second_x, near_1, near_2, far_1, out, coords):
     x, z_high = lax.axis_index("x"), lax.axis_index("z_hi")
     near_at, far_at = 8 * z_high, 8 * (1 - z_high)
     places = [2 * ((x + step) & 3) for step in range(4)]
-    for step, part in ((0, near_1), (2, near_2)):
+    for base, part, steps in ((near_at, near_1, (0, 3)), (near_at, near_2, (2, 1)), (far_at, far_1, (0, 3))):
         for i in range(2):
-            out[pl.ds(near_at + places[step + i], 2)] = part[2 * i : 2 * i + 2]
-    for i in range(2):
-        out[pl.ds(far_at + places[i], 2)] = far_1[2 * i : 2 * i + 2]
-    project_rows(tab, first_x, second_x, out, (far_at + places[2], far_at + places[3]))
+            out[pl.ds(base + places[steps[i]], 2)] = part[2 * i : 2 * i + 2]
+    project_rows(tab, first_x, second_x, out, coords, (far_at + places[2], far_at + places[1]))
 
 
 def project(kernel, owners, operands):
@@ -151,6 +162,7 @@
         out_shape=jax.ShapeDtypeStruct((owners, 16, 512), jnp.bfloat16),
         in_specs=[VMEM] * len(operands),
         out_specs=VMEM,
+        scratch_shapes=[pltpu.VMEM((4, 4, 8, LANES), jnp.int32)],
         compiler_params=pltpu.CompilerParams(vmem_limit_bytes=8 * 2**20),
     )(*operands)
 
@@ -164,9 +176,9 @@
     width = detector_coord.shape[2]
     core = lax.axis_index("core")
 
-    by_core = detector_coord.reshape(angles, 2, 2, 2, width)
-    keep = lax.dynamic_index_in_dim(by_core, core, 2, keepdims=False).reshape(8, width)
-    give = lax.dynamic_index_in_dim(by_core, 1 - core, 2, keepdims=False).reshape(8, width)
+    words = packed(detector_coord).reshape(angles, 2, 2, 2, 3 * LANES)
+    keep = lax.dynamic_index_in_dim(words, core, 2, keepdims=False).reshape(8, 3 * LANES)
+    give = lax.dynamic_index_in_dim(words, 1 - core, 2, keepdims=False).reshape(8, 3 * LANES)
     own = jnp.stack([keep, permuted(give, "core", 1, 2)])
     other = permuted(own, "z_hi", 1, 2)
 
@@ -175,12 +187,13 @@
         sinogram.reshape(slices * angles, bins), other_sino.reshape(slices * angles, bins)
     )
     near = [own] + [permuted(own, "x", s, 4) for s in (1, 2, 3)]
-    near_1 = project(quarter_kernel, 4, [tab, *near[:2]])
+    near_1 = project(quarter_kernel, 4, [tab, near[0], near[3]])
     other, near_1 = lax.optimization_barrier((other, near_1))
     far = [other] + [permuted(other, "x", s, 4) for s in (1, 2, 3)]
-    near_2 = project(quarter_kernel, 4, [tab, *near[2:]])
-    far_1 = project(quarter_kernel, 4, [tab, *far[:2]])
-    partial = project(last_kernel, 16, [tab, *far[2:], near_1, near_2, far_1])
+    near_2 = project(quarter_kernel, 4, [tab, near[2], near[1]])
+    far_1 = project(quarter_kernel, 4, [tab, far[0], far[3]])
+    operands = [tab, far[2], far[1], near_1, near_2, far_1]
+    partial = project(last_kernel, 16, operands)
     parts = lax.all_to_all(partial, ("y", "z_lo"), 0, 0, tiled=True)
     scale = jnp.float32(math.pi / (angles * lax.axis_size(("y", "z_lo", "core"))))
     image_rows = jnp.sum(parts.astype(jnp.float32), axis=0) * scale

time: 41.4 us -> 41.4 us (level)
  the two profiles are of different devices: /device:TPU:2 before, /device:TPU:32 now
where the time goes in v5:
time: 41.4 us; the launch traced here: 41.1 us
  starting transfers between devices  15.3 us (37%)
  blocking collectives  15 us (36%)
  Pallas kernels  5.87 us (14%)
  waiting for transfers between devices  2.72 us (7%)
  other arithmetic  1.42 us (3%)
  local copies, waits for them, and re-layouts  0.71 us (2%)
    ppermute x9, starting transfers between devices, permuted(): lax.ppermute(array, axis, [((i + step) % size, i) for i in range(size)])  15.3 us
    all_to_all x1, blocking collectives, image(): parts = lax.all_to_all(partial, ('y', 'z_lo'), 0, 0, tiled=True)  15 us
    pallas_call x4, Pallas kernels, project(): pl.pallas_call(kernel, out_shape=jax.ShapeDtypeStruct((owners, 16, 512),...  5.26 us
    ppermute x9, waiting for transfers between devices, permuted(): lax.ppermute(array, axis, [((i + step) % size, i) for i in range(size)])  2.72 us
  transfers between devices with their start and end apart: 9, of which 2 were waited for; matrix products, arithmetic and copies ran while one was open for 0% of the time, Pallas kernels for 11%

profile of v5, /device:TPU:32, one launch (start us, length us, event | category | flops | bytes accessed | tf_op | source)
XLA Modules:
  0.0 41.1 jit_solution(4158409792172445772)
XLA Ops:
  0.0 0.8 %shift-left_or_fusion.2 = (s32[2,8,128]{2,1,0:T(8,128)S(1)}, s32[2,8,128]{2,1,0:T(8,128)S(1)}, s32[2,8,128]{2,1,0:T(8,128)S(1)}) fusion(s32[2,8,512]{2,1,0:T(8,128)} %param.3), kind=kLoop, calls=%fused_computation.8 | loop fusion | flops 26624 | bytes 57344 | tf_op jit(solution)/shard_map/or | solution.py:84
  0.8 0.0 copy-start
  0.8 0.1 collective-permute-start.1
  0.9 0.6 %copy-done = bf16[8,2,1024]{2,1,0:T(2,128)(2,1)S(1)} copy-done((bf16[8,2,1024]{2,1,0:T(2,128)(2,1)S(1)}, bf16[8,2,1024]{2,1,0:T(2,128)(2,1)}, u32[]{:S(2)}) %copy-start) | copy-done | bytes 32792
  1.5 0.0 collective-permute-start
  1.6 0.5 %collective-permute-done.1 = s32[8,384]{1,0:T(8,128)S(1)} collective-permute-done((s32[8,384]{1,0:T(8,128)S(1)}, s32[8,384]{1,0:T(8,128)S(1)}, u32[]{:S(2)}, u32[]{:S(2)}) %collective-permute-start.1) | collective-permute-done | bytes 12320 | tf_op jit(solution)/shard_map/ppermute | solution.py:171
  2.1 1.5 %collective-permute-start.3 = (s32[2,8,384]{2,1,0:T(8,128)S(1)}, s32[2,8,384]{2,1,0:T(8,128)S(1)}, u32[]{:S(2)}, u32[]{:S(2)}) collective-permute-start(s32[2,8,384]{2,1,0:T(8,128)S(1)} %pad_add_fusion.1.first_x), channel_id=1, source_target_pairs={{3,0},{0,1},{1,2},{2,3},{7,4},{4,5},{5,6},{6,7},{11,8},{8,9},{9,10... | collective-permute-start | bytes 73736 | tf_op jit(solution)/shard_map/ppermute | solution.py:171
  3.6 6.3 %collective-permute-start.2 = (s32[2,8,384]{2,1,0:T(8,128)S(1)}, s32[2,8,384]{2,1,0:T(8,128)S(1)}, u32[]{:S(2)}, u32[]{:S(2)}) collective-permute-start(s32[2,8,384]{2,1,0:T(8,128)S(1)} %pad_add_fusion.1.first_x), channel_id=1, source_target_pairs={{4,0},{0,4},{5,1},{1,5},{6,2},{2,6},{7,3},{3,7},{12,8},{8,12},{13,... | collective-permute-start | bytes 73736 | tf_op jit(solution)/shard_map/ppermute | solution.py:171
  9.9 1.8 %collective-permute-start.7 = (s32[2,8,384]{2,1,0:T(8,128)S(1)}, s32[2,8,384]{2,1,0:T(8,128)S(1)}, u32[]{:S(2)}, u32[]{:S(2)}) collective-permute-start(s32[2,8,384]{2,1,0:T(8,128)S(1)} %pad_add_fusion.1.first_x), channel_id=1, source_target_pairs={{1,0},{2,1},{3,2},{0,3},{5,4},{6,5},{7,6},{4,7},{9,8},{10,9},{11,1... | collective-permute-start | bytes 73736 | tf_op jit(solution)/shard_map/ppermute | solution.py:171
  11.7 1.8 %collective-permute-start.6 = (s32[2,8,384]{2,1,0:T(8,128)S(1)}, s32[2,8,384]{2,1,0:T(8,128)S(1)}, u32[]{:S(2)}, u32[]{:S(2)}) collective-permute-start(s32[2,8,384]{2,1,0:T(8,128)S(1)} %pad_add_fusion.1.first_x), channel_id=1, source_target_pairs={{2,0},{3,1},{0,2},{1,3},{6,4},{7,5},{4,6},{5,7},{10,8},{11,9},{8,1... | collective-permute-start | bytes 73736 | tf_op jit(solution)/shard_map/ppermute | solution.py:171
  13.5 0.0 collective-permute-done
  13.6 0.6 %filter_rows.1.tab = f32[32,1024]{1,0:T(8,128)S(1)} custom-call(bf16[16,1024]{1,0:T(8,128)(2,1)S(1)} %reshape.18.own, bf16[16,1024]{1,0:T(8,128)(2,1)S(1)} %reshape.19.other), custom_call_target="tpu_custom_call" | custom-call | tf_op jit(solution)/shard_map/filter_rows/pallas_call | solution.py:57
  14.2 1.3 %shard_map.28.near_1 = bf16[4,16,512]{2,1,0:T(8,128)(2,1)S(1)} custom-call(f32[32,1024]{1,0:T(8,128)S(1)} %filter_rows.1.tab, s32[2,8,384]{2,1,0:T(8,128)S(1)} %pad_add_fusion.1.first_x, s32[2,8,384]{2,1,0:T(8,128)S(1)} %collective-permute-done.3.second_x), custom_call_target="tpu_custom_call" | custom-call | tf_op jit(solution)/shard_map/pallas_call | solution.py:160
  15.5 0.7 %collective-permute-start.8 = (s32[2,8,384]{2,1,0:T(8,128)S(1)}, s32[2,8,384]{2,1,0:T(8,128)S(1)}, u32[]{:S(2)}, u32[]{:S(2)}) collective-permute-start(s32[2,8,384]{2,1,0:T(8,128)S(1)} %collective-permute-done.2.first_x), channel_id=1, source_target_pairs={{3,0},{0,1},{1,2},{2,3},{7,4},{4,5},{5,6},{6,7},{11,8},{8,9},{9,10... | collective-permute-start | bytes 73736 | tf_op jit(solution)/shard_map/ppermute | solution.py:171
  16.2 2.6 %collective-permute-start.5 = (s32[2,8,384]{2,1,0:T(8,128)S(1)}, s32[2,8,384]{2,1,0:T(8,128)S(1)}, u32[]{:S(2)}, u32[]{:S(2)}) collective-permute-start(s32[2,8,384]{2,1,0:T(8,128)S(1)} %collective-permute-done.2.first_x), channel_id=1, source_target_pairs={{1,0},{2,1},{3,2},{0,3},{5,4},{6,5},{7,6},{4,7},{9,8},{10,9},{11,1... | collective-permute-start | bytes 73736 | tf_op jit(solution)/shard_map/ppermute | solution.py:171
  18.8 0.5 %collective-permute-start.4 = (s32[2,8,384]{2,1,0:T(8,128)S(1)}, s32[2,8,384]{2,1,0:T(8,128)S(1)}, u32[]{:S(2)}, u32[]{:S(2)}) collective-permute-start(s32[2,8,384]{2,1,0:T(8,128)S(1)} %collective-permute-done.2.first_x), channel_id=1, source_target_pairs={{2,0},{3,1},{0,2},{1,3},{6,4},{7,5},{4,6},{5,7},{10,8},{11,9},{8,1... | collective-permute-start | bytes 73736 | tf_op jit(solution)/shard_map/ppermute | solution.py:171
  19.3 0.0 collective-permute-done.7.second_x
  19.4 0.0 collective-permute-done.6.first_x
  19.4 1.3 %shard_map.29.near_2 = bf16[4,16,512]{2,1,0:T(8,128)(2,1)S(1)} custom-call(f32[32,1024]{1,0:T(8,128)S(1)} %filter_rows.1.tab, s32[2,8,384]{2,1,0:T(8,128)S(1)} %collective-permute-done.6.first_x, s32[2,8,384]{2,1,0:T(8,128)S(1)} %collective-permute-done.7.second_x), custom_call_target="tpu_custom_call" | custom-call | tf_op jit(solution)/shard_map/pallas_call | solution.py:160
  20.7 1.3 %shard_map.30.far_1 = bf16[4,16,512]{2,1,0:T(8,128)(2,1)S(1)} custom-call(f32[32,1024]{1,0:T(8,128)S(1)} %filter_rows.1.tab, s32[2,8,384]{2,1,0:T(8,128)S(1)} %collective-permute-done.2.first_x, s32[2,8,384]{2,1,0:T(8,128)S(1)} %collective-permute-done.8.second_x), custom_call_target="tpu_custom_call" | custom-call | tf_op jit(solution)/shard_map/pallas_call | solution.py:160
  22.0 2.2 %collective-permute-done.4.first_x = s32[2,8,384]{2,1,0:T(8,128)S(1)} collective-permute-done((s32[2,8,384]{2,1,0:T(8,128)S(1)}, s32[2,8,384]{2,1,0:T(8,128)S(1)}, u32[]{:S(2)}, u32[]{:S(2)}) %collective-permute-start.4) | collective-permute-done | bytes 24608 | tf_op jit(solution)/shard_map/ppermute | solution.py:171
  24.2 1.3 %shard_map.31 = bf16[16,16,512]{2,1,0:T(8,128)(2,1)S(1)} custom-call(f32[32,1024]{1,0:T(8,128)S(1)} %filter_rows.1.tab, s32[2,8,384]{2,1,0:T(8,128)S(1)} %collective-permute-done.4.first_x, s32[2,8,384]{2,1,0:T(8,128)S(1)} %collective-permute-done.5.second_x, bf16[4,16,512]{2,1,0:T(8,128)(2,1)S(1)} %shard_map.28.near_1, ...), custom_call_target="tpu_custom_call" | custom-call | tf_op jit(solution)/shard_map/pallas_call | solution.py:160
  25.5 15.0 %all_to_all.5 = bf16[16,16,512]{2,1,0:T(8,128)(2,1)S(1)} all-to-all(bf16[16,16,512]{2,1,0:T(8,128)(2,1)S(1)} %shard_map.31), channel_id=1, replica_groups=mesh['y'=4,'z_lo'=4,'core'=2,'z_hi'=2,'x'=4] {'y','z_lo'}, dimensions={0} | all-to-all | bytes 524288 | tf_op jit(solution)/shard_map/all_to_all | solution.py:197
  40.5 0.6 %multiply_bitcast_fusion = f32[2,8,512]{2,1,0:T(8,128)} fusion(f32[16,512]{1,0:T(8,128)S(1)} %convert_reduce_fusion), kind=kLoop, calls=%fused_computation.1 | loop fusion | flops 8192 | bytes 65536 | tf_op jit(solution)/shard_map/mul | solution.py:199
  (13 shorter events, 0.2 us)
Async XLA Ops:
  0.8 0.8 %copy-start = (bf16[8,2,1024]{2,1,0:T(2,128)(2,1)S(1)}, bf16[8,2,1024]{2,1,0:T(2,128)(2,1)}, u32[]{:S(2)}) copy-start(bf16[8,2,1024]{2,1,0:T(2,128)(2,1)} %param.2) | copy-start | bytes 98308
  0.8 1.3 %collective-permute-start.1 = (s32[8,384]{1,0:T(8,128)S(1)}, s32[8,384]{1,0:T(8,128)S(1)}, u32[]{:S(2)}, u32[]{:S(2)}) collective-permute-start(s32[8,384]{1,0:T(8,128)S(1)} %reshape.21), channel_id=1, source_target_pairs={{8,0},{0,8},{9,1},{1,9},{10,2},{2,10},{11,3},{3,11},{12,4},{4,12},... | collective-permute-start | bytes 36872 | tf_op jit(solution)/shard_map/ppermute | solution.py:171
  1.5 12.0 %collective-permute-start = (bf16[8,2,1024]{2,1,0:T(2,128)(2,1)S(1)}, bf16[8,2,1024]{2,1,0:T(2,128)(2,1)S(1)}, u32[]{:S(2)}, u32[]{:S(2)}) collective-permute-start(bf16[8,2,1024]{2,1,0:T(2,128)(2,1)S(1)} %copy-done), channel_id=1, source_target_pairs={{8,0},{0,8},{9,1},{1,9},{10,2},{2,10},{11,3},{3,11},{12,4},{4,12},... | collective-permute-start | bytes 98312 | tf_op jit(solution)/shard_map/ppermute | solution.py:171
  2.1 12.1 %collective-permute-start.3 = (s32[2,8,384]{2,1,0:T(8,128)S(1)}, s32[2,8,384]{2,1,0:T(8,128)S(1)}, u32[]{:S(2)}, u32[]{:S(2)}) collective-permute-start(s32[2,8,384]{2,1,0:T(8,128)S(1)} %pad_add_fusion.1.first_x), channel_id=1, source_target_pairs={{3,0},{0,1},{1,2},{2,3},{7,4},{4,5},{5,6},{6,7},{11,8},{8,9},{9,10... | collective-permute-start | bytes 73736 | tf_op jit(solution)/shard_map/ppermute | solution.py:171
  3.6 11.9 %collective-permute-start.2 = (s32[2,8,384]{2,1,0:T(8,128)S(1)}, s32[2,8,384]{2,1,0:T(8,128)S(1)}, u32[]{:S(2)}, u32[]{:S(2)}) collective-permute-start(s32[2,8,384]{2,1,0:T(8,128)S(1)} %pad_add_fusion.1.first_x), channel_id=1, source_target_pairs={{4,0},{0,4},{5,1},{1,5},{6,2},{2,6},{7,3},{3,7},{12,8},{8,12},{13,... | collective-permute-start | bytes 73736 | tf_op jit(solution)/shard_map/ppermute | solution.py:171
  9.9 9.4 %collective-permute-start.7 = (s32[2,8,384]{2,1,0:T(8,128)S(1)}, s32[2,8,384]{2,1,0:T(8,128)S(1)}, u32[]{:S(2)}, u32[]{:S(2)}) collective-permute-start(s32[2,8,384]{2,1,0:T(8,128)S(1)} %pad_add_fusion.1.first_x), channel_id=1, source_target_pairs={{1,0},{2,1},{3,2},{0,3},{5,4},{6,5},{7,6},{4,7},{9,8},{10,9},{11,1... | collective-permute-start | bytes 73736 | tf_op jit(solution)/shard_map/ppermute | solution.py:171
  11.7 7.6 %collective-permute-start.6 = (s32[2,8,384]{2,1,0:T(8,128)S(1)}, s32[2,8,384]{2,1,0:T(8,128)S(1)}, u32[]{:S(2)}, u32[]{:S(2)}) collective-permute-start(s32[2,8,384]{2,1,0:T(8,128)S(1)} %pad_add_fusion.1.first_x), channel_id=1, source_target_pairs={{2,0},{3,1},{0,2},{1,3},{6,4},{7,5},{4,6},{5,7},{10,8},{11,9},{8,1... | collective-permute-start | bytes 73736 | tf_op jit(solution)/shard_map/ppermute | solution.py:171
  15.5 5.1 %collective-permute-start.8 = (s32[2,8,384]{2,1,0:T(8,128)S(1)}, s32[2,8,384]{2,1,0:T(8,128)S(1)}, u32[]{:S(2)}, u32[]{:S(2)}) collective-permute-start(s32[2,8,384]{2,1,0:T(8,128)S(1)} %collective-permute-done.2.first_x), channel_id=1, source_target_pairs={{3,0},{0,1},{1,2},{2,3},{7,4},{4,5},{5,6},{6,7},{11,8},{8,9},{9,10... | collective-permute-start | bytes 73736 | tf_op jit(solution)/shard_map/ppermute | solution.py:171
  16.2 5.8 %collective-permute-start.5 = (s32[2,8,384]{2,1,0:T(8,128)S(1)}, s32[2,8,384]{2,1,0:T(8,128)S(1)}, u32[]{:S(2)}, u32[]{:S(2)}) collective-permute-start(s32[2,8,384]{2,1,0:T(8,128)S(1)} %collective-permute-done.2.first_x), channel_id=1, source_target_pairs={{1,0},{2,1},{3,2},{0,3},{5,4},{6,5},{7,6},{4,7},{9,8},{10,9},{11,1... | collective-permute-start | bytes 73736 | tf_op jit(solution)/shard_map/ppermute | solution.py:171
  18.8 5.3 %collective-permute-start.4 = (s32[2,8,384]{2,1,0:T(8,128)S(1)}, s32[2,8,384]{2,1,0:T(8,128)S(1)}, u32[]{:S(2)}, u32[]{:S(2)}) collective-permute-start(s32[2,8,384]{2,1,0:T(8,128)S(1)} %collective-permute-done.2.first_x), channel_id=1, source_target_pairs={{2,0},{3,1},{0,2},{1,3},{6,4},{7,5},{4,6},{5,7},{10,8},{11,9},{8,1... | collective-permute-start | bytes 73736 | tf_op jit(solution)/shard_map/ppermute | solution.py:171

commit v6 on v5

--- a/solution.py
+++ b/solution.py
@@ -91,69 +91,60 @@
     return [tile & 16777215 for tile in tiles] + [top[0] | (top[1] << 8) | (top[2] << 16)]
 
 
-def project_rows(tab, first_x, second_x, out, coords, places):
+def project_rows(tab, words, out, place):
     sublane = lax.broadcasted_iota(jnp.int32, (8, LANES), 0)
-    for core in range(2):
-        tiles = zip(unpacked(first_x[core]), unpacked(second_x[core]))
-        for p, (first, second) in enumerate(tiles):
-            coords[p, 2 * core] = jnp.where(sublane < 4, first, pltpu.roll(second, 4, 0))
-            coords[p, 2 * core + 1] = jnp.where(sublane < 4, pltpu.roll(first, 4, 0), second)
-
-    def one_tile(step):
-        at = pl.ds(pl.multiple_of(step * LANES, LANES), LANES)
+    tiles = [unpacked(words[core]) for core in range(2)]
+    for p in range(4):
         sums = [None] * 8
         for core in range(2):
-            for angle in range(2):
-                c = coords[step, 2 * core + angle]
-                left = c >> 14
-                fraction = (c & 16383).astype(jnp.float32) * jnp.float32(1.0 / 16384.0)
-                w_left = (1.0 - fraction).astype(jnp.bfloat16).astype(jnp.float32)
-                w_right = fraction.astype(jnp.bfloat16).astype(jnp.float32)
-                bins = jnp.concatenate([left, left + 1], axis=0).astype(jnp.int16)
-                lanes = bins & jnp.int16(LANES - 1)
-                high = [(bins & jnp.int16(bit)) != 0 for bit in (128, 256, 512)]
-                for s in range(8):
-                    row = core * 16 + s * 2 + angle
-                    taps = []
-                    for k in range(8):
-                        source = jnp.broadcast_to(
-                            tab[row : row + 1, k * LANES : (k + 1) * LANES], (16, LANES)
-                        )
-                        taps.append(lane_gather(source.astype(jnp.bfloat16), lanes))
-                    for mask in high:
-                        taps = [
-                            jnp.where(mask, taps[k + 1], taps[k]) for k in range(0, len(taps), 2)
-                        ]
-                    both = taps[0].astype(jnp.float32)
-                    part = both[:8] * w_left + both[8:] * w_right
-                    sums[s] = part if sums[s] is None else sums[s] + part
-        rows = transposed(sums)
-        for i in range(2):
-            for pair in range(2):
-                for r in range(2):
-                    value = rows[i * 4 + pair * 2 + r].astype(out.dtype)
-                    out[places[i] + pair, r * 8 : (r + 1) * 8, at] = value
-
-    def two_tiles(step, carry):
-        one_tile(2 * step)
-        one_tile(2 * step + 1)
-        return carry
-
-    lax.fori_loop(0, 2, two_tiles, 0)
+            c = tiles[core][p]
+            left = c >> 14
+            fraction = (c & 16383).astype(jnp.float32) * jnp.float32(1.0 / 16384.0)
+            w_left = (1.0 - fraction).astype(jnp.bfloat16).astype(jnp.float32)
+            w_right = fraction.astype(jnp.bfloat16).astype(jnp.float32)
+            bins = jnp.concatenate([left, left + 1], axis=0).astype(jnp.int16)
+            lanes = bins & jnp.int16(LANES - 1)
+            high = [(bins & jnp.int16(bit)) != 0 for bit in (128, 256, 512)]
+            for s in range(8):
+                row = core * 16 + s * 2
+                taps = []
+                for k in range(8):
+                    at = slice(k * LANES, (k + 1) * LANES)
+                    source = jnp.where(
+                        sublane < 4,
+                        jnp.broadcast_to(tab[row : row + 1, at], (8, LANES)),
+                        jnp.broadcast_to(tab[row + 1 : row + 2, at], (8, LANES)),
+                    )
+                    source = jnp.concatenate([source, source], axis=0).astype(jnp.bfloat16)
+                    taps.append(lane_gather(source, lanes))
+                for mask in high:
+                    taps = [jnp.where(mask, taps[k + 1], taps[k]) for k in range(0, len(taps), 2)]
+                both = taps[0].astype(jnp.float32)
+                part = both[:8] * w_left + both[8:] * w_right
+                sums[s] = part if sums[s] is None else sums[s] + part
+        rows = transposed([total + pltpu.roll(total, 4, 0) for total in sums])
+        for pair in range(2):
+            for r in range(2):
+                value = rows[pair * 2 + r].astype(out.dtype)
+                out[place + pair, r * 8 : (r + 1) * 8, p * LANES : (p + 1) * LANES] = value
 
 
-def quarter_kernel(tab, first_x, second_x, out, coords):
-    project_rows(tab, first_x, second_x, out, coords, (0, 2))
+def array_kernel(tab, words, out):
+    project_rows(tab, words, out, 0)
 
 
-def last_kernel(tab, first_x, second_x, near_1, near_2, far_1, out, coords):
+ORDER = ((0, 0), (0, 3), (0, 2), (0, 1), (1, 0), (1, 3), (1, 2), (1, 1))
+
+
+def last_kernel(tab, words, *refs):
+    parts, out = refs[:-1], refs[-1]
     x, z_high = lax.axis_index("x"), lax.axis_index("z_hi")
-    near_at, far_at = 8 * z_high, 8 * (1 - z_high)
-    places = [2 * ((x + step) & 3) for step in range(4)]
-    for base, part, steps in ((near_at, near_1, (0, 3)), (near_at, near_2, (2, 1)), (far_at, far_1, (0, 3))):
-        for i in range(2):
-            out[pl.ds(base + places[steps[i]], 2)] = part[2 * i : 2 * i + 2]
-    project_rows(tab, first_x, second_x, out, coords, (far_at + places[2], far_at + places[1]))
+    places = [
+        8 * (1 - z_high if far else z_high) + 2 * ((x + step) & 3) for far, step in ORDER
+    ]
+    for place, part in zip(places, parts):
+        out[pl.ds(place, 2)] = part[...]
+    project_rows(tab, words, out, places[-1])
 
 
 def project(kernel, owners, operands):
@@ -162,7 +153,6 @@
         out_shape=jax.ShapeDtypeStruct((owners, 16, 512), jnp.bfloat16),
         in_specs=[VMEM] * len(operands),
         out_specs=VMEM,
-        scratch_shapes=[pltpu.VMEM((4, 4, 8, LANES), jnp.int32)],
         compiler_params=pltpu.CompilerParams(vmem_limit_bytes=8 * 2**20),
     )(*operands)
 
@@ -187,13 +177,12 @@
         sinogram.reshape(slices * angles, bins), other_sino.reshape(slices * angles, bins)
     )
     near = [own] + [permuted(own, "x", s, 4) for s in (1, 2, 3)]
-    near_1 = project(quarter_kernel, 4, [tab, near[0], near[3]])
-    other, near_1 = lax.optimization_barrier((other, near_1))
+    done = [project(array_kernel, 2, [tab, near[s]]) for s in (0, 3, 2)]
+    other, *done = lax.optimization_barrier((other, *done))
     far = [other] + [permuted(other, "x", s, 4) for s in (1, 2, 3)]
-    near_2 = project(quarter_kernel, 4, [tab, near[2], near[1]])
-    far_1 = project(quarter_kernel, 4, [tab, far[0], far[3]])
-    operands = [tab, far[2], far[1], near_1, near_2, far_1]
-    partial = project(last_kernel, 16, operands)
+    done.append(project(array_kernel, 2, [tab, near[1]]))
+    done += [project(array_kernel, 2, [tab, far[s]]) for s in (0, 3, 2)]
+    partial = project(last_kernel, 16, [tab, far[1], *done])
     parts = lax.all_to_all(partial, ("y", "z_lo"), 0, 0, tiled=True)
     scale = jnp.float32(math.pi / (angles * lax.axis_size(("y", "z_lo", "core"))))
     image_rows = jnp.sum(parts.astype(jnp.float32), axis=0) * scale

time: 41.4 us -> 40.7 us (0.983)
  the two profiles are of different devices: /device:TPU:32 before, /device:TPU:2 now
where the time goes in v6:
time: 40.7 us; the launch traced here: 40.4 us
  starting transfers between devices  15.7 us (39%)
  blocking collectives  14.9 us (37%)
  Pallas kernels  5.81 us (14%)
  waiting for transfers between devices  1.74 us (4%)
  other arithmetic  1.42 us (3%)
  local copies, waits for them, and re-layouts  0.71 us (2%)
    ppermute x9, starting transfers between devices, permuted(): lax.ppermute(array, axis, [((i + step) % size, i) for i in range(size)])  15.7 us
    all_to_all x1, blocking collectives, image(): parts = lax.all_to_all(partial, ('y', 'z_lo'), 0, 0, tiled=True)  14.9 us
    pallas_call x8, Pallas kernels, project(): pl.pallas_call(kernel, out_shape=jax.ShapeDtypeStruct((owners, 16, 512),...  5.2 us
    ppermute x9, waiting for transfers between devices, permuted(): lax.ppermute(array, axis, [((i + step) % size, i) for i in range(size)])  1.74 us
  transfers between devices with their start and end apart: 9, of which 3 were waited for; matrix products, arithmetic and copies ran while one was open for 0% of the time, Pallas kernels for 13%

profile of v6, /device:TPU:2, one launch (start us, length us, event | category | flops | bytes accessed | tf_op | source)
XLA Modules:
  0.0 40.4 jit_solution(13112276783874222289)
XLA Ops:
  0.0 0.8 %shift-left_or_fusion.2 = (s32[2,8,128]{2,1,0:T(8,128)S(1)}, s32[2,8,128]{2,1,0:T(8,128)S(1)}, s32[2,8,128]{2,1,0:T(8,128)S(1)}) fusion(s32[2,8,512]{2,1,0:T(8,128)} %param.3), kind=kLoop, calls=%fused_computation.8 | loop fusion | flops 26624 | bytes 57344 | tf_op jit(solution)/shard_map/or | solution.py:84
  0.8 0.0 copy-start
  0.8 0.1 collective-permute-start.1
  0.9 0.6 %copy-done = bf16[8,2,1024]{2,1,0:T(2,128)(2,1)S(1)} copy-done((bf16[8,2,1024]{2,1,0:T(2,128)(2,1)S(1)}, bf16[8,2,1024]{2,1,0:T(2,128)(2,1)}, u32[]{:S(2)}) %copy-start) | copy-done | bytes 32792
  1.6 0.5 %collective-permute-done.1 = s32[8,384]{1,0:T(8,128)S(1)} collective-permute-done((s32[8,384]{1,0:T(8,128)S(1)}, s32[8,384]{1,0:T(8,128)S(1)}, u32[]{:S(2)}, u32[]{:S(2)}) %collective-permute-start.1) | collective-permute-done | bytes 12320 | tf_op jit(solution)/shard_map/ppermute | solution.py:161
  2.1 2.1 %collective-permute-start.4 = (s32[2,8,384]{2,1,0:T(8,128)S(1)}, s32[2,8,384]{2,1,0:T(8,128)S(1)}, u32[]{:S(2)}, u32[]{:S(2)}) collective-permute-start(s32[2,8,384]{2,1,0:T(8,128)S(1)} %pad_add_fusion.1.words), channel_id=1, source_target_pairs={{2,0},{3,1},{0,2},{1,3},{6,4},{7,5},{4,6},{5,7},{10,8},{11,9},{8,1... | collective-permute-start | bytes 73736 | tf_op jit(solution)/shard_map/ppermute | solution.py:161
  4.2 1.6 %collective-permute-start.3 = (s32[2,8,384]{2,1,0:T(8,128)S(1)}, s32[2,8,384]{2,1,0:T(8,128)S(1)}, u32[]{:S(2)}, u32[]{:S(2)}) collective-permute-start(s32[2,8,384]{2,1,0:T(8,128)S(1)} %pad_add_fusion.1.words), channel_id=1, source_target_pairs={{3,0},{0,1},{1,2},{2,3},{7,4},{4,5},{5,6},{6,7},{11,8},{8,9},{9,10... | collective-permute-start | bytes 73736 | tf_op jit(solution)/shard_map/ppermute | solution.py:161
  5.8 5.6 %collective-permute-start.2 = (s32[2,8,384]{2,1,0:T(8,128)S(1)}, s32[2,8,384]{2,1,0:T(8,128)S(1)}, u32[]{:S(2)}, u32[]{:S(2)}) collective-permute-start(s32[2,8,384]{2,1,0:T(8,128)S(1)} %pad_add_fusion.1.words), channel_id=1, source_target_pairs={{4,0},{0,4},{5,1},{1,5},{6,2},{2,6},{7,3},{3,7},{12,8},{8,12},{13,... | collective-permute-start | bytes 73736 | tf_op jit(solution)/shard_map/ppermute | solution.py:161
  11.4 2.1 %collective-permute-start.6 = (s32[2,8,384]{2,1,0:T(8,128)S(1)}, s32[2,8,384]{2,1,0:T(8,128)S(1)}, u32[]{:S(2)}, u32[]{:S(2)}) collective-permute-start(s32[2,8,384]{2,1,0:T(8,128)S(1)} %pad_add_fusion.1.words), channel_id=1, source_target_pairs={{1,0},{2,1},{3,2},{0,3},{5,4},{6,5},{7,6},{4,7},{9,8},{10,9},{11,1... | collective-permute-start | bytes 73736 | tf_op jit(solution)/shard_map/ppermute | solution.py:161
  13.6 0.6 %filter_rows.1.tab = f32[32,1024]{1,0:T(8,128)S(1)} custom-call(bf16[16,1024]{1,0:T(8,128)(2,1)S(1)} %reshape.18.own, bf16[16,1024]{1,0:T(8,128)(2,1)S(1)} %reshape.19.other), custom_call_target="tpu_custom_call" | custom-call | tf_op jit(solution)/shard_map/filter_rows/pallas_call | solution.py:57
  14.2 0.7 %shard_map.28.refs_0_ = bf16[2,16,512]{2,1,0:T(8,128)(2,1)S(1)} custom-call(f32[32,1024]{1,0:T(8,128)S(1)} %filter_rows.1.tab, s32[2,8,384]{2,1,0:T(8,128)S(1)} %pad_add_fusion.1.words), custom_call_target="tpu_custom_call" | custom-call | tf_op jit(solution)/shard_map/pallas_call | solution.py:151
  14.9 0.7 %shard_map.30.refs_2_ = bf16[2,16,512]{2,1,0:T(8,128)(2,1)S(1)} custom-call(f32[32,1024]{1,0:T(8,128)S(1)} %filter_rows.1.tab, s32[2,8,384]{2,1,0:T(8,128)S(1)} %collective-permute-done.4.words), custom_call_target="tpu_custom_call" | custom-call | tf_op jit(solution)/shard_map/pallas_call | solution.py:151
  15.5 0.7 %shard_map.29.refs_1_ = bf16[2,16,512]{2,1,0:T(8,128)(2,1)S(1)} custom-call(f32[32,1024]{1,0:T(8,128)S(1)} %filter_rows.1.tab, s32[2,8,384]{2,1,0:T(8,128)S(1)} %collective-permute-done.3.words), custom_call_target="tpu_custom_call" | custom-call | tf_op jit(solution)/shard_map/pallas_call | solution.py:151
  16.2 1.6 %collective-permute-start.8 = (s32[2,8,384]{2,1,0:T(8,128)S(1)}, s32[2,8,384]{2,1,0:T(8,128)S(1)}, u32[]{:S(2)}, u32[]{:S(2)}) collective-permute-start(s32[2,8,384]{2,1,0:T(8,128)S(1)} %collective-permute-done.2.words), channel_id=1, source_target_pairs={{2,0},{3,1},{0,2},{1,3},{6,4},{7,5},{4,6},{5,7},{10,8},{11,9},{8,1... | collective-permute-start | bytes 73736 | tf_op jit(solution)/shard_map/ppermute | solution.py:161
  17.8 2.6 %collective-permute-start.7 = (s32[2,8,384]{2,1,0:T(8,128)S(1)}, s32[2,8,384]{2,1,0:T(8,128)S(1)}, u32[]{:S(2)}, u32[]{:S(2)}) collective-permute-start(s32[2,8,384]{2,1,0:T(8,128)S(1)} %collective-permute-done.2.words), channel_id=1, source_target_pairs={{3,0},{0,1},{1,2},{2,3},{7,4},{4,5},{5,6},{6,7},{11,8},{8,9},{9,10... | collective-permute-start | bytes 73736 | tf_op jit(solution)/shard_map/ppermute | solution.py:161
  20.4 0.7 %shard_map.32.refs_4_ = bf16[2,16,512]{2,1,0:T(8,128)(2,1)S(1)} custom-call(f32[32,1024]{1,0:T(8,128)S(1)} %filter_rows.1.tab, s32[2,8,384]{2,1,0:T(8,128)S(1)} %collective-permute-done.2.words), custom_call_target="tpu_custom_call" | custom-call | tf_op jit(solution)/shard_map/pallas_call | solution.py:151
  21.0 0.7 %shard_map.31.refs_3_ = bf16[2,16,512]{2,1,0:T(8,128)(2,1)S(1)} custom-call(f32[32,1024]{1,0:T(8,128)S(1)} %filter_rows.1.tab, s32[2,8,384]{2,1,0:T(8,128)S(1)} %collective-permute-done.6.words), custom_call_target="tpu_custom_call" | custom-call | tf_op jit(solution)/shard_map/pallas_call | solution.py:151
  21.7 0.1 collective-permute-done.8.words
  21.8 0.6 %shard_map.34.refs_6_ = bf16[2,16,512]{2,1,0:T(8,128)(2,1)S(1)} custom-call(f32[32,1024]{1,0:T(8,128)S(1)} %filter_rows.1.tab, s32[2,8,384]{2,1,0:T(8,128)S(1)} %collective-permute-done.8.words), custom_call_target="tpu_custom_call" | custom-call | tf_op jit(solution)/shard_map/pallas_call | solution.py:151
  22.5 0.7 %shard_map.33.refs_5_ = bf16[2,16,512]{2,1,0:T(8,128)(2,1)S(1)} custom-call(f32[32,1024]{1,0:T(8,128)S(1)} %filter_rows.1.tab, s32[2,8,384]{2,1,0:T(8,128)S(1)} %collective-permute-done.7.words), custom_call_target="tpu_custom_call" | custom-call | tf_op jit(solution)/shard_map/pallas_call | solution.py:151
  23.1 1.1 %collective-permute-done.5.words = s32[2,8,384]{2,1,0:T(8,128)S(1)} collective-permute-done((s32[2,8,384]{2,1,0:T(8,128)S(1)}, s32[2,8,384]{2,1,0:T(8,128)S(1)}, u32[]{:S(2)}, u32[]{:S(2)}) %collective-permute-start.5) | collective-permute-done | bytes 24608 | tf_op jit(solution)/shard_map/ppermute | solution.py:161
  24.2 0.7 %shard_map.35 = bf16[16,16,512]{2,1,0:T(8,128)(2,1)S(1)} custom-call(f32[32,1024]{1,0:T(8,128)S(1)} %filter_rows.1.tab, s32[2,8,384]{2,1,0:T(8,128)S(1)} %collective-permute-done.5.words, bf16[2,16,512]{2,1,0:T(8,128)(2,1)S(1)} %shard_map.28.refs_0_, bf16[2,16,512]{2,1,0:T(8,128)(2,1)S(1)} %shard_map.29.refs_1_, bf16[2,16,512]{2,1,0:T(8,128)(2,1)S(1)} %shard_map.30.refs_2_, ...), custom_call_target="tpu_custom_call" | custom-call | tf_op jit(solution)/shard_map/pallas_call | solution.py:151
  24.9 14.9 %all_to_all.5 = bf16[16,16,512]{2,1,0:T(8,128)(2,1)S(1)} all-to-all(bf16[16,16,512]{2,1,0:T(8,128)(2,1)S(1)} %shard_map.35), channel_id=1, replica_groups=mesh['y'=4,'z_lo'=4,'core'=2,'z_hi'=2,'x'=4] {'y','z_lo'}, dimensions={0} | all-to-all | bytes 524288 | tf_op jit(solution)/shard_map/all_to_all | solution.py:186
  39.8 0.6 %multiply_bitcast_fusion = f32[2,8,512]{2,1,0:T(8,128)} fusion(f32[16,512]{1,0:T(8,128)S(1)} %convert_reduce_fusion), kind=kLoop, calls=%fused_computation.1 | loop fusion | flops 8192 | bytes 65536 | tf_op jit(solution)/shard_map/mul | solution.py:188
  (17 shorter events, 0.2 us)
Async XLA Ops:
  0.8 0.8 %copy-start = (bf16[8,2,1024]{2,1,0:T(2,128)(2,1)S(1)}, bf16[8,2,1024]{2,1,0:T(2,128)(2,1)}, u32[]{:S(2)}) copy-start(bf16[8,2,1024]{2,1,0:T(2,128)(2,1)} %param.2) | copy-start | bytes 98308
  0.8 1.3 %collective-permute-start.1 = (s32[8,384]{1,0:T(8,128)S(1)}, s32[8,384]{1,0:T(8,128)S(1)}, u32[]{:S(2)}, u32[]{:S(2)}) collective-permute-start(s32[8,384]{1,0:T(8,128)S(1)} %reshape.21), channel_id=1, source_target_pairs={{8,0},{0,8},{9,1},{1,9},{10,2},{2,10},{11,3},{3,11},{12,4},{4,12},... | collective-permute-start | bytes 36872 | tf_op jit(solution)/shard_map/ppermute | solution.py:161
  1.5 12.0 %collective-permute-start = (bf16[8,2,1024]{2,1,0:T(2,128)(2,1)S(1)}, bf16[8,2,1024]{2,1,0:T(2,128)(2,1)S(1)}, u32[]{:S(2)}, u32[]{:S(2)}) collective-permute-start(bf16[8,2,1024]{2,1,0:T(2,128)(2,1)S(1)} %copy-done), channel_id=1, source_target_pairs={{8,0},{0,8},{9,1},{1,9},{10,2},{2,10},{11,3},{3,11},{12,4},{4,12},... | collective-permute-start | bytes 98312 | tf_op jit(solution)/shard_map/ppermute | solution.py:161
  2.1 12.7 %collective-permute-start.4 = (s32[2,8,384]{2,1,0:T(8,128)S(1)}, s32[2,8,384]{2,1,0:T(8,128)S(1)}, u32[]{:S(2)}, u32[]{:S(2)}) collective-permute-start(s32[2,8,384]{2,1,0:T(8,128)S(1)} %pad_add_fusion.1.words), channel_id=1, source_target_pairs={{2,0},{3,1},{0,2},{1,3},{6,4},{7,5},{4,6},{5,7},{10,8},{11,9},{8,1... | collective-permute-start | bytes 73736 | tf_op jit(solution)/shard_map/ppermute | solution.py:161
  4.2 11.3 %collective-permute-start.3 = (s32[2,8,384]{2,1,0:T(8,128)S(1)}, s32[2,8,384]{2,1,0:T(8,128)S(1)}, u32[]{:S(2)}, u32[]{:S(2)}) collective-permute-start(s32[2,8,384]{2,1,0:T(8,128)S(1)} %pad_add_fusion.1.words), channel_id=1, source_target_pairs={{3,0},{0,1},{1,2},{2,3},{7,4},{4,5},{5,6},{6,7},{11,8},{8,9},{9,10... | collective-permute-start | bytes 73736 | tf_op jit(solution)/shard_map/ppermute | solution.py:161
  5.8 10.4 %collective-permute-start.2 = (s32[2,8,384]{2,1,0:T(8,128)S(1)}, s32[2,8,384]{2,1,0:T(8,128)S(1)}, u32[]{:S(2)}, u32[]{:S(2)}) collective-permute-start(s32[2,8,384]{2,1,0:T(8,128)S(1)} %pad_add_fusion.1.words), channel_id=1, source_target_pairs={{4,0},{0,4},{5,1},{1,5},{6,2},{2,6},{7,3},{3,7},{12,8},{8,12},{13,... | collective-permute-start | bytes 73736 | tf_op jit(solution)/shard_map/ppermute | solution.py:161
  11.4 9.6 %collective-permute-start.6 = (s32[2,8,384]{2,1,0:T(8,128)S(1)}, s32[2,8,384]{2,1,0:T(8,128)S(1)}, u32[]{:S(2)}, u32[]{:S(2)}) collective-permute-start(s32[2,8,384]{2,1,0:T(8,128)S(1)} %pad_add_fusion.1.words), channel_id=1, source_target_pairs={{1,0},{2,1},{3,2},{0,3},{5,4},{6,5},{7,6},{4,7},{9,8},{10,9},{11,1... | collective-permute-start | bytes 73736 | tf_op jit(solution)/shard_map/ppermute | solution.py:161
  16.2 5.6 %collective-permute-start.8 = (s32[2,8,384]{2,1,0:T(8,128)S(1)}, s32[2,8,384]{2,1,0:T(8,128)S(1)}, u32[]{:S(2)}, u32[]{:S(2)}) collective-permute-start(s32[2,8,384]{2,1,0:T(8,128)S(1)} %collective-permute-done.2.words), channel_id=1, source_target_pairs={{2,0},{3,1},{0,2},{1,3},{6,4},{7,5},{4,6},{5,7},{10,8},{11,9},{8,1... | collective-permute-start | bytes 73736 | tf_op jit(solution)/shard_map/ppermute | solution.py:161
  17.8 4.7 %collective-permute-start.7 = (s32[2,8,384]{2,1,0:T(8,128)S(1)}, s32[2,8,384]{2,1,0:T(8,128)S(1)}, u32[]{:S(2)}, u32[]{:S(2)}) collective-permute-start(s32[2,8,384]{2,1,0:T(8,128)S(1)} %collective-permute-done.2.words), channel_id=1, source_target_pairs={{3,0},{0,1},{1,2},{2,3},{7,4},{4,5},{5,6},{6,7},{11,8},{8,9},{9,10... | collective-permute-start | bytes 73736 | tf_op jit(solution)/shard_map/ppermute | solution.py:161
  20.4 3.8 %collective-permute-start.5 = (s32[2,8,384]{2,1,0:T(8,128)S(1)}, s32[2,8,384]{2,1,0:T(8,128)S(1)}, u32[]{:S(2)}, u32[]{:S(2)}) collective-permute-start(s32[2,8,384]{2,1,0:T(8,128)S(1)} %collective-permute-done.2.words), channel_id=1, source_target_pairs={{1,0},{2,1},{3,2},{0,3},{5,4},{6,5},{7,6},{4,7},{9,8},{10,9},{11,1... | collective-permute-start | bytes 73736 | tf_op jit(solution)/shard_map/ppermute | solution.py:161

commit v7 on v6

--- a/solution.py
+++ b/solution.py
@@ -177,10 +177,10 @@
         sinogram.reshape(slices * angles, bins), other_sino.reshape(slices * angles, bins)
     )
     near = [own] + [permuted(own, "x", s, 4) for s in (1, 2, 3)]
-    done = [project(array_kernel, 2, [tab, near[s]]) for s in (0, 3, 2)]
-    other, *done = lax.optimization_barrier((other, *done))
+    done = [project(array_kernel, 2, [tab, near[0]])]
+    other, done[0] = lax.optimization_barrier((other, done[0]))
     far = [other] + [permuted(other, "x", s, 4) for s in (1, 2, 3)]
-    done.append(project(array_kernel, 2, [tab, near[1]]))
+    done += [project(array_kernel, 2, [tab, near[s]]) for s in (3, 2, 1)]
     done += [project(array_kernel, 2, [tab, far[s]]) for s in (0, 3, 2)]
     partial = project(last_kernel, 16, [tab, far[1], *done])
     parts = lax.all_to_all(partial, ("y", "z_lo"), 0, 0, tiled=True)

time: 40.7 us -> 39.9 us (0.980); the launches traced: 40.4 us -> 39.2 us
  waiting for transfers between devices: 1.74 us -> 0.56 us
    ppermute x9, waiting for transfers between devices: 1.74 us -> 0.56 us  [permuted(): lax.ppermute(array, axis, [((i + step) % size, i) for i in range(size)])]
  transfers between devices with their start and end apart: 9 -> 9, of which waited for: 3 -> 1; matrix products, arithmetic and copies ran while one was open for 0% -> 0% of each run, Pallas kernels for 13% -> 13%
where the time goes in v7:
time: 39.9 us; the launch traced here: 39.2 us
  starting transfers between devices  15.6 us (39%)
  blocking collectives  14.9 us (37%)
  Pallas kernels  5.82 us (15%)
  other arithmetic  1.42 us (4%)
  local copies, waits for them, and re-layouts  0.71 us (2%)
  waiting for transfers between devices  0.56 us (1%)
    ppermute x9, starting transfers between devices, permuted(): lax.ppermute(array, axis, [((i + step) % size, i) for i in range(size)])  15.6 us
    all_to_all x1, blocking collectives, image(): parts = lax.all_to_all(partial, ('y', 'z_lo'), 0, 0, tiled=True)  14.9 us
    pallas_call x8, Pallas kernels, project(): pl.pallas_call(kernel, out_shape=jax.ShapeDtypeStruct((owners, 16, 512),...  5.21 us
  transfers between devices with their start and end apart: 9, of which 1 were waited for; matrix products, arithmetic and copies ran while one was open for 0% of the time, Pallas kernels for 13%

profile of v7, /device:TPU:2, one launch (start us, length us, event | category | flops | bytes accessed | tf_op | source)
XLA Modules:
  0.0 39.2 jit_solution(10382547028518084346)
XLA Ops:
  0.0 0.8 %shift-left_or_fusion.2 = (s32[2,8,128]{2,1,0:T(8,128)S(1)}, s32[2,8,128]{2,1,0:T(8,128)S(1)}, s32[2,8,128]{2,1,0:T(8,128)S(1)}) fusion(s32[2,8,512]{2,1,0:T(8,128)} %param.3), kind=kLoop, calls=%fused_computation.8 | loop fusion | flops 26624 | bytes 57344 | tf_op jit(solution)/shard_map/or | solution.py:84
  0.8 0.0 copy-start
  0.8 0.1 collective-permute-start.1
  0.9 0.6 %copy-done = bf16[8,2,1024]{2,1,0:T(2,128)(2,1)S(1)} copy-done((bf16[8,2,1024]{2,1,0:T(2,128)(2,1)S(1)}, bf16[8,2,1024]{2,1,0:T(2,128)(2,1)}, u32[]{:S(2)}) %copy-start) | copy-done | bytes 32792
  1.6 0.5 %collective-permute-done.1 = s32[8,384]{1,0:T(8,128)S(1)} collective-permute-done((s32[8,384]{1,0:T(8,128)S(1)}, s32[8,384]{1,0:T(8,128)S(1)}, u32[]{:S(2)}, u32[]{:S(2)}) %collective-permute-start.1) | collective-permute-done | bytes 12320 | tf_op jit(solution)/shard_map/ppermute | solution.py:161
  2.1 7.2 %collective-permute-start.2 = (s32[2,8,384]{2,1,0:T(8,128)S(1)}, s32[2,8,384]{2,1,0:T(8,128)S(1)}, u32[]{:S(2)}, u32[]{:S(2)}) collective-permute-start(s32[2,8,384]{2,1,0:T(8,128)S(1)} %pad_add_fusion.1.words), channel_id=1, source_target_pairs={{4,0},{0,4},{5,1},{1,5},{6,2},{2,6},{7,3},{3,7},{12,8},{8,12},{13,... | collective-permute-start | bytes 73736 | tf_op jit(solution)/shard_map/ppermute | solution.py:161
  9.3 0.5 %collective-permute-start.6 = (s32[2,8,384]{2,1,0:T(8,128)S(1)}, s32[2,8,384]{2,1,0:T(8,128)S(1)}, u32[]{:S(2)}, u32[]{:S(2)}) collective-permute-start(s32[2,8,384]{2,1,0:T(8,128)S(1)} %pad_add_fusion.1.words), channel_id=1, source_target_pairs={{1,0},{2,1},{3,2},{0,3},{5,4},{6,5},{7,6},{4,7},{9,8},{10,9},{11,1... | collective-permute-start | bytes 73736 | tf_op jit(solution)/shard_map/ppermute | solution.py:161
  9.9 2.5 %collective-permute-start.5 = (s32[2,8,384]{2,1,0:T(8,128)S(1)}, s32[2,8,384]{2,1,0:T(8,128)S(1)}, u32[]{:S(2)}, u32[]{:S(2)}) collective-permute-start(s32[2,8,384]{2,1,0:T(8,128)S(1)} %pad_add_fusion.1.words), channel_id=1, source_target_pairs={{2,0},{3,1},{0,2},{1,3},{6,4},{7,5},{4,6},{5,7},{10,8},{11,9},{8,1... | collective-permute-start | bytes 73736 | tf_op jit(solution)/shard_map/ppermute | solution.py:161
  12.4 1.8 %collective-permute-start.4 = (s32[2,8,384]{2,1,0:T(8,128)S(1)}, s32[2,8,384]{2,1,0:T(8,128)S(1)}, u32[]{:S(2)}, u32[]{:S(2)}) collective-permute-start(s32[2,8,384]{2,1,0:T(8,128)S(1)} %pad_add_fusion.1.words), channel_id=1, source_target_pairs={{3,0},{0,1},{1,2},{2,3},{7,4},{4,5},{5,6},{6,7},{11,8},{8,9},{9,10... | collective-permute-start | bytes 73736 | tf_op jit(solution)/shard_map/ppermute | solution.py:161
  14.2 0.0 collective-permute-done
  14.2 0.6 %filter_rows.1.tab = f32[32,1024]{1,0:T(8,128)S(1)} custom-call(bf16[16,1024]{1,0:T(8,128)(2,1)S(1)} %reshape.18.own, bf16[16,1024]{1,0:T(8,128)(2,1)S(1)} %reshape.19.other), custom_call_target="tpu_custom_call" | custom-call | tf_op jit(solution)/shard_map/filter_rows/pallas_call | solution.py:57
  14.8 0.7 %shard_map.28.refs_0_ = bf16[2,16,512]{2,1,0:T(8,128)(2,1)S(1)} custom-call(f32[32,1024]{1,0:T(8,128)S(1)} %filter_rows.1.tab, s32[2,8,384]{2,1,0:T(8,128)S(1)} %pad_add_fusion.1.words), custom_call_target="tpu_custom_call" | custom-call | tf_op jit(solution)/shard_map/pallas_call | solution.py:151
  15.5 1.5 %collective-permute-start.8 = (s32[2,8,384]{2,1,0:T(8,128)S(1)}, s32[2,8,384]{2,1,0:T(8,128)S(1)}, u32[]{:S(2)}, u32[]{:S(2)}) collective-permute-start(s32[2,8,384]{2,1,0:T(8,128)S(1)} %collective-permute-done.2.words), channel_id=1, source_target_pairs={{2,0},{3,1},{0,2},{1,3},{6,4},{7,5},{4,6},{5,7},{10,8},{11,9},{8,1... | collective-permute-start | bytes 73736 | tf_op jit(solution)/shard_map/ppermute | solution.py:161
  17.0 0.3 collective-permute-start.7
  17.2 1.7 %collective-permute-start.3 = (s32[2,8,384]{2,1,0:T(8,128)S(1)}, s32[2,8,384]{2,1,0:T(8,128)S(1)}, u32[]{:S(2)}, u32[]{:S(2)}) collective-permute-start(s32[2,8,384]{2,1,0:T(8,128)S(1)} %collective-permute-done.2.words), channel_id=1, source_target_pairs={{1,0},{2,1},{3,2},{0,3},{5,4},{6,5},{7,6},{4,7},{9,8},{10,9},{11,1... | collective-permute-start | bytes 73736 | tf_op jit(solution)/shard_map/ppermute | solution.py:161
  19.0 0.6 %shard_map.32.refs_4_ = bf16[2,16,512]{2,1,0:T(8,128)(2,1)S(1)} custom-call(f32[32,1024]{1,0:T(8,128)S(1)} %filter_rows.1.tab, s32[2,8,384]{2,1,0:T(8,128)S(1)} %collective-permute-done.2.words), custom_call_target="tpu_custom_call" | custom-call | tf_op jit(solution)/shard_map/pallas_call | solution.py:151
  19.6 0.7 %shard_map.31.refs_3_ = bf16[2,16,512]{2,1,0:T(8,128)(2,1)S(1)} custom-call(f32[32,1024]{1,0:T(8,128)S(1)} %filter_rows.1.tab, s32[2,8,384]{2,1,0:T(8,128)S(1)} %collective-permute-done.6.words), custom_call_target="tpu_custom_call" | custom-call | tf_op jit(solution)/shard_map/pallas_call | solution.py:151
  20.3 0.7 %shard_map.30.refs_2_ = bf16[2,16,512]{2,1,0:T(8,128)(2,1)S(1)} custom-call(f32[32,1024]{1,0:T(8,128)S(1)} %filter_rows.1.tab, s32[2,8,384]{2,1,0:T(8,128)S(1)} %collective-permute-done.5.words), custom_call_target="tpu_custom_call" | custom-call | tf_op jit(solution)/shard_map/pallas_call | solution.py:151
  21.0 0.7 %shard_map.29.refs_1_ = bf16[2,16,512]{2,1,0:T(8,128)(2,1)S(1)} custom-call(f32[32,1024]{1,0:T(8,128)S(1)} %filter_rows.1.tab, s32[2,8,384]{2,1,0:T(8,128)S(1)} %collective-permute-done.4.words), custom_call_target="tpu_custom_call" | custom-call | tf_op jit(solution)/shard_map/pallas_call | solution.py:151
  21.6 0.7 %shard_map.34.refs_6_ = bf16[2,16,512]{2,1,0:T(8,128)(2,1)S(1)} custom-call(f32[32,1024]{1,0:T(8,128)S(1)} %filter_rows.1.tab, s32[2,8,384]{2,1,0:T(8,128)S(1)} %collective-permute-done.8.words), custom_call_target="tpu_custom_call" | custom-call | tf_op jit(solution)/shard_map/pallas_call | solution.py:151
  22.3 0.7 %shard_map.33.refs_5_ = bf16[2,16,512]{2,1,0:T(8,128)(2,1)S(1)} custom-call(f32[32,1024]{1,0:T(8,128)S(1)} %filter_rows.1.tab, s32[2,8,384]{2,1,0:T(8,128)S(1)} %collective-permute-done.7.words), custom_call_target="tpu_custom_call" | custom-call | tf_op jit(solution)/shard_map/pallas_call | solution.py:151
  23.0 0.7 %shard_map.35 = bf16[16,16,512]{2,1,0:T(8,128)(2,1)S(1)} custom-call(f32[32,1024]{1,0:T(8,128)S(1)} %filter_rows.1.tab, s32[2,8,384]{2,1,0:T(8,128)S(1)} %collective-permute-done.3.words, bf16[2,16,512]{2,1,0:T(8,128)(2,1)S(1)} %shard_map.28.refs_0_, bf16[2,16,512]{2,1,0:T(8,128)(2,1)S(1)} %shard_map.29.refs_1_, bf16[2,16,512]{2,1,0:T(8,128)(2,1)S(1)} %shard_map.30.refs_2_, ...), custom_call_target="tpu_custom_call" | custom-call | tf_op jit(solution)/shard_map/pallas_call | solution.py:151
  23.6 14.9 %all_to_all.5 = bf16[16,16,512]{2,1,0:T(8,128)(2,1)S(1)} all-to-all(bf16[16,16,512]{2,1,0:T(8,128)(2,1)S(1)} %shard_map.35), channel_id=1, replica_groups=mesh['y'=4,'z_lo'=4,'core'=2,'z_hi'=2,'x'=4] {'y','z_lo'}, dimensions={0} | all-to-all | bytes 524288 | tf_op jit(solution)/shard_map/all_to_all | solution.py:186
  38.6 0.6 %multiply_bitcast_fusion = f32[2,8,512]{2,1,0:T(8,128)} fusion(f32[16,512]{1,0:T(8,128)S(1)} %convert_reduce_fusion), kind=kLoop, calls=%fused_computation.1 | loop fusion | flops 8192 | bytes 65536 | tf_op jit(solution)/shard_map/mul | solution.py:188
  (17 shorter events, 0.2 us)
Async XLA Ops:
  0.8 0.8 %copy-start = (bf16[8,2,1024]{2,1,0:T(2,128)(2,1)S(1)}, bf16[8,2,1024]{2,1,0:T(2,128)(2,1)}, u32[]{:S(2)}) copy-start(bf16[8,2,1024]{2,1,0:T(2,128)(2,1)} %param.2) | copy-start | bytes 98308
  0.8 1.3 %collective-permute-start.1 = (s32[8,384]{1,0:T(8,128)S(1)}, s32[8,384]{1,0:T(8,128)S(1)}, u32[]{:S(2)}, u32[]{:S(2)}) collective-permute-start(s32[8,384]{1,0:T(8,128)S(1)} %reshape.21), channel_id=1, source_target_pairs={{8,0},{0,8},{9,1},{1,9},{10,2},{2,10},{11,3},{3,11},{12,4},{4,12},... | collective-permute-start | bytes 36872 | tf_op jit(solution)/shard_map/ppermute | solution.py:161
  1.5 12.6 %collective-permute-start = (bf16[8,2,1024]{2,1,0:T(2,128)(2,1)S(1)}, bf16[8,2,1024]{2,1,0:T(2,128)(2,1)S(1)}, u32[]{:S(2)}, u32[]{:S(2)}) collective-permute-start(bf16[8,2,1024]{2,1,0:T(2,128)(2,1)S(1)} %copy-done), channel_id=1, source_target_pairs={{8,0},{0,8},{9,1},{1,9},{10,2},{2,10},{11,3},{3,11},{12,4},{4,12},... | collective-permute-start | bytes 98312 | tf_op jit(solution)/shard_map/ppermute | solution.py:161
  2.1 13.4 %collective-permute-start.2 = (s32[2,8,384]{2,1,0:T(8,128)S(1)}, s32[2,8,384]{2,1,0:T(8,128)S(1)}, u32[]{:S(2)}, u32[]{:S(2)}) collective-permute-start(s32[2,8,384]{2,1,0:T(8,128)S(1)} %pad_add_fusion.1.words), channel_id=1, source_target_pairs={{4,0},{0,4},{5,1},{1,5},{6,2},{2,6},{7,3},{3,7},{12,8},{8,12},{13,... | collective-permute-start | bytes 73736 | tf_op jit(solution)/shard_map/ppermute | solution.py:161
  9.3 7.9 %collective-permute-start.6 = (s32[2,8,384]{2,1,0:T(8,128)S(1)}, s32[2,8,384]{2,1,0:T(8,128)S(1)}, u32[]{:S(2)}, u32[]{:S(2)}) collective-permute-start(s32[2,8,384]{2,1,0:T(8,128)S(1)} %pad_add_fusion.1.words), channel_id=1, source_target_pairs={{1,0},{2,1},{3,2},{0,3},{5,4},{6,5},{7,6},{4,7},{9,8},{10,9},{11,1... | collective-permute-start | bytes 73736 | tf_op jit(solution)/shard_map/ppermute | solution.py:161
  9.9 10.5 %collective-permute-start.5 = (s32[2,8,384]{2,1,0:T(8,128)S(1)}, s32[2,8,384]{2,1,0:T(8,128)S(1)}, u32[]{:S(2)}, u32[]{:S(2)}) collective-permute-start(s32[2,8,384]{2,1,0:T(8,128)S(1)} %pad_add_fusion.1.words), channel_id=1, source_target_pairs={{2,0},{3,1},{0,2},{1,3},{6,4},{7,5},{4,6},{5,7},{10,8},{11,9},{8,1... | collective-permute-start | bytes 73736 | tf_op jit(solution)/shard_map/ppermute | solution.py:161
  12.4 8.6 %collective-permute-start.4 = (s32[2,8,384]{2,1,0:T(8,128)S(1)}, s32[2,8,384]{2,1,0:T(8,128)S(1)}, u32[]{:S(2)}, u32[]{:S(2)}) collective-permute-start(s32[2,8,384]{2,1,0:T(8,128)S(1)} %pad_add_fusion.1.words), channel_id=1, source_target_pairs={{3,0},{0,1},{1,2},{2,3},{7,4},{4,5},{5,6},{6,7},{11,8},{8,9},{9,10... | collective-permute-start | bytes 73736 | tf_op jit(solution)/shard_map/ppermute | solution.py:161
  15.5 6.2 %collective-permute-start.8 = (s32[2,8,384]{2,1,0:T(8,128)S(1)}, s32[2,8,384]{2,1,0:T(8,128)S(1)}, u32[]{:S(2)}, u32[]{:S(2)}) collective-permute-start(s32[2,8,384]{2,1,0:T(8,128)S(1)} %collective-permute-done.2.words), channel_id=1, source_target_pairs={{2,0},{3,1},{0,2},{1,3},{6,4},{7,5},{4,6},{5,7},{10,8},{11,9},{8,1... | collective-permute-start | bytes 73736 | tf_op jit(solution)/shard_map/ppermute | solution.py:161
  17.0 5.3 %collective-permute-start.7 = (s32[2,8,384]{2,1,0:T(8,128)S(1)}, s32[2,8,384]{2,1,0:T(8,128)S(1)}, u32[]{:S(2)}, u32[]{:S(2)}) collective-permute-start(s32[2,8,384]{2,1,0:T(8,128)S(1)} %collective-permute-done.2.words), channel_id=1, source_target_pairs={{3,0},{0,1},{1,2},{2,3},{7,4},{4,5},{5,6},{6,7},{11,8},{8,9},{9,10... | collective-permute-start | bytes 73736 | tf_op jit(solution)/shard_map/ppermute | solution.py:161
  17.2 5.7 %collective-permute-start.3 = (s32[2,8,384]{2,1,0:T(8,128)S(1)}, s32[2,8,384]{2,1,0:T(8,128)S(1)}, u32[]{:S(2)}, u32[]{:S(2)}) collective-permute-start(s32[2,8,384]{2,1,0:T(8,128)S(1)} %collective-permute-done.2.words), channel_id=1, source_target_pairs={{1,0},{2,1},{3,2},{0,3},{5,4},{6,5},{7,6},{4,7},{9,8},{10,9},{11,1... | collective-permute-start | bytes 73736 | tf_op jit(solution)/shard_map/ppermute | solution.py:161

commit v8 on v7

--- a/solution.py
+++ b/solution.py
@@ -50,19 +50,6 @@
         )
         total = part if total is None else total + part
     out[...] = total.astype(jnp.bfloat16).astype(jnp.float32)
-
-
-def filter_rows(own, other):
-    rows, bins = own.shape
-    return pl.pallas_call(
-        filter_kernel,
-        out_shape=jax.ShapeDtypeStruct((2 * rows, bins), jnp.float32),
-        in_specs=[VMEM, VMEM],
-        out_specs=VMEM,
-        scratch_shapes=[pltpu.VMEM((LANES, 2 * bins - LANES), jnp.bfloat16)],
-        compiler_params=pltpu.CompilerParams(vmem_limit_bytes=8 * 2**20),
-        name="filter_rows",
-    )(own, other)
 
 
 def transposed(tiles):
@@ -129,6 +116,45 @@
                 out[place + pair, r * 8 : (r + 1) * 8, p * LANES : (p + 1) * LANES] = value
 
 
+def prepare(own, other, words, tab, near, strip):
+    filter_kernel(own, other, tab, strip)
+    project_rows(tab, words, near, 0)
+
+
+def early_kernel(own, other, words, tab, near, strip):
+    @pl.when(lax.axis_index("z_hi") == 0)
+    def _():
+        prepare(own, other, words, tab, near, strip)
+
+
+def late_kernel(own, other, words, tab_early, near_early, tab, near, strip):
+    early = lax.axis_index("z_hi") == 0
+
+    @pl.when(early)
+    def _():
+        tab[...] = tab_early[...]
+        near[...] = near_early[...]
+
+    @pl.when(jnp.logical_not(early))
+    def _():
+        prepare(own, other, words, tab, near, strip)
+
+
+def prepared(kernel, operands):
+    rows, bins = operands[0].shape
+    return pl.pallas_call(
+        kernel,
+        out_shape=(
+            jax.ShapeDtypeStruct((2 * rows, bins), jnp.float32),
+            jax.ShapeDtypeStruct((2, 16, 512), jnp.bfloat16),
+        ),
+        in_specs=[VMEM] * len(operands),
+        out_specs=(VMEM, VMEM),
+        scratch_shapes=[pltpu.VMEM((LANES, 2 * bins - LANES), jnp.bfloat16)],
+        compiler_params=pltpu.CompilerParams(vmem_limit_bytes=8 * 2**20),
+    )(*operands)
+
+
 def array_kernel(tab, words, out):
     project_rows(tab, words, out, 0)
 
@@ -172,14 +198,14 @@
     own = jnp.stack([keep, permuted(give, "core", 1, 2)])
     other = permuted(own, "z_hi", 1, 2)
 
-    other_sino = permuted(sinogram, "core", 1, 2)
-    tab = filter_rows(
-        sinogram.reshape(slices * angles, bins), other_sino.reshape(slices * angles, bins)
-    )
+    sinos = [sinogram, permuted(sinogram, "core", 1, 2)]
+    operands = [sino.reshape(slices * angles, bins) for sino in sinos] + [own]
+    early = prepared(early_kernel, operands)
+    tab, near_0 = prepared(late_kernel, [*operands, *early])
     near = [own] + [permuted(own, "x", s, 4) for s in (1, 2, 3)]
-    done = [project(array_kernel, 2, [tab, near[0]])]
-    other, done[0] = lax.optimization_barrier((other, done[0]))
+    other, near_0 = lax.optimization_barrier((other, near_0))
     far = [other] + [permuted(other, "x", s, 4) for s in (1, 2, 3)]
+    done = [near_0]
     done += [project(array_kernel, 2, [tab, near[s]]) for s in (3, 2, 1)]
     done += [project(array_kernel, 2, [tab, far[s]]) for s in (0, 3, 2)]
     partial = project(last_kernel, 16, [tab, far[1], *done])

time: 39.9 us -> 40 us (level)
    pallas_call x1 -> x2, Pallas kernels: 0.61 us -> 1.34 us  [prepared(): pl.pallas_call(kernel, out_shape=(jax.ShapeDtypeStruct((2 * rows, bins),...]
    pallas_call x8 -> x7, Pallas kernels: 5.21 us -> 4.56 us  [project(): pl.pallas_call(kernel, out_shape=jax.ShapeDtypeStruct((owners, 16, 512),...]
where the time goes in v8:
time: 40 us; the launch traced here: 39.3 us
  starting transfers between devices  15.6 us (39%)
  blocking collectives  14.9 us (37%)
  Pallas kernels  5.9 us (15%)
  other arithmetic  1.42 us (4%)
  local copies, waits for them, and re-layouts  0.71 us (2%)
  waiting for transfers between devices  0.56 us (1%)
    ppermute x9, starting transfers between devices, permuted(): lax.ppermute(array, axis, [((i + step) % size, i) for i in range(size)])  15.6 us
    all_to_all x1, blocking collectives, image(): parts = lax.all_to_all(partial, ('y', 'z_lo'), 0, 0, tiled=True)  14.9 us
    pallas_call x7, Pallas kernels, project(): pl.pallas_call(kernel, out_shape=jax.ShapeDtypeStruct((owners, 16, 512),...  4.56 us
    pallas_call x2, Pallas kernels, prepared(): pl.pallas_call(kernel, out_shape=(jax.ShapeDtypeStruct((2 * rows, bins),...  1.34 us
  transfers between devices with their start and end apart: 9, of which 1 were waited for; matrix products, arithmetic and copies ran while one was open for 0% of the time, Pallas kernels for 13%

profile of v8, /device:TPU:2, one launch (start us, length us, event | category | flops | bytes accessed | tf_op | source)
XLA Modules:
  0.0 39.3 jit_solution(2437308805727319520)
XLA Ops:
  0.0 0.8 %shift-left_or_fusion.2 = (s32[2,8,128]{2,1,0:T(8,128)S(1)}, s32[2,8,128]{2,1,0:T(8,128)S(1)}, s32[2,8,128]{2,1,0:T(8,128)S(1)}) fusion(s32[2,8,512]{2,1,0:T(8,128)} %param.3), kind=kLoop, calls=%fused_computation.8 | loop fusion | flops 26624 | bytes 57344 | tf_op jit(solution)/shard_map/or | solution.py:71
  0.8 0.0 copy-start
  0.8 0.1 collective-permute-start.1
  0.9 0.6 %copy-done = bf16[8,2,1024]{2,1,0:T(2,128)(2,1)S(1)} copy-done((bf16[8,2,1024]{2,1,0:T(2,128)(2,1)S(1)}, bf16[8,2,1024]{2,1,0:T(2,128)(2,1)}, u32[]{:S(2)}) %copy-start) | copy-done | bytes 32792
  1.6 0.5 %collective-permute-done.1 = s32[8,384]{1,0:T(8,128)S(1)} collective-permute-done((s32[8,384]{1,0:T(8,128)S(1)}, s32[8,384]{1,0:T(8,128)S(1)}, u32[]{:S(2)}, u32[]{:S(2)}) %collective-permute-start.1) | collective-permute-done | bytes 12320 | tf_op jit(solution)/shard_map/ppermute | solution.py:187
  2.1 7.2 %collective-permute-start.2 = (s32[2,8,384]{2,1,0:T(8,128)S(1)}, s32[2,8,384]{2,1,0:T(8,128)S(1)}, u32[]{:S(2)}, u32[]{:S(2)}) collective-permute-start(s32[2,8,384]{2,1,0:T(8,128)S(1)} %pad_add_fusion.1.words), channel_id=1, source_target_pairs={{4,0},{0,4},{5,1},{1,5},{6,2},{2,6},{7,3},{3,7},{12,8},{8,12},{13,... | collective-permute-start | bytes 73736 | tf_op jit(solution)/shard_map/ppermute | solution.py:187
  9.3 0.5 %collective-permute-start.6 = (s32[2,8,384]{2,1,0:T(8,128)S(1)}, s32[2,8,384]{2,1,0:T(8,128)S(1)}, u32[]{:S(2)}, u32[]{:S(2)}) collective-permute-start(s32[2,8,384]{2,1,0:T(8,128)S(1)} %pad_add_fusion.1.words), channel_id=1, source_target_pairs={{1,0},{2,1},{3,2},{0,3},{5,4},{6,5},{7,6},{4,7},{9,8},{10,9},{11,1... | collective-permute-start | bytes 73736 | tf_op jit(solution)/shard_map/ppermute | solution.py:187
  9.9 2.5 %collective-permute-start.5 = (s32[2,8,384]{2,1,0:T(8,128)S(1)}, s32[2,8,384]{2,1,0:T(8,128)S(1)}, u32[]{:S(2)}, u32[]{:S(2)}) collective-permute-start(s32[2,8,384]{2,1,0:T(8,128)S(1)} %pad_add_fusion.1.words), channel_id=1, source_target_pairs={{2,0},{3,1},{0,2},{1,3},{6,4},{7,5},{4,6},{5,7},{10,8},{11,9},{8,1... | collective-permute-start | bytes 73736 | tf_op jit(solution)/shard_map/ppermute | solution.py:187
  12.4 1.8 %collective-permute-start.4 = (s32[2,8,384]{2,1,0:T(8,128)S(1)}, s32[2,8,384]{2,1,0:T(8,128)S(1)}, u32[]{:S(2)}, u32[]{:S(2)}) collective-permute-start(s32[2,8,384]{2,1,0:T(8,128)S(1)} %pad_add_fusion.1.words), channel_id=1, source_target_pairs={{3,0},{0,1},{1,2},{2,3},{7,4},{4,5},{5,6},{6,7},{11,8},{8,9},{9,10... | collective-permute-start | bytes 73736 | tf_op jit(solution)/shard_map/ppermute | solution.py:187
  14.2 0.0 collective-permute-done
  14.2 1.3 %shard_map.28 = (f32[32,1024]{1,0:T(8,128)S(1)}, bf16[2,16,512]{2,1,0:T(8,128)(2,1)S(1)}) custom-call(bf16[16,1024]{1,0:T(8,128)(2,1)S(1)} %reshape.18.own, bf16[16,1024]{1,0:T(8,128)(2,1)S(1)} %reshape.19.other, s32[2,8,384]{2,1,0:T(8,128)S(1)} %pad_add_fusion.1.words), custom_call_target="tpu_custom_call" | custom-call | tf_op jit(solution)/shard_map/pallas_call | solution.py:145
  15.5 0.0 collective-permute-done.2.words
  15.5 1.5 %collective-permute-start.8 = (s32[2,8,384]{2,1,0:T(8,128)S(1)}, s32[2,8,384]{2,1,0:T(8,128)S(1)}, u32[]{:S(2)}, u32[]{:S(2)}) collective-permute-start(s32[2,8,384]{2,1,0:T(8,128)S(1)} %collective-permute-done.2.words), channel_id=1, source_target_pairs={{2,0},{3,1},{0,2},{1,3},{6,4},{7,5},{4,6},{5,7},{10,8},{11,9},{8,1... | collective-permute-start | bytes 73736 | tf_op jit(solution)/shard_map/ppermute | solution.py:187
  17.0 0.3 collective-permute-start.7
  17.3 1.7 %collective-permute-start.3 = (s32[2,8,384]{2,1,0:T(8,128)S(1)}, s32[2,8,384]{2,1,0:T(8,128)S(1)}, u32[]{:S(2)}, u32[]{:S(2)}) collective-permute-start(s32[2,8,384]{2,1,0:T(8,128)S(1)} %collective-permute-done.2.words), channel_id=1, source_target_pairs={{1,0},{2,1},{3,2},{0,3},{5,4},{6,5},{7,6},{4,7},{9,8},{10,9},{11,1... | collective-permute-start | bytes 73736 | tf_op jit(solution)/shard_map/ppermute | solution.py:187
  19.1 0.6 %shard_map.33.refs_4_ = bf16[2,16,512]{2,1,0:T(8,128)(2,1)S(1)} custom-call(f32[32,1024]{1,0:T(8,128)S(1)} %get-tuple-element.13.tab, s32[2,8,384]{2,1,0:T(8,128)S(1)} %collective-permute-done.2.words), custom_call_target="tpu_custom_call" | custom-call | tf_op jit(solution)/shard_map/pallas_call | solution.py:177
  19.7 0.7 %shard_map.32.refs_3_ = bf16[2,16,512]{2,1,0:T(8,128)(2,1)S(1)} custom-call(f32[32,1024]{1,0:T(8,128)S(1)} %get-tuple-element.13.tab, s32[2,8,384]{2,1,0:T(8,128)S(1)} %collective-permute-done.6.words), custom_call_target="tpu_custom_call" | custom-call | tf_op jit(solution)/shard_map/pallas_call | solution.py:177
  20.4 0.7 %shard_map.31.refs_2_ = bf16[2,16,512]{2,1,0:T(8,128)(2,1)S(1)} custom-call(f32[32,1024]{1,0:T(8,128)S(1)} %get-tuple-element.13.tab, s32[2,8,384]{2,1,0:T(8,128)S(1)} %collective-permute-done.5.words), custom_call_target="tpu_custom_call" | custom-call | tf_op jit(solution)/shard_map/pallas_call | solution.py:177
  21.1 0.7 %shard_map.30.refs_1_ = bf16[2,16,512]{2,1,0:T(8,128)(2,1)S(1)} custom-call(f32[32,1024]{1,0:T(8,128)S(1)} %get-tuple-element.13.tab, s32[2,8,384]{2,1,0:T(8,128)S(1)} %collective-permute-done.4.words), custom_call_target="tpu_custom_call" | custom-call | tf_op jit(solution)/shard_map/pallas_call | solution.py:177
  21.7 0.7 %shard_map.35.refs_6_ = bf16[2,16,512]{2,1,0:T(8,128)(2,1)S(1)} custom-call(f32[32,1024]{1,0:T(8,128)S(1)} %get-tuple-element.13.tab, s32[2,8,384]{2,1,0:T(8,128)S(1)} %collective-permute-done.8.words), custom_call_target="tpu_custom_call" | custom-call | tf_op jit(solution)/shard_map/pallas_call | solution.py:177
  22.4 0.7 %shard_map.34.refs_5_ = bf16[2,16,512]{2,1,0:T(8,128)(2,1)S(1)} custom-call(f32[32,1024]{1,0:T(8,128)S(1)} %get-tuple-element.13.tab, s32[2,8,384]{2,1,0:T(8,128)S(1)} %collective-permute-done.7.words), custom_call_target="tpu_custom_call" | custom-call | tf_op jit(solution)/shard_map/pallas_call | solution.py:177
  23.1 0.7 %shard_map.36 = bf16[16,16,512]{2,1,0:T(8,128)(2,1)S(1)} custom-call(f32[32,1024]{1,0:T(8,128)S(1)} %get-tuple-element.13.tab, s32[2,8,384]{2,1,0:T(8,128)S(1)} %collective-permute-done.3.words, bf16[2,16,512]{2,1,0:T(8,128)(2,1)S(1)} %get-tuple-element.16.refs_0_, bf16[2,16,512]{2,1,0:T(8,128)(2,1)S(1)} %shard_map.30.refs_1_, ...), custom_call_target="tpu_custom_call" | custom-call | tf_op jit(solution)/shard_map/pallas_call | solution.py:177
  23.7 14.9 %all_to_all.5 = bf16[16,16,512]{2,1,0:T(8,128)(2,1)S(1)} all-to-all(bf16[16,16,512]{2,1,0:T(8,128)(2,1)S(1)} %shard_map.36), channel_id=1, replica_groups=mesh['y'=4,'z_lo'=4,'core'=2,'z_hi'=2,'x'=4] {'y','z_lo'}, dimensions={0} | all-to-all | bytes 524288 | tf_op jit(solution)/shard_map/all_to_all | solution.py:212
  38.6 0.6 %multiply_bitcast_fusion = f32[2,8,512]{2,1,0:T(8,128)} fusion(f32[16,512]{1,0:T(8,128)S(1)} %convert_reduce_fusion), kind=kLoop, calls=%fused_computation.1 | loop fusion | flops 8192 | bytes 65536 | tf_op jit(solution)/shard_map/mul | solution.py:214
  (17 shorter events, 0.2 us)
Async XLA Ops:
  0.8 0.8 %copy-start = (bf16[8,2,1024]{2,1,0:T(2,128)(2,1)S(1)}, bf16[8,2,1024]{2,1,0:T(2,128)(2,1)}, u32[]{:S(2)}) copy-start(bf16[8,2,1024]{2,1,0:T(2,128)(2,1)} %param.2) | copy-start | bytes 98308
  0.8 1.3 %collective-permute-start.1 = (s32[8,384]{1,0:T(8,128)S(1)}, s32[8,384]{1,0:T(8,128)S(1)}, u32[]{:S(2)}, u32[]{:S(2)}) collective-permute-start(s32[8,384]{1,0:T(8,128)S(1)} %reshape.21), channel_id=1, source_target_pairs={{8,0},{0,8},{9,1},{1,9},{10,2},{2,10},{11,3},{3,11},{12,4},{4,12},... | collective-permute-start | bytes 36872 | tf_op jit(solution)/shard_map/ppermute | solution.py:187
  1.5 12.6 %collective-permute-start = (bf16[8,2,1024]{2,1,0:T(2,128)(2,1)S(1)}, bf16[8,2,1024]{2,1,0:T(2,128)(2,1)S(1)}, u32[]{:S(2)}, u32[]{:S(2)}) collective-permute-start(bf16[8,2,1024]{2,1,0:T(2,128)(2,1)S(1)} %copy-done), channel_id=1, source_target_pairs={{8,0},{0,8},{9,1},{1,9},{10,2},{2,10},{11,3},{3,11},{12,4},{4,12},... | collective-permute-start | bytes 98312 | tf_op jit(solution)/shard_map/ppermute | solution.py:187
  2.1 13.4 %collective-permute-start.2 = (s32[2,8,384]{2,1,0:T(8,128)S(1)}, s32[2,8,384]{2,1,0:T(8,128)S(1)}, u32[]{:S(2)}, u32[]{:S(2)}) collective-permute-start(s32[2,8,384]{2,1,0:T(8,128)S(1)} %pad_add_fusion.1.words), channel_id=1, source_target_pairs={{4,0},{0,4},{5,1},{1,5},{6,2},{2,6},{7,3},{3,7},{12,8},{8,12},{13,... | collective-permute-start | bytes 73736 | tf_op jit(solution)/shard_map/ppermute | solution.py:187
  9.3 8.0 %collective-permute-start.6 = (s32[2,8,384]{2,1,0:T(8,128)S(1)}, s32[2,8,384]{2,1,0:T(8,128)S(1)}, u32[]{:S(2)}, u32[]{:S(2)}) collective-permute-start(s32[2,8,384]{2,1,0:T(8,128)S(1)} %pad_add_fusion.1.words), channel_id=1, source_target_pairs={{1,0},{2,1},{3,2},{0,3},{5,4},{6,5},{7,6},{4,7},{9,8},{10,9},{11,1... | collective-permute-start | bytes 73736 | tf_op jit(solution)/shard_map/ppermute | solution.py:187
  9.9 10.5 %collective-permute-start.5 = (s32[2,8,384]{2,1,0:T(8,128)S(1)}, s32[2,8,384]{2,1,0:T(8,128)S(1)}, u32[]{:S(2)}, u32[]{:S(2)}) collective-permute-start(s32[2,8,384]{2,1,0:T(8,128)S(1)} %pad_add_fusion.1.words), channel_id=1, source_target_pairs={{2,0},{3,1},{0,2},{1,3},{6,4},{7,5},{4,6},{5,7},{10,8},{11,9},{8,1... | collective-permute-start | bytes 73736 | tf_op jit(solution)/shard_map/ppermute | solution.py:187
  12.4 8.7 %collective-permute-start.4 = (s32[2,8,384]{2,1,0:T(8,128)S(1)}, s32[2,8,384]{2,1,0:T(8,128)S(1)}, u32[]{:S(2)}, u32[]{:S(2)}) collective-permute-start(s32[2,8,384]{2,1,0:T(8,128)S(1)} %pad_add_fusion.1.words), channel_id=1, source_target_pairs={{3,0},{0,1},{1,2},{2,3},{7,4},{4,5},{5,6},{6,7},{11,8},{8,9},{9,10... | collective-permute-start | bytes 73736 | tf_op jit(solution)/shard_map/ppermute | solution.py:187
  15.5 6.2 %collective-permute-start.8 = (s32[2,8,384]{2,1,0:T(8,128)S(1)}, s32[2,8,384]{2,1,0:T(8,128)S(1)}, u32[]{:S(2)}, u32[]{:S(2)}) collective-permute-start(s32[2,8,384]{2,1,0:T(8,128)S(1)} %collective-permute-done.2.words), channel_id=1, source_target_pairs={{2,0},{3,1},{0,2},{1,3},{6,4},{7,5},{4,6},{5,7},{10,8},{11,9},{8,1... | collective-permute-start | bytes 73736 | tf_op jit(solution)/shard_map/ppermute | solution.py:187
  17.0 5.3 %collective-permute-start.7 = (s32[2,8,384]{2,1,0:T(8,128)S(1)}, s32[2,8,384]{2,1,0:T(8,128)S(1)}, u32[]{:S(2)}, u32[]{:S(2)}) collective-permute-start(s32[2,8,384]{2,1,0:T(8,128)S(1)} %collective-permute-done.2.words), channel_id=1, source_target_pairs={{3,0},{0,1},{1,2},{2,3},{7,4},{4,5},{5,6},{6,7},{11,8},{8,9},{9,10... | collective-permute-start | bytes 73736 | tf_op jit(solution)/shard_map/ppermute | solution.py:187
  17.3 5.7 %collective-permute-start.3 = (s32[2,8,384]{2,1,0:T(8,128)S(1)}, s32[2,8,384]{2,1,0:T(8,128)S(1)}, u32[]{:S(2)}, u32[]{:S(2)}) collective-permute-start(s32[2,8,384]{2,1,0:T(8,128)S(1)} %collective-permute-done.2.words), channel_id=1, source_target_pairs={{1,0},{2,1},{3,2},{0,3},{5,4},{6,5},{7,6},{4,7},{9,8},{10,9},{11,1... | collective-permute-start | bytes 73736 | tf_op jit(solution)/shard_map/ppermute | solution.py:187

commit v9 on v7

--- a/solution.py
+++ b/solution.py
@@ -133,7 +133,7 @@
     project_rows(tab, words, out, 0)
 
 
-ORDER = ((0, 0), (0, 3), (0, 2), (0, 1), (1, 0), (1, 3), (1, 2), (1, 1))
+ORDER = ((0, 0), (0, 3), (0, 1), (1, 0), (1, 3), (1, 2), (1, 1), (0, 2))
 
 
 def last_kernel(tab, words, *refs):
@@ -180,9 +180,9 @@
     done = [project(array_kernel, 2, [tab, near[0]])]
     other, done[0] = lax.optimization_barrier((other, done[0]))
     far = [other] + [permuted(other, "x", s, 4) for s in (1, 2, 3)]
-    done += [project(array_kernel, 2, [tab, near[s]]) for s in (3, 2, 1)]
-    done += [project(array_kernel, 2, [tab, far[s]]) for s in (0, 3, 2)]
-    partial = project(last_kernel, 16, [tab, far[1], *done])
+    done += [project(array_kernel, 2, [tab, near[s]]) for s in (3, 1)]
+    done += [project(array_kernel, 2, [tab, far[s]]) for s in (0, 3, 2, 1)]
+    partial = project(last_kernel, 16, [tab, near[2], *done])
     parts = lax.all_to_all(partial, ("y", "z_lo"), 0, 0, tiled=True)
     scale = jnp.float32(math.pi / (angles * lax.axis_size(("y", "z_lo", "core"))))
     image_rows = jnp.sum(parts.astype(jnp.float32), axis=0) * scale

time: 39.9 us -> 40.6 us (1.018); the launches traced: 39.2 us -> 40.3 us
  waiting for transfers between devices: 0.56 us -> 1.31 us
    ppermute x9, waiting for transfers between devices: 0.56 us -> 1.31 us  [permuted(): lax.ppermute(array, axis, [((i + step) % size, i) for i in range(size)])]
  transfers between devices with their start and end apart: 9 -> 9, of which waited for: 1 -> 2; matrix products, arithmetic and copies ran while one was open for 0% -> 0% of each run, Pallas kernels for 13% -> 13%
where the time goes in v9:
time: 40.6 us; the launch traced here: 40.3 us
  starting transfers between devices  16 us (39%)
  blocking collectives  14.9 us (37%)
  Pallas kernels  5.82 us (14%)
  other arithmetic  1.42 us (3%)
  waiting for transfers between devices  1.31 us (3%)
  local copies, waits for them, and re-layouts  0.71 us (2%)
    ppermute x9, starting transfers between devices, permuted(): lax.ppermute(array, axis, [((i + step) % size, i) for i in range(size)])  16 us
    all_to_all x1, blocking collectives, image(): parts = lax.all_to_all(partial, ('y', 'z_lo'), 0, 0, tiled=True)  14.9 us
    pallas_call x8, Pallas kernels, project(): pl.pallas_call(kernel, out_shape=jax.ShapeDtypeStruct((owners, 16, 512),...  5.21 us
    ppermute x9, waiting for transfers between devices, permuted(): lax.ppermute(array, axis, [((i + step) % size, i) for i in range(size)])  1.31 us
  transfers between devices with their start and end apart: 9, of which 2 were waited for; matrix products, arithmetic and copies ran while one was open for 0% of the time, Pallas kernels for 13%

profile of v9, /device:TPU:2, one launch (start us, length us, event | category | flops | bytes accessed | tf_op | source)
XLA Modules:
  0.0 40.3 jit_solution(8227732633197494673)
XLA Ops:
  0.0 0.8 %shift-left_or_fusion.2 = (s32[2,8,128]{2,1,0:T(8,128)S(1)}, s32[2,8,128]{2,1,0:T(8,128)S(1)}, s32[2,8,128]{2,1,0:T(8,128)S(1)}) fusion(s32[2,8,512]{2,1,0:T(8,128)} %param.3), kind=kLoop, calls=%fused_computation.8 | loop fusion | flops 26624 | bytes 57344 | tf_op jit(solution)/shard_map/or | solution.py:84
  0.8 0.0 copy-start
  0.8 0.1 collective-permute-start.1
  0.9 0.6 %copy-done = bf16[8,2,1024]{2,1,0:T(2,128)(2,1)S(1)} copy-done((bf16[8,2,1024]{2,1,0:T(2,128)(2,1)S(1)}, bf16[8,2,1024]{2,1,0:T(2,128)(2,1)}, u32[]{:S(2)}) %copy-start) | copy-done | bytes 32792
  1.6 0.5 %collective-permute-done.1 = s32[8,384]{1,0:T(8,128)S(1)} collective-permute-done((s32[8,384]{1,0:T(8,128)S(1)}, s32[8,384]{1,0:T(8,128)S(1)}, u32[]{:S(2)}, u32[]{:S(2)}) %collective-permute-start.1) | collective-permute-done | bytes 12320 | tf_op jit(solution)/shard_map/ppermute | solution.py:161
  2.1 7.2 %collective-permute-start.3 = (s32[2,8,384]{2,1,0:T(8,128)S(1)}, s32[2,8,384]{2,1,0:T(8,128)S(1)}, u32[]{:S(2)}, u32[]{:S(2)}) collective-permute-start(s32[2,8,384]{2,1,0:T(8,128)S(1)} %pad_add_fusion.1.words), channel_id=1, source_target_pairs={{4,0},{0,4},{5,1},{1,5},{6,2},{2,6},{7,3},{3,7},{12,8},{8,12},{13,... | collective-permute-start | bytes 73736 | tf_op jit(solution)/shard_map/ppermute | solution.py:161
  9.3 0.5 %collective-permute-start.5 = (s32[2,8,384]{2,1,0:T(8,128)S(1)}, s32[2,8,384]{2,1,0:T(8,128)S(1)}, u32[]{:S(2)}, u32[]{:S(2)}) collective-permute-start(s32[2,8,384]{2,1,0:T(8,128)S(1)} %pad_add_fusion.1.words), channel_id=1, source_target_pairs={{1,0},{2,1},{3,2},{0,3},{5,4},{6,5},{7,6},{4,7},{9,8},{10,9},{11,1... | collective-permute-start | bytes 73736 | tf_op jit(solution)/shard_map/ppermute | solution.py:161
  9.9 1.6 %collective-permute-start.4 = (s32[2,8,384]{2,1,0:T(8,128)S(1)}, s32[2,8,384]{2,1,0:T(8,128)S(1)}, u32[]{:S(2)}, u32[]{:S(2)}) collective-permute-start(s32[2,8,384]{2,1,0:T(8,128)S(1)} %pad_add_fusion.1.words), channel_id=1, source_target_pairs={{3,0},{0,1},{1,2},{2,3},{7,4},{4,5},{5,6},{6,7},{11,8},{8,9},{9,10... | collective-permute-start | bytes 73736 | tf_op jit(solution)/shard_map/ppermute | solution.py:161
  11.4 0.6 %filter_rows.1.tab = f32[32,1024]{1,0:T(8,128)S(1)} custom-call(bf16[16,1024]{1,0:T(8,128)(2,1)S(1)} %reshape.18.own, bf16[16,1024]{1,0:T(8,128)(2,1)S(1)} %reshape.19.other), custom_call_target="tpu_custom_call" | custom-call | tf_op jit(solution)/shard_map/filter_rows/pallas_call | solution.py:57
  12.1 0.7 %shard_map.28.refs_0_ = bf16[2,16,512]{2,1,0:T(8,128)(2,1)S(1)} custom-call(f32[32,1024]{1,0:T(8,128)S(1)} %filter_rows.1.tab, s32[2,8,384]{2,1,0:T(8,128)S(1)} %pad_add_fusion.1.words), custom_call_target="tpu_custom_call" | custom-call | tf_op jit(solution)/shard_map/pallas_call | solution.py:151
  12.7 1.4 %collective-permute-start.8 = (s32[2,8,384]{2,1,0:T(8,128)S(1)}, s32[2,8,384]{2,1,0:T(8,128)S(1)}, u32[]{:S(2)}, u32[]{:S(2)}) collective-permute-start(s32[2,8,384]{2,1,0:T(8,128)S(1)} %collective-permute-done.3.words), channel_id=1, source_target_pairs={{1,0},{2,1},{3,2},{0,3},{5,4},{6,5},{7,6},{4,7},{9,8},{10,9},{11,1... | collective-permute-start | bytes 73736 | tf_op jit(solution)/shard_map/ppermute | solution.py:161
  14.1 2.1 %collective-permute-start.7 = (s32[2,8,384]{2,1,0:T(8,128)S(1)}, s32[2,8,384]{2,1,0:T(8,128)S(1)}, u32[]{:S(2)}, u32[]{:S(2)}) collective-permute-start(s32[2,8,384]{2,1,0:T(8,128)S(1)} %collective-permute-done.3.words), channel_id=1, source_target_pairs={{2,0},{3,1},{0,2},{1,3},{6,4},{7,5},{4,6},{5,7},{10,8},{11,9},{8,1... | collective-permute-start | bytes 73736 | tf_op jit(solution)/shard_map/ppermute | solution.py:161
  16.2 2.5 %collective-permute-start.6 = (s32[2,8,384]{2,1,0:T(8,128)S(1)}, s32[2,8,384]{2,1,0:T(8,128)S(1)}, u32[]{:S(2)}, u32[]{:S(2)}) collective-permute-start(s32[2,8,384]{2,1,0:T(8,128)S(1)} %collective-permute-done.3.words), channel_id=1, source_target_pairs={{3,0},{0,1},{1,2},{2,3},{7,4},{4,5},{5,6},{6,7},{11,8},{8,9},{9,10... | collective-permute-start | bytes 73736 | tf_op jit(solution)/shard_map/ppermute | solution.py:161
  18.8 0.6 %collective-permute-start.2 = (s32[2,8,384]{2,1,0:T(8,128)S(1)}, s32[2,8,384]{2,1,0:T(8,128)S(1)}, u32[]{:S(2)}, u32[]{:S(2)}) collective-permute-start(s32[2,8,384]{2,1,0:T(8,128)S(1)} %pad_add_fusion.1.words), channel_id=1, source_target_pairs={{2,0},{3,1},{0,2},{1,3},{6,4},{7,5},{4,6},{5,7},{10,8},{11,9},{8,1... | collective-permute-start | bytes 73736 | tf_op jit(solution)/shard_map/ppermute | solution.py:161
  19.4 0.6 %shard_map.31.refs_3_ = bf16[2,16,512]{2,1,0:T(8,128)(2,1)S(1)} custom-call(f32[32,1024]{1,0:T(8,128)S(1)} %filter_rows.1.tab, s32[2,8,384]{2,1,0:T(8,128)S(1)} %collective-permute-done.3.words), custom_call_target="tpu_custom_call" | custom-call | tf_op jit(solution)/shard_map/pallas_call | solution.py:151
  20.0 0.7 %shard_map.30.refs_2_ = bf16[2,16,512]{2,1,0:T(8,128)(2,1)S(1)} custom-call(f32[32,1024]{1,0:T(8,128)S(1)} %filter_rows.1.tab, s32[2,8,384]{2,1,0:T(8,128)S(1)} %collective-permute-done.5.words), custom_call_target="tpu_custom_call" | custom-call | tf_op jit(solution)/shard_map/pallas_call | solution.py:151
  20.7 0.7 %shard_map.29.refs_1_ = bf16[2,16,512]{2,1,0:T(8,128)(2,1)S(1)} custom-call(f32[32,1024]{1,0:T(8,128)S(1)} %filter_rows.1.tab, s32[2,8,384]{2,1,0:T(8,128)S(1)} %collective-permute-done.4.words), custom_call_target="tpu_custom_call" | custom-call | tf_op jit(solution)/shard_map/pallas_call | solution.py:151
  21.4 0.7 %shard_map.34.refs_6_ = bf16[2,16,512]{2,1,0:T(8,128)(2,1)S(1)} custom-call(f32[32,1024]{1,0:T(8,128)S(1)} %filter_rows.1.tab, s32[2,8,384]{2,1,0:T(8,128)S(1)} %collective-permute-done.8.words), custom_call_target="tpu_custom_call" | custom-call | tf_op jit(solution)/shard_map/pallas_call | solution.py:151
  22.0 0.7 %shard_map.33.refs_5_ = bf16[2,16,512]{2,1,0:T(8,128)(2,1)S(1)} custom-call(f32[32,1024]{1,0:T(8,128)S(1)} %filter_rows.1.tab, s32[2,8,384]{2,1,0:T(8,128)S(1)} %collective-permute-done.7.words), custom_call_target="tpu_custom_call" | custom-call | tf_op jit(solution)/shard_map/pallas_call | solution.py:151
  22.7 0.7 %shard_map.32.refs_4_ = bf16[2,16,512]{2,1,0:T(8,128)(2,1)S(1)} custom-call(f32[32,1024]{1,0:T(8,128)S(1)} %filter_rows.1.tab, s32[2,8,384]{2,1,0:T(8,128)S(1)} %collective-permute-done.6.words), custom_call_target="tpu_custom_call" | custom-call | tf_op jit(solution)/shard_map/pallas_call | solution.py:151
  23.4 0.8 %collective-permute-done.2.words = s32[2,8,384]{2,1,0:T(8,128)S(1)} collective-permute-done((s32[2,8,384]{2,1,0:T(8,128)S(1)}, s32[2,8,384]{2,1,0:T(8,128)S(1)}, u32[]{:S(2)}, u32[]{:S(2)}) %collective-permute-start.2) | collective-permute-done | bytes 24608 | tf_op jit(solution)/shard_map/ppermute | solution.py:161
  24.1 0.7 %shard_map.35 = bf16[16,16,512]{2,1,0:T(8,128)(2,1)S(1)} custom-call(f32[32,1024]{1,0:T(8,128)S(1)} %filter_rows.1.tab, s32[2,8,384]{2,1,0:T(8,128)S(1)} %collective-permute-done.2.words, bf16[2,16,512]{2,1,0:T(8,128)(2,1)S(1)} %shard_map.28.refs_0_, bf16[2,16,512]{2,1,0:T(8,128)(2,1)S(1)} %shard_map.29.refs_1_, bf16[2,16,512]{2,1,0:T(8,128)(2,1)S(1)} %shard_map.30.refs_2_, ...), custom_call_target="tpu_custom_call" | custom-call | tf_op jit(solution)/shard_map/pallas_call | solution.py:151
  24.8 14.9 %all_to_all.5 = bf16[16,16,512]{2,1,0:T(8,128)(2,1)S(1)} all-to-all(bf16[16,16,512]{2,1,0:T(8,128)(2,1)S(1)} %shard_map.35), channel_id=1, replica_groups=mesh['y'=4,'z_lo'=4,'core'=2,'z_hi'=2,'x'=4] {'y','z_lo'}, dimensions={0} | all-to-all | bytes 524288 | tf_op jit(solution)/shard_map/all_to_all | solution.py:186
  39.7 0.6 %multiply_bitcast_fusion = f32[2,8,512]{2,1,0:T(8,128)} fusion(f32[16,512]{1,0:T(8,128)S(1)} %convert_reduce_fusion), kind=kLoop, calls=%fused_computation.1 | loop fusion | flops 8192 | bytes 65536 | tf_op jit(solution)/shard_map/mul | solution.py:188
  (17 shorter events, 0.2 us)
Async XLA Ops:
  0.8 0.8 %copy-start = (bf16[8,2,1024]{2,1,0:T(2,128)(2,1)S(1)}, bf16[8,2,1024]{2,1,0:T(2,128)(2,1)}, u32[]{:S(2)}) copy-start(bf16[8,2,1024]{2,1,0:T(2,128)(2,1)} %param.2) | copy-start | bytes 98308
  0.8 1.3 %collective-permute-start.1 = (s32[8,384]{1,0:T(8,128)S(1)}, s32[8,384]{1,0:T(8,128)S(1)}, u32[]{:S(2)}, u32[]{:S(2)}) collective-permute-start(s32[8,384]{1,0:T(8,128)S(1)} %reshape.21), channel_id=1, source_target_pairs={{8,0},{0,8},{9,1},{1,9},{10,2},{2,10},{11,3},{3,11},{12,4},{4,12},... | collective-permute-start | bytes 36872 | tf_op jit(solution)/shard_map/ppermute | solution.py:161
  1.5 9.9 %collective-permute-start = (bf16[8,2,1024]{2,1,0:T(2,128)(2,1)S(1)}, bf16[8,2,1024]{2,1,0:T(2,128)(2,1)S(1)}, u32[]{:S(2)}, u32[]{:S(2)}) collective-permute-start(bf16[8,2,1024]{2,1,0:T(2,128)(2,1)S(1)} %copy-done), channel_id=1, source_target_pairs={{8,0},{0,8},{9,1},{1,9},{10,2},{2,10},{11,3},{3,11},{12,4},{4,12},... | collective-permute-start | bytes 98312 | tf_op jit(solution)/shard_map/ppermute | solution.py:161
  2.1 10.6 %collective-permute-start.3 = (s32[2,8,384]{2,1,0:T(8,128)S(1)}, s32[2,8,384]{2,1,0:T(8,128)S(1)}, u32[]{:S(2)}, u32[]{:S(2)}) collective-permute-start(s32[2,8,384]{2,1,0:T(8,128)S(1)} %pad_add_fusion.1.words), channel_id=1, source_target_pairs={{4,0},{0,4},{5,1},{1,5},{6,2},{2,6},{7,3},{3,7},{12,8},{8,12},{13,... | collective-permute-start | bytes 73736 | tf_op jit(solution)/shard_map/ppermute | solution.py:161
  9.3 9.5 %collective-permute-start.5 = (s32[2,8,384]{2,1,0:T(8,128)S(1)}, s32[2,8,384]{2,1,0:T(8,128)S(1)}, u32[]{:S(2)}, u32[]{:S(2)}) collective-permute-start(s32[2,8,384]{2,1,0:T(8,128)S(1)} %pad_add_fusion.1.words), channel_id=1, source_target_pairs={{1,0},{2,1},{3,2},{0,3},{5,4},{6,5},{7,6},{4,7},{9,8},{10,9},{11,1... | collective-permute-start | bytes 73736 | tf_op jit(solution)/shard_map/ppermute | solution.py:161
  9.9 10.8 %collective-permute-start.4 = (s32[2,8,384]{2,1,0:T(8,128)S(1)}, s32[2,8,384]{2,1,0:T(8,128)S(1)}, u32[]{:S(2)}, u32[]{:S(2)}) collective-permute-start(s32[2,8,384]{2,1,0:T(8,128)S(1)} %pad_add_fusion.1.words), channel_id=1, source_target_pairs={{3,0},{0,1},{1,2},{2,3},{7,4},{4,5},{5,6},{6,7},{11,8},{8,9},{9,10... | collective-permute-start | bytes 73736 | tf_op jit(solution)/shard_map/ppermute | solution.py:161
  12.7 8.6 %collective-permute-start.8 = (s32[2,8,384]{2,1,0:T(8,128)S(1)}, s32[2,8,384]{2,1,0:T(8,128)S(1)}, u32[]{:S(2)}, u32[]{:S(2)}) collective-permute-start(s32[2,8,384]{2,1,0:T(8,128)S(1)} %collective-permute-done.3.words), channel_id=1, source_target_pairs={{1,0},{2,1},{3,2},{0,3},{5,4},{6,5},{7,6},{4,7},{9,8},{10,9},{11,1... | collective-permute-start | bytes 73736 | tf_op jit(solution)/shard_map/ppermute | solution.py:161
  14.1 7.9 %collective-permute-start.7 = (s32[2,8,384]{2,1,0:T(8,128)S(1)}, s32[2,8,384]{2,1,0:T(8,128)S(1)}, u32[]{:S(2)}, u32[]{:S(2)}) collective-permute-start(s32[2,8,384]{2,1,0:T(8,128)S(1)} %collective-permute-done.3.words), channel_id=1, source_target_pairs={{2,0},{3,1},{0,2},{1,3},{6,4},{7,5},{4,6},{5,7},{10,8},{11,9},{8,1... | collective-permute-start | bytes 73736 | tf_op jit(solution)/shard_map/ppermute | solution.py:161
  16.2 6.5 %collective-permute-start.6 = (s32[2,8,384]{2,1,0:T(8,128)S(1)}, s32[2,8,384]{2,1,0:T(8,128)S(1)}, u32[]{:S(2)}, u32[]{:S(2)}) collective-permute-start(s32[2,8,384]{2,1,0:T(8,128)S(1)} %collective-permute-done.3.words), channel_id=1, source_target_pairs={{3,0},{0,1},{1,2},{2,3},{7,4},{4,5},{5,6},{6,7},{11,8},{8,9},{9,10... | collective-permute-start | bytes 73736 | tf_op jit(solution)/shard_map/ppermute | solution.py:161
  18.8 5.3 %collective-permute-start.2 = (s32[2,8,384]{2,1,0:T(8,128)S(1)}, s32[2,8,384]{2,1,0:T(8,128)S(1)}, u32[]{:S(2)}, u32[]{:S(2)}) collective-permute-start(s32[2,8,384]{2,1,0:T(8,128)S(1)} %pad_add_fusion.1.words), channel_id=1, source_target_pairs={{2,0},{3,1},{0,2},{1,3},{6,4},{7,5},{4,6},{5,7},{10,8},{11,9},{8,1... | collective-permute-start | bytes 73736 | tf_op jit(solution)/shard_map/ppermute | solution.py:161

commit v10 on v8

--- a/solution.py
+++ b/solution.py
@@ -116,40 +116,37 @@
                 out[place + pair, r * 8 : (r + 1) * 8, p * LANES : (p + 1) * LANES] = value
 
 
-def prepare(own, other, words, tab, near, strip):
-    filter_kernel(own, other, tab, strip)
-    project_rows(tab, words, near, 0)
-
-
-def early_kernel(own, other, words, tab, near, strip):
+def early_kernel(own, other, tab, strip):
     @pl.when(lax.axis_index("z_hi") == 0)
     def _():
-        prepare(own, other, words, tab, near, strip)
-
-
-def late_kernel(own, other, words, tab_early, near_early, tab, near, strip):
+        filter_kernel(own, other, tab, strip)
+
+
+def late_kernel(own, other, words, tab_early, tab, near, strip):
     early = lax.axis_index("z_hi") == 0
 
     @pl.when(early)
     def _():
         tab[...] = tab_early[...]
-        near[...] = near_early[...]
 
     @pl.when(jnp.logical_not(early))
     def _():
-        prepare(own, other, words, tab, near, strip)
-
-
-def prepared(kernel, operands):
+        filter_kernel(own, other, tab, strip)
+
+    project_rows(tab, words, near, 0)
+
+
+def prepared(kernel, outs, operands):
     rows, bins = operands[0].shape
+    shapes = (
+        jax.ShapeDtypeStruct((2 * rows, bins), jnp.float32),
+        jax.ShapeDtypeStruct((2, 16, 512), jnp.bfloat16),
+    )
     return pl.pallas_call(
         kernel,
-        out_shape=(
-            jax.ShapeDtypeStruct((2 * rows, bins), jnp.float32),
-            jax.ShapeDtypeStruct((2, 16, 512), jnp.bfloat16),
-        ),
+        out_shape=shapes[:outs],
         in_specs=[VMEM] * len(operands),
-        out_specs=(VMEM, VMEM),
+        out_specs=(VMEM,) * outs,
         scratch_shapes=[pltpu.VMEM((LANES, 2 * bins - LANES), jnp.bfloat16)],
         compiler_params=pltpu.CompilerParams(vmem_limit_bytes=8 * 2**20),
     )(*operands)
@@ -166,7 +163,7 @@
     parts, out = refs[:-1], refs[-1]
     x, z_high = lax.axis_index("x"), lax.axis_index("z_hi")
     places = [
-        8 * (1 - z_high if far else z_high) + 2 * ((x + step) & 3) for far, step in ORDER
+        8 * (1 - z_high if far else z_high) + 2 * (x ^ step) for far, step in ORDER
     ]
     for place, part in zip(places, parts):
         out[pl.ds(place, 2)] = part[...]
@@ -184,7 +181,7 @@
 
 
 def permuted(array, axis, step, size):
-    return lax.ppermute(array, axis, [((i + step) % size, i) for i in range(size)])
+    return lax.ppermute(array, axis, [(i ^ step, i) for i in range(size)])
 
 
 def image(sinogram, detector_coord):
@@ -199,9 +196,9 @@
     other = permuted(own, "z_hi", 1, 2)
 
     sinos = [sinogram, permuted(sinogram, "core", 1, 2)]
-    operands = [sino.reshape(slices * angles, bins) for sino in sinos] + [own]
-    early = prepared(early_kernel, operands)
-    tab, near_0 = prepared(late_kernel, [*operands, *early])
+    rows = [sino.reshape(slices * angles, bins) for sino in sinos]
+    (early,) = prepared(early_kernel, 1, rows)
+    tab, near_0 = prepared(late_kernel, 2, [*rows, own, early])
     near = [own] + [permuted(own, "x", s, 4) for s in (1, 2, 3)]
     other, near_0 = lax.optimization_barrier((other, near_0))
     far = [other] + [permuted(other, "x", s, 4) for s in (1, 2, 3)]

time: 40 us -> 39.8 us (level); the launches traced: 39.3 us -> 39.5 us
  no operation moved by 1% of the time
where the time goes in v10:
time: 39.8 us; the launch traced here: 39.5 us
  starting transfers between devices  15.6 us (39%)
  blocking collectives  15.2 us (38%)
  Pallas kernels  5.86 us (15%)
  other arithmetic  1.42 us (4%)
  local copies, waits for them, and re-layouts  0.71 us (2%)
  waiting for transfers between devices  0.56 us (1%)
    ppermute x9, starting transfers between devices, permuted(): return lax.ppermute(array, axis, [(i ^ step, i) for i in range(size)])  15.6 us
    all_to_all x1, blocking collectives, image(): parts = lax.all_to_all(partial, ('y', 'z_lo'), 0, 0, tiled=True)  15.2 us
    pallas_call x7, Pallas kernels, project(): pl.pallas_call(kernel, out_shape=jax.ShapeDtypeStruct((owners, 16, 512),...  4.56 us
    pallas_call x2, Pallas kernels, prepared(): pl.pallas_call(kernel, out_shape=shapes[:outs], in_specs=[VMEM] * len(ope...  1.3 us
  transfers between devices with their start and end apart: 9, of which 1 were waited for; matrix products, arithmetic and copies ran while one was open for 0% of the time, Pallas kernels for 13%

profile of v10, /device:TPU:2, one launch (start us, length us, event | category | flops | bytes accessed | tf_op | source)
XLA Modules:
  0.0 39.5 jit_solution(3864359556861077606)
XLA Ops:
  0.0 0.8 %shift-left_or_fusion.2 = (s32[2,8,128]{2,1,0:T(8,128)S(1)}, s32[2,8,128]{2,1,0:T(8,128)S(1)}, s32[2,8,128]{2,1,0:T(8,128)S(1)}) fusion(s32[2,8,512]{2,1,0:T(8,128)} %param.3), kind=kLoop, calls=%fused_computation.8 | loop fusion | flops 26624 | bytes 57344 | tf_op jit(solution)/shard_map/or | solution.py:71
  0.8 0.0 copy-start
  0.8 0.1 collective-permute-start.1
  0.9 0.6 %copy-done = bf16[8,2,1024]{2,1,0:T(2,128)(2,1)S(1)} copy-done((bf16[8,2,1024]{2,1,0:T(2,128)(2,1)S(1)}, bf16[8,2,1024]{2,1,0:T(2,128)(2,1)}, u32[]{:S(2)}) %copy-start) | copy-done | bytes 32792
  1.6 0.5 %collective-permute-done.1 = s32[8,384]{1,0:T(8,128)S(1)} collective-permute-done((s32[8,384]{1,0:T(8,128)S(1)}, s32[8,384]{1,0:T(8,128)S(1)}, u32[]{:S(2)}, u32[]{:S(2)}) %collective-permute-start.1) | collective-permute-done | bytes 12320 | tf_op jit(solution)/shard_map/ppermute | solution.py:184
  2.1 7.2 %collective-permute-start.2 = (s32[2,8,384]{2,1,0:T(8,128)S(1)}, s32[2,8,384]{2,1,0:T(8,128)S(1)}, u32[]{:S(2)}, u32[]{:S(2)}) collective-permute-start(s32[2,8,384]{2,1,0:T(8,128)S(1)} %pad_add_fusion.1.words), channel_id=1, source_target_pairs={{4,0},{0,4},{5,1},{1,5},{6,2},{2,6},{7,3},{3,7},{12,8},{8,12},{13,... | collective-permute-start | bytes 73736 | tf_op jit(solution)/shard_map/ppermute | solution.py:184
  9.3 0.5 %collective-permute-start.6 = (s32[2,8,384]{2,1,0:T(8,128)S(1)}, s32[2,8,384]{2,1,0:T(8,128)S(1)}, u32[]{:S(2)}, u32[]{:S(2)}) collective-permute-start(s32[2,8,384]{2,1,0:T(8,128)S(1)} %pad_add_fusion.1.words), channel_id=1, source_target_pairs={{1,0},{0,1},{3,2},{2,3},{5,4},{4,5},{7,6},{6,7},{9,8},{8,9},{11,10... | collective-permute-start | bytes 73736 | tf_op jit(solution)/shard_map/ppermute | solution.py:184
  9.9 2.5 %collective-permute-start.5 = (s32[2,8,384]{2,1,0:T(8,128)S(1)}, s32[2,8,384]{2,1,0:T(8,128)S(1)}, u32[]{:S(2)}, u32[]{:S(2)}) collective-permute-start(s32[2,8,384]{2,1,0:T(8,128)S(1)} %pad_add_fusion.1.words), channel_id=1, source_target_pairs={{2,0},{3,1},{0,2},{1,3},{6,4},{7,5},{4,6},{5,7},{10,8},{11,9},{8,1... | collective-permute-start | bytes 73736 | tf_op jit(solution)/shard_map/ppermute | solution.py:184
  12.4 0.5 %collective-permute-start.4 = (s32[2,8,384]{2,1,0:T(8,128)S(1)}, s32[2,8,384]{2,1,0:T(8,128)S(1)}, u32[]{:S(2)}, u32[]{:S(2)}) collective-permute-start(s32[2,8,384]{2,1,0:T(8,128)S(1)} %pad_add_fusion.1.words), channel_id=1, source_target_pairs={{3,0},{2,1},{1,2},{0,3},{7,4},{6,5},{5,6},{4,7},{11,8},{10,9},{9,1... | collective-permute-start | bytes 73736 | tf_op jit(solution)/shard_map/ppermute | solution.py:184
  12.9 0.0 collective-permute-done
  12.9 0.6 %shard_map.28.tab_early = f32[32,1024]{1,0:T(8,128)S(1)} custom-call(bf16[16,1024]{1,0:T(8,128)(2,1)S(1)} %reshape.18.own, bf16[16,1024]{1,0:T(8,128)(2,1)S(1)} %reshape.19.other), custom_call_target="tpu_custom_call" | custom-call | tf_op jit(solution)/shard_map/pallas_call | solution.py:145
  13.5 0.7 %shard_map.29 = (f32[32,1024]{1,0:T(8,128)S(1)}, bf16[2,16,512]{2,1,0:T(8,128)(2,1)S(1)}) custom-call(bf16[16,1024]{1,0:T(8,128)(2,1)S(1)} %reshape.18.own, bf16[16,1024]{1,0:T(8,128)(2,1)S(1)} %reshape.19.other, s32[2,8,384]{2,1,0:T(8,128)S(1)} %pad_add_fusion.1.words, f32[32,1024]{1,0:T(8,128)S(1)} %shard_map.28.tab_early), custom_call_target="tpu_custom_call" | custom-call | tf_op jit(solution)/shard_map/pallas_call | solution.py:145
  14.2 3.4 %collective-permute-start.8 = (s32[2,8,384]{2,1,0:T(8,128)S(1)}, s32[2,8,384]{2,1,0:T(8,128)S(1)}, u32[]{:S(2)}, u32[]{:S(2)}) collective-permute-start(s32[2,8,384]{2,1,0:T(8,128)S(1)} %collective-permute-done.2.words), channel_id=1, source_target_pairs={{2,0},{3,1},{0,2},{1,3},{6,4},{7,5},{4,6},{5,7},{10,8},{11,9},{8,1... | collective-permute-start | bytes 73736 | tf_op jit(solution)/shard_map/ppermute | solution.py:184
  17.7 1.4 %collective-permute-start.3 = (s32[2,8,384]{2,1,0:T(8,128)S(1)}, s32[2,8,384]{2,1,0:T(8,128)S(1)}, u32[]{:S(2)}, u32[]{:S(2)}) collective-permute-start(s32[2,8,384]{2,1,0:T(8,128)S(1)} %collective-permute-done.2.words), channel_id=1, source_target_pairs={{1,0},{0,1},{3,2},{2,3},{5,4},{4,5},{7,6},{6,7},{9,8},{8,9},{11,10... | collective-permute-start | bytes 73736 | tf_op jit(solution)/shard_map/ppermute | solution.py:184
  19.0 0.6 %shard_map.33.refs_4_ = bf16[2,16,512]{2,1,0:T(8,128)(2,1)S(1)} custom-call(f32[32,1024]{1,0:T(8,128)S(1)} %get-tuple-element.9.tab, s32[2,8,384]{2,1,0:T(8,128)S(1)} %collective-permute-done.2.words), custom_call_target="tpu_custom_call" | custom-call | tf_op jit(solution)/shard_map/pallas_call | solution.py:174
  19.7 0.7 %shard_map.32.refs_3_ = bf16[2,16,512]{2,1,0:T(8,128)(2,1)S(1)} custom-call(f32[32,1024]{1,0:T(8,128)S(1)} %get-tuple-element.9.tab, s32[2,8,384]{2,1,0:T(8,128)S(1)} %collective-permute-done.6.words), custom_call_target="tpu_custom_call" | custom-call | tf_op jit(solution)/shard_map/pallas_call | solution.py:174
  20.3 0.7 %shard_map.31.refs_2_ = bf16[2,16,512]{2,1,0:T(8,128)(2,1)S(1)} custom-call(f32[32,1024]{1,0:T(8,128)S(1)} %get-tuple-element.9.tab, s32[2,8,384]{2,1,0:T(8,128)S(1)} %collective-permute-done.5.words), custom_call_target="tpu_custom_call" | custom-call | tf_op jit(solution)/shard_map/pallas_call | solution.py:174
  21.0 0.7 %shard_map.30.refs_1_ = bf16[2,16,512]{2,1,0:T(8,128)(2,1)S(1)} custom-call(f32[32,1024]{1,0:T(8,128)S(1)} %get-tuple-element.9.tab, s32[2,8,384]{2,1,0:T(8,128)S(1)} %collective-permute-done.4.words), custom_call_target="tpu_custom_call" | custom-call | tf_op jit(solution)/shard_map/pallas_call | solution.py:174
  21.7 0.0 collective-permute-done.8.words
  21.7 0.7 %shard_map.35.refs_6_ = bf16[2,16,512]{2,1,0:T(8,128)(2,1)S(1)} custom-call(f32[32,1024]{1,0:T(8,128)S(1)} %get-tuple-element.9.tab, s32[2,8,384]{2,1,0:T(8,128)S(1)} %collective-permute-done.8.words), custom_call_target="tpu_custom_call" | custom-call | tf_op jit(solution)/shard_map/pallas_call | solution.py:174
  22.3 0.7 %shard_map.34.refs_5_ = bf16[2,16,512]{2,1,0:T(8,128)(2,1)S(1)} custom-call(f32[32,1024]{1,0:T(8,128)S(1)} %get-tuple-element.9.tab, s32[2,8,384]{2,1,0:T(8,128)S(1)} %collective-permute-done.7.words), custom_call_target="tpu_custom_call" | custom-call | tf_op jit(solution)/shard_map/pallas_call | solution.py:174
  23.0 0.7 %shard_map.36 = bf16[16,16,512]{2,1,0:T(8,128)(2,1)S(1)} custom-call(f32[32,1024]{1,0:T(8,128)S(1)} %get-tuple-element.9.tab, s32[2,8,384]{2,1,0:T(8,128)S(1)} %collective-permute-done.3.words, bf16[2,16,512]{2,1,0:T(8,128)(2,1)S(1)} %get-tuple-element.12.refs_0_, bf16[2,16,512]{2,1,0:T(8,128)(2,1)S(1)} %shard_map.30.refs_1_, ...), custom_call_target="tpu_custom_call" | custom-call | tf_op jit(solution)/shard_map/pallas_call | solution.py:174
  23.7 15.2 %all_to_all.5 = bf16[16,16,512]{2,1,0:T(8,128)(2,1)S(1)} all-to-all(bf16[16,16,512]{2,1,0:T(8,128)(2,1)S(1)} %shard_map.36), channel_id=1, replica_groups=mesh['y'=4,'z_lo'=4,'core'=2,'z_hi'=2,'x'=4] {'y','z_lo'}, dimensions={0} | all-to-all | bytes 524288 | tf_op jit(solution)/shard_map/all_to_all | solution.py:209
  38.9 0.6 %multiply_bitcast_fusion = f32[2,8,512]{2,1,0:T(8,128)} fusion(f32[16,512]{1,0:T(8,128)S(1)} %convert_reduce_fusion), kind=kLoop, calls=%fused_computation.1 | loop fusion | flops 8192 | bytes 65536 | tf_op jit(solution)/shard_map/mul | solution.py:211
  (17 shorter events, 0.2 us)
Async XLA Ops:
  0.8 0.8 %copy-start = (bf16[8,2,1024]{2,1,0:T(2,128)(2,1)S(1)}, bf16[8,2,1024]{2,1,0:T(2,128)(2,1)}, u32[]{:S(2)}) copy-start(bf16[8,2,1024]{2,1,0:T(2,128)(2,1)} %param.2) | copy-start | bytes 98308
  0.8 1.3 %collective-permute-start.1 = (s32[8,384]{1,0:T(8,128)S(1)}, s32[8,384]{1,0:T(8,128)S(1)}, u32[]{:S(2)}, u32[]{:S(2)}) collective-permute-start(s32[8,384]{1,0:T(8,128)S(1)} %reshape.21), channel_id=1, source_target_pairs={{8,0},{0,8},{9,1},{1,9},{10,2},{2,10},{11,3},{3,11},{12,4},{4,12},... | collective-permute-start | bytes 36872 | tf_op jit(solution)/shard_map/ppermute | solution.py:184
  1.5 11.4 %collective-permute-start = (bf16[8,2,1024]{2,1,0:T(2,128)(2,1)S(1)}, bf16[8,2,1024]{2,1,0:T(2,128)(2,1)S(1)}, u32[]{:S(2)}, u32[]{:S(2)}) collective-permute-start(bf16[8,2,1024]{2,1,0:T(2,128)(2,1)S(1)} %copy-done), channel_id=1, source_target_pairs={{8,0},{0,8},{9,1},{1,9},{10,2},{2,10},{11,3},{3,11},{12,4},{4,12},... | collective-permute-start | bytes 98312 | tf_op jit(solution)/shard_map/ppermute | solution.py:184
  2.1 12.1 %collective-permute-start.2 = (s32[2,8,384]{2,1,0:T(8,128)S(1)}, s32[2,8,384]{2,1,0:T(8,128)S(1)}, u32[]{:S(2)}, u32[]{:S(2)}) collective-permute-start(s32[2,8,384]{2,1,0:T(8,128)S(1)} %pad_add_fusion.1.words), channel_id=1, source_target_pairs={{4,0},{0,4},{5,1},{1,5},{6,2},{2,6},{7,3},{3,7},{12,8},{8,12},{13,... | collective-permute-start | bytes 73736 | tf_op jit(solution)/shard_map/ppermute | solution.py:184
  9.3 8.4 %collective-permute-start.6 = (s32[2,8,384]{2,1,0:T(8,128)S(1)}, s32[2,8,384]{2,1,0:T(8,128)S(1)}, u32[]{:S(2)}, u32[]{:S(2)}) collective-permute-start(s32[2,8,384]{2,1,0:T(8,128)S(1)} %pad_add_fusion.1.words), channel_id=1, source_target_pairs={{1,0},{0,1},{3,2},{2,3},{5,4},{4,5},{7,6},{6,7},{9,8},{8,9},{11,10... | collective-permute-start | bytes 73736 | tf_op jit(solution)/shard_map/ppermute | solution.py:184
  9.9 10.5 %collective-permute-start.5 = (s32[2,8,384]{2,1,0:T(8,128)S(1)}, s32[2,8,384]{2,1,0:T(8,128)S(1)}, u32[]{:S(2)}, u32[]{:S(2)}) collective-permute-start(s32[2,8,384]{2,1,0:T(8,128)S(1)} %pad_add_fusion.1.words), channel_id=1, source_target_pairs={{2,0},{3,1},{0,2},{1,3},{6,4},{7,5},{4,6},{5,7},{10,8},{11,9},{8,1... | collective-permute-start | bytes 73736 | tf_op jit(solution)/shard_map/ppermute | solution.py:184
  12.4 8.6 %collective-permute-start.4 = (s32[2,8,384]{2,1,0:T(8,128)S(1)}, s32[2,8,384]{2,1,0:T(8,128)S(1)}, u32[]{:S(2)}, u32[]{:S(2)}) collective-permute-start(s32[2,8,384]{2,1,0:T(8,128)S(1)} %pad_add_fusion.1.words), channel_id=1, source_target_pairs={{3,0},{2,1},{1,2},{0,3},{7,4},{6,5},{5,6},{4,7},{11,8},{10,9},{9,1... | collective-permute-start | bytes 73736 | tf_op jit(solution)/shard_map/ppermute | solution.py:184
  14.2 7.4 %collective-permute-start.8 = (s32[2,8,384]{2,1,0:T(8,128)S(1)}, s32[2,8,384]{2,1,0:T(8,128)S(1)}, u32[]{:S(2)}, u32[]{:S(2)}) collective-permute-start(s32[2,8,384]{2,1,0:T(8,128)S(1)} %collective-permute-done.2.words), channel_id=1, source_target_pairs={{2,0},{3,1},{0,2},{1,3},{6,4},{7,5},{4,6},{5,7},{10,8},{11,9},{8,1... | collective-permute-start | bytes 73736 | tf_op jit(solution)/shard_map/ppermute | solution.py:184
  17.7 4.7 %collective-permute-start.7 = (s32[2,8,384]{2,1,0:T(8,128)S(1)}, s32[2,8,384]{2,1,0:T(8,128)S(1)}, u32[]{:S(2)}, u32[]{:S(2)}) collective-permute-start(s32[2,8,384]{2,1,0:T(8,128)S(1)} %collective-permute-done.2.words), channel_id=1, source_target_pairs={{3,0},{2,1},{1,2},{0,3},{7,4},{6,5},{5,6},{4,7},{11,8},{10,9},{9,1... | collective-permute-start | bytes 73736 | tf_op jit(solution)/shard_map/ppermute | solution.py:184
  17.7 5.3 %collective-permute-start.3 = (s32[2,8,384]{2,1,0:T(8,128)S(1)}, s32[2,8,384]{2,1,0:T(8,128)S(1)}, u32[]{:S(2)}, u32[]{:S(2)}) collective-permute-start(s32[2,8,384]{2,1,0:T(8,128)S(1)} %collective-permute-done.2.words), channel_id=1, source_target_pairs={{1,0},{0,1},{3,2},{2,3},{5,4},{4,5},{7,6},{6,7},{9,8},{8,9},{11,10... | collective-permute-start | bytes 73736 | tf_op jit(solution)/shard_map/ppermute | solution.py:184

commit v11 on v10

--- a/solution.py
+++ b/solution.py
@@ -156,7 +156,7 @@
     project_rows(tab, words, out, 0)
 
 
-ORDER = ((0, 0), (0, 3), (0, 2), (0, 1), (1, 0), (1, 3), (1, 2), (1, 1))
+ORDER = ((0, 0), (0, 3), (0, 1), (1, 0), (1, 3), (1, 1), (0, 2), (1, 2))
 
 
 def last_kernel(tab, words, *refs):
@@ -184,6 +184,12 @@
     return lax.ppermute(array, axis, [(i ^ step, i) for i in range(size)])
 
 
+def along_x(array):
+    three = permuted(array, "x", 3, 4)
+    one = permuted(array, "x", 1, 4)
+    return [array, one, permuted(three, "x", 1, 4), three]
+
+
 def image(sinogram, detector_coord):
     slices, angles, bins = sinogram.shape
     width = detector_coord.shape[2]
@@ -199,13 +205,13 @@
     rows = [sino.reshape(slices * angles, bins) for sino in sinos]
     (early,) = prepared(early_kernel, 1, rows)
     tab, near_0 = prepared(late_kernel, 2, [*rows, own, early])
-    near = [own] + [permuted(own, "x", s, 4) for s in (1, 2, 3)]
     other, near_0 = lax.optimization_barrier((other, near_0))
-    far = [other] + [permuted(other, "x", s, 4) for s in (1, 2, 3)]
+    near, far = along_x(own), along_x(other)
     done = [near_0]
-    done += [project(array_kernel, 2, [tab, near[s]]) for s in (3, 2, 1)]
-    done += [project(array_kernel, 2, [tab, far[s]]) for s in (0, 3, 2)]
-    partial = project(last_kernel, 16, [tab, far[1], *done])
+    done += [project(array_kernel, 2, [tab, near[s]]) for s in (3, 1)]
+    done += [project(array_kernel, 2, [tab, far[s]]) for s in (0, 3, 1)]
+    done.append(project(array_kernel, 2, [tab, near[2]]))
+    partial = project(last_kernel, 16, [tab, far[2], *done])
     parts = lax.all_to_all(partial, ("y", "z_lo"), 0, 0, tiled=True)
     scale = jnp.float32(math.pi / (angles * lax.axis_size(("y", "z_lo", "core"))))
     image_rows = jnp.sum(parts.astype(jnp.float32), axis=0) * scale

time: 39.8 us -> 39.6 us (level)
  no operation moved by 1% of the time
where the time goes in v11:
time: 39.6 us; the launch traced here: 39.3 us
  starting transfers between devices  15.8 us (40%)
  blocking collectives  14.9 us (38%)
  Pallas kernels  5.86 us (15%)
  other arithmetic  1.42 us (4%)
  local copies, waits for them, and re-layouts  0.71 us (2%)
  waiting for transfers between devices  0.56 us (1%)
    ppermute x9, starting transfers between devices, permuted(): return lax.ppermute(array, axis, [(i ^ step, i) for i in range(size)])  15.8 us
    all_to_all x1, blocking collectives, image(): parts = lax.all_to_all(partial, ('y', 'z_lo'), 0, 0, tiled=True)  14.9 us
    pallas_call x7, Pallas kernels, project(): pl.pallas_call(kernel, out_shape=jax.ShapeDtypeStruct((owners, 16, 512),...  4.57 us
    pallas_call x2, Pallas kernels, prepared(): pl.pallas_call(kernel, out_shape=shapes[:outs], in_specs=[VMEM] * len(ope...  1.3 us
  transfers between devices with their start and end apart: 9, of which 1 were waited for; matrix products, arithmetic and copies ran while one was open for 0% of the time, Pallas kernels for 13%

profile of v11, /device:TPU:2, one launch (start us, length us, event | category | flops | bytes accessed | tf_op | source)
XLA Modules:
  0.0 39.3 jit_solution(13954941381997970157)
XLA Ops:
  0.0 0.8 %shift-left_or_fusion.2 = (s32[2,8,128]{2,1,0:T(8,128)S(1)}, s32[2,8,128]{2,1,0:T(8,128)S(1)}, s32[2,8,128]{2,1,0:T(8,128)S(1)}) fusion(s32[2,8,512]{2,1,0:T(8,128)} %param.3), kind=kLoop, calls=%fused_computation.8 | loop fusion | flops 26624 | bytes 57344 | tf_op jit(solution)/shard_map/or | solution.py:71
  0.8 0.0 copy-start
  0.8 0.1 collective-permute-start.1
  0.9 0.6 %copy-done = bf16[8,2,1024]{2,1,0:T(2,128)(2,1)S(1)} copy-done((bf16[8,2,1024]{2,1,0:T(2,128)(2,1)S(1)}, bf16[8,2,1024]{2,1,0:T(2,128)(2,1)}, u32[]{:S(2)}) %copy-start) | copy-done | bytes 32792
  1.6 0.5 %collective-permute-done.1 = s32[8,384]{1,0:T(8,128)S(1)} collective-permute-done((s32[8,384]{1,0:T(8,128)S(1)}, s32[8,384]{1,0:T(8,128)S(1)}, u32[]{:S(2)}, u32[]{:S(2)}) %collective-permute-start.1) | collective-permute-done | bytes 12320 | tf_op jit(solution)/shard_map/ppermute | solution.py:184
  2.1 7.2 %collective-permute-start.2 = (s32[2,8,384]{2,1,0:T(8,128)S(1)}, s32[2,8,384]{2,1,0:T(8,128)S(1)}, u32[]{:S(2)}, u32[]{:S(2)}) collective-permute-start(s32[2,8,384]{2,1,0:T(8,128)S(1)} %pad_add_fusion.1.words), channel_id=1, source_target_pairs={{4,0},{0,4},{5,1},{1,5},{6,2},{2,6},{7,3},{3,7},{12,8},{8,12},{13,... | collective-permute-start | bytes 73736 | tf_op jit(solution)/shard_map/ppermute | solution.py:184
  9.3 1.6 %collective-permute-start.5 = (s32[2,8,384]{2,1,0:T(8,128)S(1)}, s32[2,8,384]{2,1,0:T(8,128)S(1)}, u32[]{:S(2)}, u32[]{:S(2)}) collective-permute-start(s32[2,8,384]{2,1,0:T(8,128)S(1)} %pad_add_fusion.1.words), channel_id=1, source_target_pairs={{3,0},{2,1},{1,2},{0,3},{7,4},{6,5},{5,6},{4,7},{11,8},{10,9},{9,1... | collective-permute-start | bytes 73736 | tf_op jit(solution)/shard_map/ppermute | solution.py:184
  10.9 0.0 collective-permute-done
  10.9 0.6 %shard_map.28.tab_early = f32[32,1024]{1,0:T(8,128)S(1)} custom-call(bf16[16,1024]{1,0:T(8,128)(2,1)S(1)} %reshape.18.own, bf16[16,1024]{1,0:T(8,128)(2,1)S(1)} %reshape.19.other), custom_call_target="tpu_custom_call" | custom-call | tf_op jit(solution)/shard_map/pallas_call | solution.py:145
  11.5 0.7 %shard_map.29 = (f32[32,1024]{1,0:T(8,128)S(1)}, bf16[2,16,512]{2,1,0:T(8,128)(2,1)S(1)}) custom-call(bf16[16,1024]{1,0:T(8,128)(2,1)S(1)} %reshape.18.own, bf16[16,1024]{1,0:T(8,128)(2,1)S(1)} %reshape.19.other, s32[2,8,384]{2,1,0:T(8,128)S(1)} %pad_add_fusion.1.words, f32[32,1024]{1,0:T(8,128)S(1)} %shard_map.28.tab_early), custom_call_target="tpu_custom_call" | custom-call | tf_op jit(solution)/shard_map/pallas_call | solution.py:145
  12.2 0.6 %collective-permute-start.3 = (s32[2,8,384]{2,1,0:T(8,128)S(1)}, s32[2,8,384]{2,1,0:T(8,128)S(1)}, u32[]{:S(2)}, u32[]{:S(2)}) collective-permute-start(s32[2,8,384]{2,1,0:T(8,128)S(1)} %collective-permute-done.2.words), channel_id=1, source_target_pairs={{3,0},{2,1},{1,2},{0,3},{7,4},{6,5},{5,6},{4,7},{11,8},{10,9},{9,1... | collective-permute-start | bytes 73736 | tf_op jit(solution)/shard_map/ppermute | solution.py:184
  12.9 1.7 %collective-permute-start.6 = (s32[2,8,384]{2,1,0:T(8,128)S(1)}, s32[2,8,384]{2,1,0:T(8,128)S(1)}, u32[]{:S(2)}, u32[]{:S(2)}) collective-permute-start(s32[2,8,384]{2,1,0:T(8,128)S(1)} %pad_add_fusion.1.words), channel_id=1, source_target_pairs={{1,0},{0,1},{3,2},{2,3},{5,4},{4,5},{7,6},{6,7},{9,8},{8,9},{11,10... | collective-permute-start | bytes 73736 | tf_op jit(solution)/shard_map/ppermute | solution.py:184
  14.6 0.4 collective-permute-start.8
  15.0 1.7 %collective-permute-start.7 = (s32[2,8,384]{2,1,0:T(8,128)S(1)}, s32[2,8,384]{2,1,0:T(8,128)S(1)}, u32[]{:S(2)}, u32[]{:S(2)}) collective-permute-start(s32[2,8,384]{2,1,0:T(8,128)S(1)} %collective-permute-done.2.words), channel_id=1, source_target_pairs={{1,0},{0,1},{3,2},{2,3},{5,4},{4,5},{7,6},{6,7},{9,8},{8,9},{11,10... | collective-permute-start | bytes 73736 | tf_op jit(solution)/shard_map/ppermute | solution.py:184
  16.6 2.5 %collective-permute-start.4 = (s32[2,8,384]{2,1,0:T(8,128)S(1)}, s32[2,8,384]{2,1,0:T(8,128)S(1)}, u32[]{:S(2)}, u32[]{:S(2)}) collective-permute-start(s32[2,8,384]{2,1,0:T(8,128)S(1)} %collective-permute-done.3.words), channel_id=1, source_target_pairs={{1,0},{0,1},{3,2},{2,3},{5,4},{4,5},{7,6},{6,7},{9,8},{8,9},{11,10... | collective-permute-start | bytes 73736 | tf_op jit(solution)/shard_map/ppermute | solution.py:184
  19.2 0.6 %shard_map.32.refs_3_ = bf16[2,16,512]{2,1,0:T(8,128)(2,1)S(1)} custom-call(f32[32,1024]{1,0:T(8,128)S(1)} %get-tuple-element.9.tab, s32[2,8,384]{2,1,0:T(8,128)S(1)} %collective-permute-done.2.words), custom_call_target="tpu_custom_call" | custom-call | tf_op jit(solution)/shard_map/pallas_call | solution.py:174
  19.8 0.7 %shard_map.30.refs_1_ = bf16[2,16,512]{2,1,0:T(8,128)(2,1)S(1)} custom-call(f32[32,1024]{1,0:T(8,128)S(1)} %get-tuple-element.9.tab, s32[2,8,384]{2,1,0:T(8,128)S(1)} %collective-permute-done.5.words), custom_call_target="tpu_custom_call" | custom-call | tf_op jit(solution)/shard_map/pallas_call | solution.py:174
  20.5 0.7 %shard_map.31.refs_2_ = bf16[2,16,512]{2,1,0:T(8,128)(2,1)S(1)} custom-call(f32[32,1024]{1,0:T(8,128)S(1)} %get-tuple-element.9.tab, s32[2,8,384]{2,1,0:T(8,128)S(1)} %collective-permute-done.6.words), custom_call_target="tpu_custom_call" | custom-call | tf_op jit(solution)/shard_map/pallas_call | solution.py:174
  21.1 0.7 %shard_map.33.refs_4_ = bf16[2,16,512]{2,1,0:T(8,128)(2,1)S(1)} custom-call(f32[32,1024]{1,0:T(8,128)S(1)} %get-tuple-element.9.tab, s32[2,8,384]{2,1,0:T(8,128)S(1)} %collective-permute-done.3.words), custom_call_target="tpu_custom_call" | custom-call | tf_op jit(solution)/shard_map/pallas_call | solution.py:174
  21.8 0.7 %shard_map.35.refs_6_ = bf16[2,16,512]{2,1,0:T(8,128)(2,1)S(1)} custom-call(f32[32,1024]{1,0:T(8,128)S(1)} %get-tuple-element.9.tab, s32[2,8,384]{2,1,0:T(8,128)S(1)} %collective-permute-done.8.words), custom_call_target="tpu_custom_call" | custom-call | tf_op jit(solution)/shard_map/pallas_call | solution.py:174
  22.5 0.7 %shard_map.34.refs_5_ = bf16[2,16,512]{2,1,0:T(8,128)(2,1)S(1)} custom-call(f32[32,1024]{1,0:T(8,128)S(1)} %get-tuple-element.9.tab, s32[2,8,384]{2,1,0:T(8,128)S(1)} %collective-permute-done.7.words), custom_call_target="tpu_custom_call" | custom-call | tf_op jit(solution)/shard_map/pallas_call | solution.py:174
  23.1 0.7 %shard_map.36 = bf16[16,16,512]{2,1,0:T(8,128)(2,1)S(1)} custom-call(f32[32,1024]{1,0:T(8,128)S(1)} %get-tuple-element.9.tab, s32[2,8,384]{2,1,0:T(8,128)S(1)} %collective-permute-done.4.words, bf16[2,16,512]{2,1,0:T(8,128)(2,1)S(1)} %get-tuple-element.12.refs_0_, bf16[2,16,512]{2,1,0:T(8,128)(2,1)S(1)} %shard_map.30.refs_1_, ...), custom_call_target="tpu_custom_call" | custom-call | tf_op jit(solution)/shard_map/pallas_call | solution.py:174
  23.8 14.9 %all_to_all.5 = bf16[16,16,512]{2,1,0:T(8,128)(2,1)S(1)} all-to-all(bf16[16,16,512]{2,1,0:T(8,128)(2,1)S(1)} %shard_map.36), channel_id=1, replica_groups=mesh['y'=4,'z_lo'=4,'core'=2,'z_hi'=2,'x'=4] {'y','z_lo'}, dimensions={0} | all-to-all | bytes 524288 | tf_op jit(solution)/shard_map/all_to_all | solution.py:215
  38.7 0.6 %multiply_bitcast_fusion = f32[2,8,512]{2,1,0:T(8,128)} fusion(f32[16,512]{1,0:T(8,128)S(1)} %convert_reduce_fusion), kind=kLoop, calls=%fused_computation.1 | loop fusion | flops 8192 | bytes 65536 | tf_op jit(solution)/shard_map/mul | solution.py:217
  (17 shorter events, 0.2 us)
Async XLA Ops:
  0.8 0.8 %copy-start = (bf16[8,2,1024]{2,1,0:T(2,128)(2,1)S(1)}, bf16[8,2,1024]{2,1,0:T(2,128)(2,1)}, u32[]{:S(2)}) copy-start(bf16[8,2,1024]{2,1,0:T(2,128)(2,1)} %param.2) | copy-start | bytes 98308
  0.8 1.3 %collective-permute-start.1 = (s32[8,384]{1,0:T(8,128)S(1)}, s32[8,384]{1,0:T(8,128)S(1)}, u32[]{:S(2)}, u32[]{:S(2)}) collective-permute-start(s32[8,384]{1,0:T(8,128)S(1)} %reshape.21), channel_id=1, source_target_pairs={{8,0},{0,8},{9,1},{1,9},{10,2},{2,10},{11,3},{3,11},{12,4},{4,12},... | collective-permute-start | bytes 36872 | tf_op jit(solution)/shard_map/ppermute | solution.py:184
  1.5 9.4 %collective-permute-start = (bf16[8,2,1024]{2,1,0:T(2,128)(2,1)S(1)}, bf16[8,2,1024]{2,1,0:T(2,128)(2,1)S(1)}, u32[]{:S(2)}, u32[]{:S(2)}) collective-permute-start(bf16[8,2,1024]{2,1,0:T(2,128)(2,1)S(1)} %copy-done), channel_id=1, source_target_pairs={{8,0},{0,8},{9,1},{1,9},{10,2},{2,10},{11,3},{3,11},{12,4},{4,12},... | collective-permute-start | bytes 98312 | tf_op jit(solution)/shard_map/ppermute | solution.py:184
  2.1 10.1 %collective-permute-start.2 = (s32[2,8,384]{2,1,0:T(8,128)S(1)}, s32[2,8,384]{2,1,0:T(8,128)S(1)}, u32[]{:S(2)}, u32[]{:S(2)}) collective-permute-start(s32[2,8,384]{2,1,0:T(8,128)S(1)} %pad_add_fusion.1.words), channel_id=1, source_target_pairs={{4,0},{0,4},{5,1},{1,5},{6,2},{2,6},{7,3},{3,7},{12,8},{8,12},{13,... | collective-permute-start | bytes 73736 | tf_op jit(solution)/shard_map/ppermute | solution.py:184
  9.3 5.3 %collective-permute-start.5 = (s32[2,8,384]{2,1,0:T(8,128)S(1)}, s32[2,8,384]{2,1,0:T(8,128)S(1)}, u32[]{:S(2)}, u32[]{:S(2)}) collective-permute-start(s32[2,8,384]{2,1,0:T(8,128)S(1)} %pad_add_fusion.1.words), channel_id=1, source_target_pairs={{3,0},{2,1},{1,2},{0,3},{7,4},{6,5},{5,6},{4,7},{11,8},{10,9},{9,1... | collective-permute-start | bytes 73736 | tf_op jit(solution)/shard_map/ppermute | solution.py:184
  12.2 4.4 %collective-permute-start.3 = (s32[2,8,384]{2,1,0:T(8,128)S(1)}, s32[2,8,384]{2,1,0:T(8,128)S(1)}, u32[]{:S(2)}, u32[]{:S(2)}) collective-permute-start(s32[2,8,384]{2,1,0:T(8,128)S(1)} %collective-permute-done.2.words), channel_id=1, source_target_pairs={{3,0},{2,1},{1,2},{0,3},{7,4},{6,5},{5,6},{4,7},{11,8},{10,9},{9,1... | collective-permute-start | bytes 73736 | tf_op jit(solution)/shard_map/ppermute | solution.py:184
  12.9 7.6 %collective-permute-start.6 = (s32[2,8,384]{2,1,0:T(8,128)S(1)}, s32[2,8,384]{2,1,0:T(8,128)S(1)}, u32[]{:S(2)}, u32[]{:S(2)}) collective-permute-start(s32[2,8,384]{2,1,0:T(8,128)S(1)} %pad_add_fusion.1.words), channel_id=1, source_target_pairs={{1,0},{0,1},{3,2},{2,3},{5,4},{4,5},{7,6},{6,7},{9,8},{8,9},{11,10... | collective-permute-start | bytes 73736 | tf_op jit(solution)/shard_map/ppermute | solution.py:184
  14.6 7.2 %collective-permute-start.8 = (s32[2,8,384]{2,1,0:T(8,128)S(1)}, s32[2,8,384]{2,1,0:T(8,128)S(1)}, u32[]{:S(2)}, u32[]{:S(2)}) collective-permute-start(s32[2,8,384]{2,1,0:T(8,128)S(1)} %collective-permute-done.5.words), channel_id=1, source_target_pairs={{1,0},{0,1},{3,2},{2,3},{5,4},{4,5},{7,6},{6,7},{9,8},{8,9},{11,10... | collective-permute-start | bytes 73736 | tf_op jit(solution)/shard_map/ppermute | solution.py:184
  15.0 7.5 %collective-permute-start.7 = (s32[2,8,384]{2,1,0:T(8,128)S(1)}, s32[2,8,384]{2,1,0:T(8,128)S(1)}, u32[]{:S(2)}, u32[]{:S(2)}) collective-permute-start(s32[2,8,384]{2,1,0:T(8,128)S(1)} %collective-permute-done.2.words), channel_id=1, source_target_pairs={{1,0},{0,1},{3,2},{2,3},{5,4},{4,5},{7,6},{6,7},{9,8},{8,9},{11,10... | collective-permute-start | bytes 73736 | tf_op jit(solution)/shard_map/ppermute | solution.py:184
  16.6 6.5 %collective-permute-start.4 = (s32[2,8,384]{2,1,0:T(8,128)S(1)}, s32[2,8,384]{2,1,0:T(8,128)S(1)}, u32[]{:S(2)}, u32[]{:S(2)}) collective-permute-start(s32[2,8,384]{2,1,0:T(8,128)S(1)} %collective-permute-done.3.words), channel_id=1, source_target_pairs={{1,0},{0,1},{3,2},{2,3},{5,4},{4,5},{7,6},{6,7},{9,8},{8,9},{11,10... | collective-permute-start | bytes 73736 | tf_op jit(solution)/shard_map/ppermute | solution.py:184

commit v12 on v10

--- a/solution.py
+++ b/solution.py
@@ -156,7 +156,7 @@
     project_rows(tab, words, out, 0)
 
 
-ORDER = ((0, 0), (0, 3), (0, 2), (0, 1), (1, 0), (1, 3), (1, 2), (1, 1))
+ORDER = ((0, 0), (0, 3), (0, 1), (1, 0), (1, 2), (1, 3), (1, 1), (0, 2))
 
 
 def last_kernel(tab, words, *refs):
@@ -199,13 +199,14 @@
     rows = [sino.reshape(slices * angles, bins) for sino in sinos]
     (early,) = prepared(early_kernel, 1, rows)
     tab, near_0 = prepared(late_kernel, 2, [*rows, own, early])
-    near = [own] + [permuted(own, "x", s, 4) for s in (1, 2, 3)]
     other, near_0 = lax.optimization_barrier((other, near_0))
+    near_3, near_1 = (permuted(own, "x", s, 4) for s in (3, 1))
+    near = [own, near_1, permuted(near_3, "x", 1, 4), near_3]
     far = [other] + [permuted(other, "x", s, 4) for s in (1, 2, 3)]
     done = [near_0]
-    done += [project(array_kernel, 2, [tab, near[s]]) for s in (3, 2, 1)]
-    done += [project(array_kernel, 2, [tab, far[s]]) for s in (0, 3, 2)]
-    partial = project(last_kernel, 16, [tab, far[1], *done])
+    done += [project(array_kernel, 2, [tab, near[s]]) for s in (3, 1)]
+    done += [project(array_kernel, 2, [tab, far[s]]) for s in (0, 2, 3, 1)]
+    partial = project(last_kernel, 16, [tab, near[2], *done])
     parts = lax.all_to_all(partial, ("y", "z_lo"), 0, 0, tiled=True)
     scale = jnp.float32(math.pi / (angles * lax.axis_size(("y", "z_lo", "core"))))
     image_rows = jnp.sum(parts.astype(jnp.float32), axis=0) * scale

time: 39.8 us -> 39.3 us (0.987)
  starting transfers between devices: 15.6 us -> 15.1 us
    ppermute x9, starting transfers between devices: 15.6 us -> 15.1 us  [permuted(): return lax.ppermute(array, axis, [(i ^ step, i) for i in range(size)])]
where the time goes in v12:
time: 39.3 us; the launch traced here: 38.9 us
  blocking collectives  15.2 us (39%)
  starting transfers between devices  15.1 us (38%)
  Pallas kernels  5.86 us (15%)
  other arithmetic  1.42 us (4%)
  local copies, waits for them, and re-layouts  0.71 us (2%)
  waiting for transfers between devices  0.56 us (1%)
    all_to_all x1, blocking collectives, image(): parts = lax.all_to_all(partial, ('y', 'z_lo'), 0, 0, tiled=True)  15.2 us
    ppermute x9, starting transfers between devices, permuted(): return lax.ppermute(array, axis, [(i ^ step, i) for i in range(size)])  15.1 us
    pallas_call x7, Pallas kernels, project(): pl.pallas_call(kernel, out_shape=jax.ShapeDtypeStruct((owners, 16, 512),...  4.57 us
    pallas_call x2, Pallas kernels, prepared(): pl.pallas_call(kernel, out_shape=shapes[:outs], in_specs=[VMEM] * len(ope...  1.3 us
  transfers between devices with their start and end apart: 9, of which 1 were waited for; matrix products, arithmetic and copies ran while one was open for 0% of the time, Pallas kernels for 13%

profile of v12, /device:TPU:2, one launch (start us, length us, event | category | flops | bytes accessed | tf_op | source)
XLA Modules:
  0.0 38.9 jit_solution(5805043437656899263)
XLA Ops:
  0.0 0.8 %shift-left_or_fusion.2 = (s32[2,8,128]{2,1,0:T(8,128)S(1)}, s32[2,8,128]{2,1,0:T(8,128)S(1)}, s32[2,8,128]{2,1,0:T(8,128)S(1)}) fusion(s32[2,8,512]{2,1,0:T(8,128)} %param.3), kind=kLoop, calls=%fused_computation.8 | loop fusion | flops 26624 | bytes 57344 | tf_op jit(solution)/shard_map/or | solution.py:71
  0.8 0.0 copy-start
  0.8 0.1 collective-permute-start.1
  0.9 0.6 %copy-done = bf16[8,2,1024]{2,1,0:T(2,128)(2,1)S(1)} copy-done((bf16[8,2,1024]{2,1,0:T(2,128)(2,1)S(1)}, bf16[8,2,1024]{2,1,0:T(2,128)(2,1)}, u32[]{:S(2)}) %copy-start) | copy-done | bytes 32792
  1.6 0.5 %collective-permute-done.1 = s32[8,384]{1,0:T(8,128)S(1)} collective-permute-done((s32[8,384]{1,0:T(8,128)S(1)}, s32[8,384]{1,0:T(8,128)S(1)}, u32[]{:S(2)}, u32[]{:S(2)}) %collective-permute-start.1) | collective-permute-done | bytes 12320 | tf_op jit(solution)/shard_map/ppermute | solution.py:184
  2.1 7.2 %collective-permute-start.4 = (s32[2,8,384]{2,1,0:T(8,128)S(1)}, s32[2,8,384]{2,1,0:T(8,128)S(1)}, u32[]{:S(2)}, u32[]{:S(2)}) collective-permute-start(s32[2,8,384]{2,1,0:T(8,128)S(1)} %pad_add_fusion.1.words), channel_id=1, source_target_pairs={{4,0},{0,4},{5,1},{1,5},{6,2},{2,6},{7,3},{3,7},{12,8},{8,12},{13,... | collective-permute-start | bytes 73736 | tf_op jit(solution)/shard_map/ppermute | solution.py:184
  9.3 1.5 %collective-permute-start.2 = (s32[2,8,384]{2,1,0:T(8,128)S(1)}, s32[2,8,384]{2,1,0:T(8,128)S(1)}, u32[]{:S(2)}, u32[]{:S(2)}) collective-permute-start(s32[2,8,384]{2,1,0:T(8,128)S(1)} %pad_add_fusion.1.words), channel_id=1, source_target_pairs={{3,0},{2,1},{1,2},{0,3},{7,4},{6,5},{5,6},{4,7},{11,8},{10,9},{9,1... | collective-permute-start | bytes 73736 | tf_op jit(solution)/shard_map/ppermute | solution.py:184
  10.8 1.9 %collective-permute-start.5 = (s32[2,8,384]{2,1,0:T(8,128)S(1)}, s32[2,8,384]{2,1,0:T(8,128)S(1)}, u32[]{:S(2)}, u32[]{:S(2)}) collective-permute-start(s32[2,8,384]{2,1,0:T(8,128)S(1)} %pad_add_fusion.1.words), channel_id=1, source_target_pairs={{1,0},{0,1},{3,2},{2,3},{5,4},{4,5},{7,6},{6,7},{9,8},{8,9},{11,10... | collective-permute-start | bytes 73736 | tf_op jit(solution)/shard_map/ppermute | solution.py:184
  12.7 0.6 %shard_map.28.tab_early = f32[32,1024]{1,0:T(8,128)S(1)} custom-call(bf16[16,1024]{1,0:T(8,128)(2,1)S(1)} %reshape.18.own, bf16[16,1024]{1,0:T(8,128)(2,1)S(1)} %reshape.19.other), custom_call_target="tpu_custom_call" | custom-call | tf_op jit(solution)/shard_map/pallas_call | solution.py:145
  13.4 0.7 %shard_map.29 = (f32[32,1024]{1,0:T(8,128)S(1)}, bf16[2,16,512]{2,1,0:T(8,128)(2,1)S(1)}) custom-call(bf16[16,1024]{1,0:T(8,128)(2,1)S(1)} %reshape.18.own, bf16[16,1024]{1,0:T(8,128)(2,1)S(1)} %reshape.19.other, s32[2,8,384]{2,1,0:T(8,128)S(1)} %pad_add_fusion.1.words, f32[32,1024]{1,0:T(8,128)S(1)} %shard_map.28.tab_early), custom_call_target="tpu_custom_call" | custom-call | tf_op jit(solution)/shard_map/pallas_call | solution.py:145
  14.0 0.3 collective-permute-start.8
  14.4 0.5 %collective-permute-start.7 = (s32[2,8,384]{2,1,0:T(8,128)S(1)}, s32[2,8,384]{2,1,0:T(8,128)S(1)}, u32[]{:S(2)}, u32[]{:S(2)}) collective-permute-start(s32[2,8,384]{2,1,0:T(8,128)S(1)} %collective-permute-done.4.words), channel_id=1, source_target_pairs={{3,0},{2,1},{1,2},{0,3},{7,4},{6,5},{5,6},{4,7},{11,8},{10,9},{9,1... | collective-permute-start | bytes 73736 | tf_op jit(solution)/shard_map/ppermute | solution.py:184
  14.9 3.3 %collective-permute-start.6 = (s32[2,8,384]{2,1,0:T(8,128)S(1)}, s32[2,8,384]{2,1,0:T(8,128)S(1)}, u32[]{:S(2)}, u32[]{:S(2)}) collective-permute-start(s32[2,8,384]{2,1,0:T(8,128)S(1)} %collective-permute-done.4.words), channel_id=1, source_target_pairs={{2,0},{3,1},{0,2},{1,3},{6,4},{7,5},{4,6},{5,7},{10,8},{11,9},{8,1... | collective-permute-start | bytes 73736 | tf_op jit(solution)/shard_map/ppermute | solution.py:184
  18.2 0.0 collective-permute-done.2.words
  18.2 0.2 collective-permute-start.3
  18.5 0.6 %shard_map.32.refs_3_ = bf16[2,16,512]{2,1,0:T(8,128)(2,1)S(1)} custom-call(f32[32,1024]{1,0:T(8,128)S(1)} %get-tuple-element.9.tab, s32[2,8,384]{2,1,0:T(8,128)S(1)} %collective-permute-done.4.words), custom_call_target="tpu_custom_call" | custom-call | tf_op jit(solution)/shard_map/pallas_call | solution.py:174
  19.1 0.7 %shard_map.30.refs_1_ = bf16[2,16,512]{2,1,0:T(8,128)(2,1)S(1)} custom-call(f32[32,1024]{1,0:T(8,128)S(1)} %get-tuple-element.9.tab, s32[2,8,384]{2,1,0:T(8,128)S(1)} %collective-permute-done.2.words), custom_call_target="tpu_custom_call" | custom-call | tf_op jit(solution)/shard_map/pallas_call | solution.py:174
  19.8 0.7 %shard_map.31.refs_2_ = bf16[2,16,512]{2,1,0:T(8,128)(2,1)S(1)} custom-call(f32[32,1024]{1,0:T(8,128)S(1)} %get-tuple-element.9.tab, s32[2,8,384]{2,1,0:T(8,128)S(1)} %collective-permute-done.5.words), custom_call_target="tpu_custom_call" | custom-call | tf_op jit(solution)/shard_map/pallas_call | solution.py:174
  20.4 0.7 %shard_map.35.refs_6_ = bf16[2,16,512]{2,1,0:T(8,128)(2,1)S(1)} custom-call(f32[32,1024]{1,0:T(8,128)S(1)} %get-tuple-element.9.tab, s32[2,8,384]{2,1,0:T(8,128)S(1)} %collective-permute-done.8.words), custom_call_target="tpu_custom_call" | custom-call | tf_op jit(solution)/shard_map/pallas_call | solution.py:174
  21.1 0.7 %shard_map.34.refs_5_ = bf16[2,16,512]{2,1,0:T(8,128)(2,1)S(1)} custom-call(f32[32,1024]{1,0:T(8,128)S(1)} %get-tuple-element.9.tab, s32[2,8,384]{2,1,0:T(8,128)S(1)} %collective-permute-done.7.words), custom_call_target="tpu_custom_call" | custom-call | tf_op jit(solution)/shard_map/pallas_call | solution.py:174
  21.8 0.7 %shard_map.33.refs_4_ = bf16[2,16,512]{2,1,0:T(8,128)(2,1)S(1)} custom-call(f32[32,1024]{1,0:T(8,128)S(1)} %get-tuple-element.9.tab, s32[2,8,384]{2,1,0:T(8,128)S(1)} %collective-permute-done.6.words), custom_call_target="tpu_custom_call" | custom-call | tf_op jit(solution)/shard_map/pallas_call | solution.py:174
  22.4 0.7 %shard_map.36 = bf16[16,16,512]{2,1,0:T(8,128)(2,1)S(1)} custom-call(f32[32,1024]{1,0:T(8,128)S(1)} %get-tuple-element.9.tab, s32[2,8,384]{2,1,0:T(8,128)S(1)} %collective-permute-done.3.words, bf16[2,16,512]{2,1,0:T(8,128)(2,1)S(1)} %get-tuple-element.11.refs_0_, bf16[2,16,512]{2,1,0:T(8,128)(2,1)S(1)} %shard_map.30.refs_1_, ...), custom_call_target="tpu_custom_call" | custom-call | tf_op jit(solution)/shard_map/pallas_call | solution.py:174
  23.1 15.2 %all_to_all.5 = bf16[16,16,512]{2,1,0:T(8,128)(2,1)S(1)} all-to-all(bf16[16,16,512]{2,1,0:T(8,128)(2,1)S(1)} %shard_map.36), channel_id=1, replica_groups=mesh['y'=4,'z_lo'=4,'core'=2,'z_hi'=2,'x'=4] {'y','z_lo'}, dimensions={0} | all-to-all | bytes 524288 | tf_op jit(solution)/shard_map/all_to_all | solution.py:210
  38.3 0.6 %multiply_bitcast_fusion = f32[2,8,512]{2,1,0:T(8,128)} fusion(f32[16,512]{1,0:T(8,128)S(1)} %convert_reduce_fusion), kind=kLoop, calls=%fused_computation.1 | loop fusion | flops 8192 | bytes 65536 | tf_op jit(solution)/shard_map/mul | solution.py:212
  (17 shorter events, 0.2 us)
Async XLA Ops:
  0.8 0.8 %copy-start = (bf16[8,2,1024]{2,1,0:T(2,128)(2,1)S(1)}, bf16[8,2,1024]{2,1,0:T(2,128)(2,1)}, u32[]{:S(2)}) copy-start(bf16[8,2,1024]{2,1,0:T(2,128)(2,1)} %param.2) | copy-start | bytes 98308
  0.8 1.3 %collective-permute-start.1 = (s32[8,384]{1,0:T(8,128)S(1)}, s32[8,384]{1,0:T(8,128)S(1)}, u32[]{:S(2)}, u32[]{:S(2)}) collective-permute-start(s32[8,384]{1,0:T(8,128)S(1)} %reshape.21), channel_id=1, source_target_pairs={{8,0},{0,8},{9,1},{1,9},{10,2},{2,10},{11,3},{3,11},{12,4},{4,12},... | collective-permute-start | bytes 36872 | tf_op jit(solution)/shard_map/ppermute | solution.py:184
  1.5 11.2 %collective-permute-start = (bf16[8,2,1024]{2,1,0:T(2,128)(2,1)S(1)}, bf16[8,2,1024]{2,1,0:T(2,128)(2,1)S(1)}, u32[]{:S(2)}, u32[]{:S(2)}) collective-permute-start(bf16[8,2,1024]{2,1,0:T(2,128)(2,1)S(1)} %copy-done), channel_id=1, source_target_pairs={{8,0},{0,8},{9,1},{1,9},{10,2},{2,10},{11,3},{3,11},{12,4},{4,12},... | collective-permute-start | bytes 98312 | tf_op jit(solution)/shard_map/ppermute | solution.py:184
  2.1 11.9 %collective-permute-start.4 = (s32[2,8,384]{2,1,0:T(8,128)S(1)}, s32[2,8,384]{2,1,0:T(8,128)S(1)}, u32[]{:S(2)}, u32[]{:S(2)}) collective-permute-start(s32[2,8,384]{2,1,0:T(8,128)S(1)} %pad_add_fusion.1.words), channel_id=1, source_target_pairs={{4,0},{0,4},{5,1},{1,5},{6,2},{2,6},{7,3},{3,7},{12,8},{8,12},{13,... | collective-permute-start | bytes 73736 | tf_op jit(solution)/shard_map/ppermute | solution.py:184
  9.3 8.9 %collective-permute-start.2 = (s32[2,8,384]{2,1,0:T(8,128)S(1)}, s32[2,8,384]{2,1,0:T(8,128)S(1)}, u32[]{:S(2)}, u32[]{:S(2)}) collective-permute-start(s32[2,8,384]{2,1,0:T(8,128)S(1)} %pad_add_fusion.1.words), channel_id=1, source_target_pairs={{3,0},{2,1},{1,2},{0,3},{7,4},{6,5},{5,6},{4,7},{11,8},{10,9},{9,1... | collective-permute-start | bytes 73736 | tf_op jit(solution)/shard_map/ppermute | solution.py:184
  10.8 9.0 %collective-permute-start.5 = (s32[2,8,384]{2,1,0:T(8,128)S(1)}, s32[2,8,384]{2,1,0:T(8,128)S(1)}, u32[]{:S(2)}, u32[]{:S(2)}) collective-permute-start(s32[2,8,384]{2,1,0:T(8,128)S(1)} %pad_add_fusion.1.words), channel_id=1, source_target_pairs={{1,0},{0,1},{3,2},{2,3},{5,4},{4,5},{7,6},{6,7},{9,8},{8,9},{11,10... | collective-permute-start | bytes 73736 | tf_op jit(solution)/shard_map/ppermute | solution.py:184
  14.0 6.4 %collective-permute-start.8 = (s32[2,8,384]{2,1,0:T(8,128)S(1)}, s32[2,8,384]{2,1,0:T(8,128)S(1)}, u32[]{:S(2)}, u32[]{:S(2)}) collective-permute-start(s32[2,8,384]{2,1,0:T(8,128)S(1)} %collective-permute-done.4.words), channel_id=1, source_target_pairs={{1,0},{0,1},{3,2},{2,3},{5,4},{4,5},{7,6},{6,7},{9,8},{8,9},{11,10... | collective-permute-start | bytes 73736 | tf_op jit(solution)/shard_map/ppermute | solution.py:184
  14.4 6.7 %collective-permute-start.7 = (s32[2,8,384]{2,1,0:T(8,128)S(1)}, s32[2,8,384]{2,1,0:T(8,128)S(1)}, u32[]{:S(2)}, u32[]{:S(2)}) collective-permute-start(s32[2,8,384]{2,1,0:T(8,128)S(1)} %collective-permute-done.4.words), channel_id=1, source_target_pairs={{3,0},{2,1},{1,2},{0,3},{7,4},{6,5},{5,6},{4,7},{11,8},{10,9},{9,1... | collective-permute-start | bytes 73736 | tf_op jit(solution)/shard_map/ppermute | solution.py:184
  14.9 6.9 %collective-permute-start.6 = (s32[2,8,384]{2,1,0:T(8,128)S(1)}, s32[2,8,384]{2,1,0:T(8,128)S(1)}, u32[]{:S(2)}, u32[]{:S(2)}) collective-permute-start(s32[2,8,384]{2,1,0:T(8,128)S(1)} %collective-permute-done.4.words), channel_id=1, source_target_pairs={{2,0},{3,1},{0,2},{1,3},{6,4},{7,5},{4,6},{5,7},{10,8},{11,9},{8,1... | collective-permute-start | bytes 73736 | tf_op jit(solution)/shard_map/ppermute | solution.py:184
  18.2 4.2 %collective-permute-start.3 = (s32[2,8,384]{2,1,0:T(8,128)S(1)}, s32[2,8,384]{2,1,0:T(8,128)S(1)}, u32[]{:S(2)}, u32[]{:S(2)}) collective-permute-start(s32[2,8,384]{2,1,0:T(8,128)S(1)} %collective-permute-done.2.words), channel_id=1, source_target_pairs={{1,0},{0,1},{3,2},{2,3},{5,4},{4,5},{7,6},{6,7},{9,8},{8,9},{11,10... | collective-permute-start | bytes 73736 | tf_op jit(solution)/shard_map/ppermute | solution.py:184

commit v13 on v11

--- a/solution.py
+++ b/solution.py
@@ -116,23 +116,8 @@
                 out[place + pair, r * 8 : (r + 1) * 8, p * LANES : (p + 1) * LANES] = value
 
 
-def early_kernel(own, other, tab, strip):
-    @pl.when(lax.axis_index("z_hi") == 0)
-    def _():
-        filter_kernel(own, other, tab, strip)
-
-
-def late_kernel(own, other, words, tab_early, tab, near, strip):
-    early = lax.axis_index("z_hi") == 0
-
-    @pl.when(early)
-    def _():
-        tab[...] = tab_early[...]
-
-    @pl.when(jnp.logical_not(early))
-    def _():
-        filter_kernel(own, other, tab, strip)
-
+def prepare_kernel(own, other, words, tab, near, strip):
+    filter_kernel(own, other, tab, strip)
     project_rows(tab, words, near, 0)
 
 
@@ -203,8 +188,7 @@
 
     sinos = [sinogram, permuted(sinogram, "core", 1, 2)]
     rows = [sino.reshape(slices * angles, bins) for sino in sinos]
-    (early,) = prepared(early_kernel, 1, rows)
-    tab, near_0 = prepared(late_kernel, 2, [*rows, own, early])
+    tab, near_0 = prepared(prepare_kernel, 2, [*rows, own])
     other, near_0 = lax.optimization_barrier((other, near_0))
     near, far = along_x(own), along_x(other)
     done = [near_0]

time: 39.6 us -> 39.6 us (level)
    pallas_call x2 -> x1, Pallas kernels: 1.3 us -> 1.3 us  [prepared(): pl.pallas_call(kernel, out_shape=shapes[:outs], in_specs=[VMEM] * len(ope...]
where the time goes in v13:
time: 39.6 us; the launch traced here: 39.3 us
  starting transfers between devices  15.8 us (40%)
  blocking collectives  14.9 us (38%)
  Pallas kernels  5.87 us (15%)
  other arithmetic  1.42 us (4%)
  local copies, waits for them, and re-layouts  0.71 us (2%)
  waiting for transfers between devices  0.56 us (1%)
    ppermute x9, starting transfers between devices, permuted(): return lax.ppermute(array, axis, [(i ^ step, i) for i in range(size)])  15.8 us
    all_to_all x1, blocking collectives, image(): parts = lax.all_to_all(partial, ('y', 'z_lo'), 0, 0, tiled=True)  14.9 us
    pallas_call x7, Pallas kernels, project(): pl.pallas_call(kernel, out_shape=jax.ShapeDtypeStruct((owners, 16, 512),...  4.57 us
    pallas_call x1, Pallas kernels, prepared(): pl.pallas_call(kernel, out_shape=shapes[:outs], in_specs=[VMEM] * len(ope...  1.3 us
  transfers between devices with their start and end apart: 9, of which 1 were waited for; matrix products, arithmetic and copies ran while one was open for 0% of the time, Pallas kernels for 13%

profile of v13, /device:TPU:2, one launch (start us, length us, event | category | flops | bytes accessed | tf_op | source)
XLA Modules:
  0.0 39.3 jit_solution(281911138701943062)
XLA Ops:
  0.0 0.8 %shift-left_or_fusion.2 = (s32[2,8,128]{2,1,0:T(8,128)S(1)}, s32[2,8,128]{2,1,0:T(8,128)S(1)}, s32[2,8,128]{2,1,0:T(8,128)S(1)}) fusion(s32[2,8,512]{2,1,0:T(8,128)} %param.3), kind=kLoop, calls=%fused_computation.8 | loop fusion | flops 26624 | bytes 57344 | tf_op jit(solution)/shard_map/or | solution.py:71
  0.8 0.0 copy-start
  0.8 0.1 collective-permute-start.1
  0.9 0.6 %copy-done = bf16[8,2,1024]{2,1,0:T(2,128)(2,1)S(1)} copy-done((bf16[8,2,1024]{2,1,0:T(2,128)(2,1)S(1)}, bf16[8,2,1024]{2,1,0:T(2,128)(2,1)}, u32[]{:S(2)}) %copy-start) | copy-done | bytes 32792
  1.6 0.5 %collective-permute-done.1 = s32[8,384]{1,0:T(8,128)S(1)} collective-permute-done((s32[8,384]{1,0:T(8,128)S(1)}, s32[8,384]{1,0:T(8,128)S(1)}, u32[]{:S(2)}, u32[]{:S(2)}) %collective-permute-start.1) | collective-permute-done | bytes 12320 | tf_op jit(solution)/shard_map/ppermute | solution.py:169
  2.1 7.2 %collective-permute-start.2 = (s32[2,8,384]{2,1,0:T(8,128)S(1)}, s32[2,8,384]{2,1,0:T(8,128)S(1)}, u32[]{:S(2)}, u32[]{:S(2)}) collective-permute-start(s32[2,8,384]{2,1,0:T(8,128)S(1)} %pad_add_fusion.1.words), channel_id=1, source_target_pairs={{4,0},{0,4},{5,1},{1,5},{6,2},{2,6},{7,3},{3,7},{12,8},{8,12},{13,... | collective-permute-start | bytes 73736 | tf_op jit(solution)/shard_map/ppermute | solution.py:169
  9.3 1.6 %collective-permute-start.5 = (s32[2,8,384]{2,1,0:T(8,128)S(1)}, s32[2,8,384]{2,1,0:T(8,128)S(1)}, u32[]{:S(2)}, u32[]{:S(2)}) collective-permute-start(s32[2,8,384]{2,1,0:T(8,128)S(1)} %pad_add_fusion.1.words), channel_id=1, source_target_pairs={{3,0},{2,1},{1,2},{0,3},{7,4},{6,5},{5,6},{4,7},{11,8},{10,9},{9,1... | collective-permute-start | bytes 73736 | tf_op jit(solution)/shard_map/ppermute | solution.py:169
  10.9 0.0 collective-permute-done
  10.9 1.3 %shard_map.28 = (f32[32,1024]{1,0:T(8,128)S(1)}, bf16[2,16,512]{2,1,0:T(8,128)(2,1)S(1)}) custom-call(bf16[16,1024]{1,0:T(8,128)(2,1)S(1)} %reshape.18.own, bf16[16,1024]{1,0:T(8,128)(2,1)S(1)} %reshape.19.other, s32[2,8,384]{2,1,0:T(8,128)S(1)} %pad_add_fusion.1.words), custom_call_target="tpu_custom_call" | custom-call | tf_op jit(solution)/shard_map/pallas_call | solution.py:130
  12.2 0.6 %collective-permute-start.3 = (s32[2,8,384]{2,1,0:T(8,128)S(1)}, s32[2,8,384]{2,1,0:T(8,128)S(1)}, u32[]{:S(2)}, u32[]{:S(2)}) collective-permute-start(s32[2,8,384]{2,1,0:T(8,128)S(1)} %collective-permute-done.2.words), channel_id=1, source_target_pairs={{3,0},{2,1},{1,2},{0,3},{7,4},{6,5},{5,6},{4,7},{11,8},{10,9},{9,1... | collective-permute-start | bytes 73736 | tf_op jit(solution)/shard_map/ppermute | solution.py:169
  12.9 1.7 %collective-permute-start.6 = (s32[2,8,384]{2,1,0:T(8,128)S(1)}, s32[2,8,384]{2,1,0:T(8,128)S(1)}, u32[]{:S(2)}, u32[]{:S(2)}) collective-permute-start(s32[2,8,384]{2,1,0:T(8,128)S(1)} %pad_add_fusion.1.words), channel_id=1, source_target_pairs={{1,0},{0,1},{3,2},{2,3},{5,4},{4,5},{7,6},{6,7},{9,8},{8,9},{11,10... | collective-permute-start | bytes 73736 | tf_op jit(solution)/shard_map/ppermute | solution.py:169
  14.6 0.0 collective-permute-done.5.words
  14.6 0.4 collective-permute-start.8
  15.0 1.7 %collective-permute-start.7 = (s32[2,8,384]{2,1,0:T(8,128)S(1)}, s32[2,8,384]{2,1,0:T(8,128)S(1)}, u32[]{:S(2)}, u32[]{:S(2)}) collective-permute-start(s32[2,8,384]{2,1,0:T(8,128)S(1)} %collective-permute-done.2.words), channel_id=1, source_target_pairs={{1,0},{0,1},{3,2},{2,3},{5,4},{4,5},{7,6},{6,7},{9,8},{8,9},{11,10... | collective-permute-start | bytes 73736 | tf_op jit(solution)/shard_map/ppermute | solution.py:169
  16.6 2.5 %collective-permute-start.4 = (s32[2,8,384]{2,1,0:T(8,128)S(1)}, s32[2,8,384]{2,1,0:T(8,128)S(1)}, u32[]{:S(2)}, u32[]{:S(2)}) collective-permute-start(s32[2,8,384]{2,1,0:T(8,128)S(1)} %collective-permute-done.3.words), channel_id=1, source_target_pairs={{1,0},{0,1},{3,2},{2,3},{5,4},{4,5},{7,6},{6,7},{9,8},{8,9},{11,10... | collective-permute-start | bytes 73736 | tf_op jit(solution)/shard_map/ppermute | solution.py:169
  19.2 0.6 %shard_map.31.refs_3_ = bf16[2,16,512]{2,1,0:T(8,128)(2,1)S(1)} custom-call(f32[32,1024]{1,0:T(8,128)S(1)} %get-tuple-element.9.tab, s32[2,8,384]{2,1,0:T(8,128)S(1)} %collective-permute-done.2.words), custom_call_target="tpu_custom_call" | custom-call | tf_op jit(solution)/shard_map/pallas_call | solution.py:159
  19.8 0.7 %shard_map.29.refs_1_ = bf16[2,16,512]{2,1,0:T(8,128)(2,1)S(1)} custom-call(f32[32,1024]{1,0:T(8,128)S(1)} %get-tuple-element.9.tab, s32[2,8,384]{2,1,0:T(8,128)S(1)} %collective-permute-done.5.words), custom_call_target="tpu_custom_call" | custom-call | tf_op jit(solution)/shard_map/pallas_call | solution.py:159
  20.5 0.7 %shard_map.30.refs_2_ = bf16[2,16,512]{2,1,0:T(8,128)(2,1)S(1)} custom-call(f32[32,1024]{1,0:T(8,128)S(1)} %get-tuple-element.9.tab, s32[2,8,384]{2,1,0:T(8,128)S(1)} %collective-permute-done.6.words), custom_call_target="tpu_custom_call" | custom-call | tf_op jit(solution)/shard_map/pallas_call | solution.py:159
  21.1 0.7 %shard_map.32.refs_4_ = bf16[2,16,512]{2,1,0:T(8,128)(2,1)S(1)} custom-call(f32[32,1024]{1,0:T(8,128)S(1)} %get-tuple-element.9.tab, s32[2,8,384]{2,1,0:T(8,128)S(1)} %collective-permute-done.3.words), custom_call_target="tpu_custom_call" | custom-call | tf_op jit(solution)/shard_map/pallas_call | solution.py:159
  21.8 0.7 %shard_map.34.refs_6_ = bf16[2,16,512]{2,1,0:T(8,128)(2,1)S(1)} custom-call(f32[32,1024]{1,0:T(8,128)S(1)} %get-tuple-element.9.tab, s32[2,8,384]{2,1,0:T(8,128)S(1)} %collective-permute-done.8.words), custom_call_target="tpu_custom_call" | custom-call | tf_op jit(solution)/shard_map/pallas_call | solution.py:159
  22.5 0.7 %shard_map.33.refs_5_ = bf16[2,16,512]{2,1,0:T(8,128)(2,1)S(1)} custom-call(f32[32,1024]{1,0:T(8,128)S(1)} %get-tuple-element.9.tab, s32[2,8,384]{2,1,0:T(8,128)S(1)} %collective-permute-done.7.words), custom_call_target="tpu_custom_call" | custom-call | tf_op jit(solution)/shard_map/pallas_call | solution.py:159
  23.1 0.7 %shard_map.35 = bf16[16,16,512]{2,1,0:T(8,128)(2,1)S(1)} custom-call(f32[32,1024]{1,0:T(8,128)S(1)} %get-tuple-element.9.tab, s32[2,8,384]{2,1,0:T(8,128)S(1)} %collective-permute-done.4.words, bf16[2,16,512]{2,1,0:T(8,128)(2,1)S(1)} %get-tuple-element.12.refs_0_, bf16[2,16,512]{2,1,0:T(8,128)(2,1)S(1)} %shard_map.29.refs_1_, ...), custom_call_target="tpu_custom_call" | custom-call | tf_op jit(solution)/shard_map/pallas_call | solution.py:159
  23.8 14.9 %all_to_all.5 = bf16[16,16,512]{2,1,0:T(8,128)(2,1)S(1)} all-to-all(bf16[16,16,512]{2,1,0:T(8,128)(2,1)S(1)} %shard_map.35), channel_id=1, replica_groups=mesh['y'=4,'z_lo'=4,'core'=2,'z_hi'=2,'x'=4] {'y','z_lo'}, dimensions={0} | all-to-all | bytes 524288 | tf_op jit(solution)/shard_map/all_to_all | solution.py:199
  38.7 0.6 %multiply_bitcast_fusion = f32[2,8,512]{2,1,0:T(8,128)} fusion(f32[16,512]{1,0:T(8,128)S(1)} %convert_reduce_fusion), kind=kLoop, calls=%fused_computation.1 | loop fusion | flops 8192 | bytes 65536 | tf_op jit(solution)/shard_map/mul | solution.py:201
  (16 shorter events, 0.2 us)
Async XLA Ops:
  0.8 0.8 %copy-start = (bf16[8,2,1024]{2,1,0:T(2,128)(2,1)S(1)}, bf16[8,2,1024]{2,1,0:T(2,128)(2,1)}, u32[]{:S(2)}) copy-start(bf16[8,2,1024]{2,1,0:T(2,128)(2,1)} %param.2) | copy-start | bytes 98308
  0.8 1.3 %collective-permute-start.1 = (s32[8,384]{1,0:T(8,128)S(1)}, s32[8,384]{1,0:T(8,128)S(1)}, u32[]{:S(2)}, u32[]{:S(2)}) collective-permute-start(s32[8,384]{1,0:T(8,128)S(1)} %reshape.21), channel_id=1, source_target_pairs={{8,0},{0,8},{9,1},{1,9},{10,2},{2,10},{11,3},{3,11},{12,4},{4,12},... | collective-permute-start | bytes 36872 | tf_op jit(solution)/shard_map/ppermute | solution.py:169
  1.5 9.4 %collective-permute-start = (bf16[8,2,1024]{2,1,0:T(2,128)(2,1)S(1)}, bf16[8,2,1024]{2,1,0:T(2,128)(2,1)S(1)}, u32[]{:S(2)}, u32[]{:S(2)}) collective-permute-start(bf16[8,2,1024]{2,1,0:T(2,128)(2,1)S(1)} %copy-done), channel_id=1, source_target_pairs={{8,0},{0,8},{9,1},{1,9},{10,2},{2,10},{11,3},{3,11},{12,4},{4,12},... | collective-permute-start | bytes 98312 | tf_op jit(solution)/shard_map/ppermute | solution.py:169
  2.1 10.1 %collective-permute-start.2 = (s32[2,8,384]{2,1,0:T(8,128)S(1)}, s32[2,8,384]{2,1,0:T(8,128)S(1)}, u32[]{:S(2)}, u32[]{:S(2)}) collective-permute-start(s32[2,8,384]{2,1,0:T(8,128)S(1)} %pad_add_fusion.1.words), channel_id=1, source_target_pairs={{4,0},{0,4},{5,1},{1,5},{6,2},{2,6},{7,3},{3,7},{12,8},{8,12},{13,... | collective-permute-start | bytes 73736 | tf_op jit(solution)/shard_map/ppermute | solution.py:169
  9.3 5.3 %collective-permute-start.5 = (s32[2,8,384]{2,1,0:T(8,128)S(1)}, s32[2,8,384]{2,1,0:T(8,128)S(1)}, u32[]{:S(2)}, u32[]{:S(2)}) collective-permute-start(s32[2,8,384]{2,1,0:T(8,128)S(1)} %pad_add_fusion.1.words), channel_id=1, source_target_pairs={{3,0},{2,1},{1,2},{0,3},{7,4},{6,5},{5,6},{4,7},{11,8},{10,9},{9,1... | collective-permute-start | bytes 73736 | tf_op jit(solution)/shard_map/ppermute | solution.py:169
  12.2 4.4 %collective-permute-start.3 = (s32[2,8,384]{2,1,0:T(8,128)S(1)}, s32[2,8,384]{2,1,0:T(8,128)S(1)}, u32[]{:S(2)}, u32[]{:S(2)}) collective-permute-start(s32[2,8,384]{2,1,0:T(8,128)S(1)} %collective-permute-done.2.words), channel_id=1, source_target_pairs={{3,0},{2,1},{1,2},{0,3},{7,4},{6,5},{5,6},{4,7},{11,8},{10,9},{9,1... | collective-permute-start | bytes 73736 | tf_op jit(solution)/shard_map/ppermute | solution.py:169
  12.9 7.6 %collective-permute-start.6 = (s32[2,8,384]{2,1,0:T(8,128)S(1)}, s32[2,8,384]{2,1,0:T(8,128)S(1)}, u32[]{:S(2)}, u32[]{:S(2)}) collective-permute-start(s32[2,8,384]{2,1,0:T(8,128)S(1)} %pad_add_fusion.1.words), channel_id=1, source_target_pairs={{1,0},{0,1},{3,2},{2,3},{5,4},{4,5},{7,6},{6,7},{9,8},{8,9},{11,10... | collective-permute-start | bytes 73736 | tf_op jit(solution)/shard_map/ppermute | solution.py:169
  14.6 7.2 %collective-permute-start.8 = (s32[2,8,384]{2,1,0:T(8,128)S(1)}, s32[2,8,384]{2,1,0:T(8,128)S(1)}, u32[]{:S(2)}, u32[]{:S(2)}) collective-permute-start(s32[2,8,384]{2,1,0:T(8,128)S(1)} %collective-permute-done.5.words), channel_id=1, source_target_pairs={{1,0},{0,1},{3,2},{2,3},{5,4},{4,5},{7,6},{6,7},{9,8},{8,9},{11,10... | collective-permute-start | bytes 73736 | tf_op jit(solution)/shard_map/ppermute | solution.py:169
  15.0 7.5 %collective-permute-start.7 = (s32[2,8,384]{2,1,0:T(8,128)S(1)}, s32[2,8,384]{2,1,0:T(8,128)S(1)}, u32[]{:S(2)}, u32[]{:S(2)}) collective-permute-start(s32[2,8,384]{2,1,0:T(8,128)S(1)} %collective-permute-done.2.words), channel_id=1, source_target_pairs={{1,0},{0,1},{3,2},{2,3},{5,4},{4,5},{7,6},{6,7},{9,8},{8,9},{11,10... | collective-permute-start | bytes 73736 | tf_op jit(solution)/shard_map/ppermute | solution.py:169
  16.6 6.5 %collective-permute-start.4 = (s32[2,8,384]{2,1,0:T(8,128)S(1)}, s32[2,8,384]{2,1,0:T(8,128)S(1)}, u32[]{:S(2)}, u32[]{:S(2)}) collective-permute-start(s32[2,8,384]{2,1,0:T(8,128)S(1)} %collective-permute-done.3.words), channel_id=1, source_target_pairs={{1,0},{0,1},{3,2},{2,3},{5,4},{4,5},{7,6},{6,7},{9,8},{8,9},{11,10... | collective-permute-start | bytes 73736 | tf_op jit(solution)/shard_map/ppermute | solution.py:169
